TPU v7x, 32 devices: a whole 2x2x4 slice. The times are simulated.
32 devices in a mesh: dp: 8 (over z, y), vp: 4 (over x, core).
Axes of the slice: x: 2, y: 2, z: 4, core: 2. Of those that a mesh axis runs over, the one named last changes fastest.
Arguments:
- hidden: bfloat16 [8, 2048, 768], P('dp', 'vp')
- targets: int32 [8, 2048], P('dp', 'vp')
- loss_mask: int32 [8, 2048], P('dp', 'vp')
- norm_scale: float32 [768], replicated
- w_head: bfloat16 [768, 65536], P(None, 'vp')
Outputs:
- output 1: float32 [], replicated
- output 2: bfloat16 [8, 2048, 768], P('dp', 'vp')
- output 3: float32 [768, 65536], P(None, 'vp')
- output 4: float32 [768], replicated
All inputs are finite; a program needn't handle non-finite values.
Results may differ from a plain program's by a relative error of at most 0.001.
Values sent between devices are 32-bit elements.
A program may use at most 1 GiB of HBM per device.

v0:
```python
import jax
import jax.numpy as jnp
from jax import lax
from jax.sharding import PartitionSpec as P

EPS = 1e-5


def solution(mesh):
    vp_count = mesh.shape['vp']

    def local_step(hidden, targets, loss_mask, norm_scale, w_head):
        vocab_local = w_head.shape[1]
        x_f32 = hidden.astype(jnp.float32)
        inv_rms = lax.rsqrt(jnp.mean(x_f32 * x_f32, axis=-1, keepdims=True) + EPS)
        x_hat = x_f32 * inv_rms
        mask_count = lax.psum(jnp.sum(loss_mask.astype(jnp.float32)), ('dp', 'vp'))
        value_a10 = lax.all_gather(x_hat, 'vp', axis=1, tiled=True)
        group_targets = lax.all_gather(targets, 'vp', axis=1, tiled=True)
        group_mask = lax.all_gather(loss_mask, 'vp', axis=1, tiled=True)
        group_normed = (value_a10 * norm_scale).astype(jnp.bfloat16)
        group_weight = group_mask.astype(jnp.float32) / mask_count
        logits = jnp.einsum('btd,dv->btv', group_normed, w_head, preferred_element_type=jnp.float32)
        row_max = lax.pmax(jnp.max(logits, axis=-1), 'vp')
        exp_logits = jnp.exp(logits - row_max[..., None])
        row_sum = lax.psum(jnp.sum(exp_logits, axis=-1), 'vp')
        log_norm = row_max + jnp.log(row_sum)
        col_ids = lax.axis_index('vp') * vocab_local + lax.broadcasted_iota(jnp.int32, (1, 1, vocab_local), 2)
        is_target = col_ids == group_targets[..., None]
        tgt_logit = jnp.sum(jnp.where(is_target, logits, 0.0), axis=-1)
        loss_part = jnp.sum(group_weight * log_norm) / vp_count - jnp.sum(group_weight * tgt_logit)
        total_loss = lax.psum(loss_part, ('dp', 'vp'))
        d_logits = ((exp_logits / row_sum[..., None] - is_target.astype(jnp.float32)) * group_weight[..., None]).astype(jnp.bfloat16)
        dn_part = jnp.einsum('btv,dv->btd', d_logits, w_head, preferred_element_type=jnp.float32)
        d_normed = lax.psum_scatter(dn_part, 'vp', scatter_dimension=1, tiled=True)
        dw_part = jnp.einsum('btd,btv->dv', group_normed, d_logits, preferred_element_type=jnp.float32)
        d_w = lax.psum(dw_part, 'dp')
        d_scale = lax.psum(jnp.sum(d_normed * x_hat, axis=(0, 1)), ('dp', 'vp'))
        value_a6 = d_normed * norm_scale
        d_x = inv_rms * (value_a6 - x_hat * jnp.mean(value_a6 * x_hat, axis=-1, keepdims=True))
        return total_loss, d_x.astype(jnp.bfloat16), d_w, d_scale

    return jax.shard_map(
        local_step,
        mesh=mesh,
        in_specs=(P('dp', 'vp', None), P('dp', 'vp'), P('dp', 'vp'), P(None), P(None, 'vp')),
        out_specs=(P(), P('dp', 'vp', None), P(None, 'vp'), P(None)),
        check_vma=False,
    )
```

profile of v0, /device:TPU:0, one launch (start us, length us, event | category | flops | bytes accessed | tf_op | source)
XLA Modules:
  0.0 1894.3 jit_solution(15632936424872256430)
XLA Ops:
  7.2 0.0 all-gather.2.cloned.1.call-start
  7.2 1.4 fusion.6
  8.6 0.0 copy-start.3
  8.6 0.6 copy-done.3
  9.2 2.5 convert_multiply_fusion
  11.7 0.0 all-gather.2.cloned.1.call-update
  11.7 0.0 reduce-scatter.2.cloned.1.call-start
  11.7 1.3 convert_reduce_fusion
  13.0 43.0 %psum.35 = f32[]{:T(128)} all-reduce(f32[]{:T(128)} %convert_reduce_fusion), channel_id=1, replica_groups=mesh['dp'=8,'vp'=4] {'dp','vp'}, use_global_device_ids=true, to_apply=%region_1.0 | all-reduce | flops 1 | bytes 8 | tf_op jit(solution)/shard_map/psum | solution.py:17
  56.1 7.6 all_gather.9
  63.6 5.3 all_gather.11
  69.0 0.0 all-gather.2.cloned.1.call-done
  69.0 3.3 fusion.10.clone.4
  72.3 67.0 %fusion.11 = (f32[2048]{0:T(1024)S(1)}, f32[2048,16384]{1,0:T(8,128)}) fusion(bf16[768,16384]{1,0:T(8,128)(2,1)} %param.9, bf16[2048,768]{1,0:T(8,128)(2,1)S(1)} %fusion.10.clone.4), kind=kOutput, calls=%fused_computation.26 | convolution fusion | flops 51573161984 | bytes 162537472 | tf_op jit(solution)/shard_map/btd,dv->btv/dot_general | solution.py:23
  139.3 6.4 pmax.7
  145.7 0.0 copy-start.2
  145.7 42.7 %fusion = (f32[2048]{0:T(1024)S(1)}, f32[2048]{0:T(1024)S(1)}) fusion(f32[2048,16384]{1,0:T(8,128)} %get-tuple-element.14, s32[16384]{0:T(1024)S(1)} %iota_add_fusion, s32[2048]{0:T(1024)S(1)} %bitcast.29, f32[2048]{0:T(1024)S(1)} %bitcast.27), kind=kLoop, calls=%fused_computation.2 | loop fusion | flops 167768064 | bytes 134316032 | tf_op jit(solution)/shard_map/reduce_sum | solution.py:30
  188.5 5.9 psum.36
  194.4 0.0 copy-done.2
  194.4 1.3 multiply_reduce_fusion.2
  195.7 64.7 %fusion.3 = bf16[2048,16384]{1,0:T(8,128)(2,1)} fusion(f32[2048,16384]{1,0:T(8,128)} %get-tuple-element.14, f32[2048]{0:T(1024)S(1)} %bitcast.33, f32[2048]{0:T(1024)S(1)} %bitcast.31, s32[16384]{0:T(1024)S(1)} %iota_add_fusion, f32[2048]{0:T(1024)S(1)} %bitcast.28, s32[2048]{0:T(1024)S(1)} %bitcast.30), kind=kLoop, calls=%fused_computation.5 | loop fusion | flops 234881024 | bytes 201424896 | tf_op jit(solution)/shard_map/convert_element_type | solution.py:33
  260.4 0.0 copy-start.1
  260.4 61.0 %convolution_bitcast_fusion = f32[1,2048,768]{2,1,0:T(8,128)} fusion(bf16[2048,16384]{1,0:T(8,128)(2,1)} %fusion.3, bf16[768,16384]{1,0:T(8,128)(2,1)} %param.9), kind=kOutput, calls=%fused_computation.9 | convolution fusion | flops 51539607552 | bytes 98566144 | tf_op jit(solution)/shard_map/btv,dv->btd/dot_general | solution.py:34
  321.4 0.0 reduce-scatter.2.cloned.1.call-update
  321.4 0.3 all-reduce.3.cloned.1.call-start
  321.7 0.0 copy-done.1
  321.7 63.0 %fusion.7 = f32[768,16384]{1,0:T(8,128)} fusion(bf16[2048,16384]{1,0:T(8,128)(2,1)} %fusion.3, f32[1,2048,768]{2,1,0:T(8,128)} %all-gather.2.cloned.1.call-done, f32[768]{0:T(1024)S(1)} %copy-done.1), kind=kOutput, calls=%fused_computation.17 | convolution fusion | flops 51542753280 | bytes 123735040 | tf_op jit(solution)/shard_map/btd,btv->dv/dot_general | solution.py:36
  384.7 0.0 copy-start
  384.7 0.0 copy-start.4
  384.7 0.0 all-reduce.3.cloned.1.call-update
  386.0 0.0 reduce-scatter.2.cloned.1.call-done
  386.0 0.0 copy-done
  386.0 0.0 copy-done.4
  386.0 2.0 multiply_reduce_fusion
  388.0 42.8 %all-reduce = (f32[]{:T(128)}, f32[768]{0:T(1024)}) all-reduce(f32[]{:T(128)S(6)} %sub.24, f32[768]{0:T(1024)S(1)} %get-tuple-element.6), channel_id=1, replica_groups=mesh['dp'=8,'vp'=4] {'dp','vp'}, use_global_device_ids=true, to_apply=%region_10.11 | all-reduce | flops 769 | bytes 6152 | tf_op jit(solution)/shard_map/psum | solution.py:32
  430.8 2.7 multiply_convert_fusion.1
  433.5 1420.6 %all-reduce.3.cloned.1.call-done = f32[768,16384]{1,0:T(8,128)} async-done(((f32[768,16384]{1,0:T(8,128)}), f32[768,16384]{1,0:T(8,128)}) %all-reduce.3.cloned.1.call-update) | async-done | bytes 50331664 | tf_op jit(solution)/shard_map/psum | solution.py:37
  1854.1 33.7 %copy.10 = f32[768,16384]{1,0:T(8,128)} copy(f32[768,16384]{1,0:T(8,128)} %all-reduce.3.cloned.1.call-done) | data formatting | bytes 100663296
  (3 shorter events, 0.0 us)
Async XLA Ops:
  7.2 61.8 %all-gather.2.cloned.1.call-start = ((), (), s32[]{:S(2)}) async-start(), calls=%async_computation.1 | async-start | bytes 7864320 | tf_op jit(solution)/shard_map/all_gather | solution.py:18
  8.6 0.6 copy-start.3
  11.7 374.3 %reduce-scatter.2.cloned.1.call-start = ((), (), s32[]{:S(2)}) async-start(), calls=%async_computation.2 | async-start | bytes 7864320 | tf_op jit(solution)/shard_map/reduce_scatter | solution.py:35
  145.7 48.7 %copy-start.2 = (s32[1,2048]{1,0:T(1,128)S(1)}, s32[1,2048]{1,0:T(1,128)}, u32[]{:S(2)}) copy-start(s32[1,2048]{1,0:T(1,128)} %all_gather.9) | copy-start | bytes 24580
  260.4 61.3 %copy-start.1 = (f32[768]{0:T(1024)S(1)}, f32[768]{0:T(1024)}, u32[]{:S(2)}) copy-start(f32[768]{0:T(1024)} %param.8) | copy-start | bytes 9220
  321.4 1532.7 %all-reduce.3.cloned.1.call-start = ((), (), s32[]{:S(2)}) async-start(), calls=%async_computation.3 | async-start | bytes 100663296 | tf_op jit(solution)/shard_map/psum | solution.py:37
  384.7 1.3 copy-start
  384.7 1.3 copy-start.4
Sparse Core Ops, SparseCore 0:
  11.8 49.9 all-gather.1
  321.5 57.8 reduce-scatter.1
  384.8 1469.2 all-reduce.2
where the time goes:
time: 1890 us
  waiting for transfers between devices  1420 us (75%)
  matrix products  191 us (10%)
  other arithmetic  122 us (6%)
  blocking collectives  111 us (6%)
  local copies, waits for them, and re-layouts  34.2 us (2%)
    psum x1, waiting for transfers between devices, local_step(): d_w = lax.psum(dw_part, 'dp')  1420 us
    dot_general x1, matrix products, local_step(): jnp.einsum('btd,dv->btv', group_normed, w_head, preferred_element_type=jn...  67 us
    convert_element_type x1, other arithmetic, local_step(): ((exp_logits / row_sum[..., None] - is_target.astype(jnp.float32)) * grou...  64.7 us
    dot_general x1, matrix products, local_step(): jnp.einsum('btd,btv->dv', group_normed, d_logits, preferred_element_type=...  63 us
    dot_general x1, matrix products, local_step(): jnp.einsum('btv,dv->btd', d_logits, w_head, preferred_element_type=jnp.fl...  61 us
    psum x1, blocking collectives, local_step(): mask_count = lax.psum(jnp.sum(loss_mask.astype(jnp.float32)), ('dp', 'vp'))  43 us
    psum x1, blocking collectives, local_step(): total_loss = lax.psum(loss_part, ('dp', 'vp'))  42.8 us
    reduce_sum x1, other arithmetic, local_step(): tgt_logit = jnp.sum(jnp.where(is_target, logits, 0.0), axis=-1)  42.7 us
  transfers between devices with their start and end apart: 3, of which 1 were waited for; matrix products, arithmetic and copies ran while one was open for 4% of the time, Pallas kernels for 0%

commit v1 on v0

v1 whole, which is shorter than its diff:
```python
import functools

import jax
import jax.numpy as jnp
from jax import lax
from jax.experimental import pallas as pl
from jax.experimental.pallas import tpu as pltpu
from jax.sharding import PartitionSpec as P


EPS = 1e-5
BLK = 512
DIM = 768
ALIGN = 16
FWD_COLS = 1024
DN_COLS = 512
DW_COLS = 512
DW_TOK = 1024
SUB = 256
DROPPED = 1e30


f32, bf16, i32 = jnp.float32, jnp.bfloat16, jnp.int32


def place_tokens(offs_ref, count, dst, get):
    for b in range(count):
        off = pl.multiple_of(offs_ref[b], ALIGN)
        dst[pl.ds(off, BLK), :] = get(b)


def aux_columns(aux):
    pad = jnp.zeros((120, BLK), f32)
    return jnp.concatenate([aux, pad], axis=0).T


def fwd_kernel(offs_ref, nt_ref, xh_ref, g_ref, w_ref, n_ref, st_ref, m_ref, s_ref):
    j = pl.program_id(0)

    @pl.when(j == 0)
    def _():
        n_ref[...] = jnp.zeros_like(n_ref)
        m_ref[...] = jnp.full_like(m_ref, -DROPPED)
        s_ref[...] = jnp.zeros_like(s_ref)
        place_tokens(offs_ref, 4, n_ref, lambda b: (xh_ref[pl.ds(b * BLK, BLK), :] * g_ref[...]).astype(bf16))

    def tile(i, carry):
        for u in range(2):
            rows = pl.ds(pl.multiple_of(i * 256, 256) + u * 128, 128)
            z = jnp.dot(n_ref[rows, :], w_ref[...], preferred_element_type=f32)
            parts = [z[:, k * 128 : (k + 1) * 128] for k in range(FWD_COLS // 128)]
            m_old = m_ref[rows, :]
            m_new = functools.reduce(jnp.maximum, parts, m_old)
            total = s_ref[rows, :] * jnp.exp(m_old - m_new)
            for part in parts:
                total += jnp.exp(part - m_new)
            m_ref[rows, :] = m_new
            s_ref[rows, :] = total
        return carry

    lax.fori_loop(0, nt_ref[0], tile, 0)

    @pl.when(j == pl.num_programs(0) - 1)
    def _():
        for b in range(4):
            rows = pl.ds(pl.multiple_of(offs_ref[b], ALIGN), BLK)
            m_lane = m_ref[rows, :]
            m = jnp.max(m_lane, axis=1, keepdims=True)
            s = jnp.sum(s_ref[rows, :] * jnp.exp(m_lane - m), axis=1, keepdims=True)
            st_ref[b, 0:1, :] = jnp.broadcast_to(m, (BLK, 128)).T[0:1, :]
            st_ref[b, 1:2, :] = jnp.broadcast_to(s, (BLK, 128)).T[0:1, :]


def forward_stats(offs, ntiles, xh_row, g, w):
    vocab = w.shape[1]
    steps = vocab // FWD_COLS
    return pl.pallas_call(
        fwd_kernel,
        grid_spec=pltpu.PrefetchScalarGridSpec(
            num_scalar_prefetch=2,
            grid=(steps,),
            in_specs=[
                pl.BlockSpec((4 * BLK, DIM), lambda j, *_: (0, 0)),
                pl.BlockSpec((1, DIM), lambda j, *_: (0, 0)),
                pl.BlockSpec((DIM, FWD_COLS), lambda j, *_: (0, j)),
            ],
            out_specs=[
                pl.BlockSpec((4 * BLK, DIM), lambda j, *_: (0, 0)),
                pl.BlockSpec((4, 2, BLK), lambda j, *_: (0, 0, 0)),
            ],
            scratch_shapes=[pltpu.VMEM((4 * BLK, 128), f32), pltpu.VMEM((4 * BLK, 128), f32)],
        ),
        out_shape=[
            jax.ShapeDtypeStruct((4 * BLK, DIM), bf16),
            jax.ShapeDtypeStruct((4, 2, BLK), f32),
        ],
        compiler_params=pltpu.CompilerParams(dimension_semantics=("arbitrary",)),
        cost_estimate=pl.CostEstimate(
            flops=2 * 4 * BLK * DIM * vocab, bytes_accessed=2 * DIM * vocab + 10 * BLK * DIM * 4, transcendentals=4 * BLK * vocab
        ),
        name="fwd_stats",
    )(offs, ntiles, xh_row, g, w)


def grad_logits(z, aux, col0):
    target = aux[:, 2:3].astype(i32) - col0
    hot = lax.broadcasted_iota(i32, z.shape, 1) == target
    p = jnp.exp(z - aux[:, 0:1])
    dz = (jnp.where(hot, p - 1.0, p) * aux[:, 1:2]).astype(bf16)
    return dz, hot


def dn_kernel(offs_ref, kept_ref, nt_ref, col_ref, n_ref, aux_ref, w_ref, dn_ref, tl_ref, acc_ref, auxc_ref):
    j = pl.program_id(0)

    @pl.when(j == 0)
    def _():
        acc_ref[...] = jnp.zeros_like(acc_ref)
        auxc_ref[...] = jnp.zeros_like(auxc_ref)
        tl_ref[...] = jnp.zeros_like(tl_ref)
        place_tokens(offs_ref, 4, auxc_ref, lambda b: aux_columns(aux_ref[b]))

    col0 = col_ref[0] + j * DN_COLS

    def tile(i, carry):
        rows = pl.ds(pl.multiple_of(i * 256, 256), 256)
        aux = auxc_ref[rows, :]
        z = jnp.dot(n_ref[rows, :], w_ref[...], preferred_element_type=f32)
        dz, hot = grad_logits(z, aux, col0)
        picked = jnp.where(hot, z, 0.0)
        picked = functools.reduce(jnp.add, [picked[:, k * 128 : (k + 1) * 128] for k in range(DN_COLS // 128)])
        tl_ref[...] += jnp.sum((picked * aux[:, 1:2]).reshape(32, 8, 128), axis=0)
        acc_ref[rows, :] += lax.dot_general(dz, w_ref[...], (((1,), (1,)), ((), ())), preferred_element_type=f32)
        return carry

    lax.fori_loop(0, nt_ref[0], tile, 0)

    @pl.when(j == pl.num_programs(0) - 1)
    def _():
        for b in range(4):
            got = acc_ref[pl.ds(pl.multiple_of(offs_ref[b], ALIGN), BLK), :]
            live = lax.broadcasted_iota(i32, (BLK, 1), 0) < kept_ref[b]
            dn_ref[pl.ds(b * BLK, BLK), :] = jnp.where(live, got, 0.0)


def backward_dn(offs, kept, ntiles, col0, n_row, aux_row, w):
    vocab = w.shape[1]
    return pl.pallas_call(
        dn_kernel,
        grid_spec=pltpu.PrefetchScalarGridSpec(
            num_scalar_prefetch=4,
            grid=(vocab // DN_COLS,),
            in_specs=[
                pl.BlockSpec((4 * BLK, DIM), lambda j, *_: (0, 0)),
                pl.BlockSpec((4, 8, BLK), lambda j, *_: (0, 0, 0)),
                pl.BlockSpec((DIM, DN_COLS), lambda j, *_: (0, j)),
            ],
            out_specs=[
                pl.BlockSpec((4 * BLK, DIM), lambda j, *_: (0, 0)),
                pl.BlockSpec((8, 128), lambda j, *_: (0, 0)),
            ],
            scratch_shapes=[pltpu.VMEM((4 * BLK, DIM), f32), pltpu.VMEM((4 * BLK, 128), f32)],
        ),
        out_shape=[
            jax.ShapeDtypeStruct((4 * BLK, DIM), f32),
            jax.ShapeDtypeStruct((8, 128), f32),
        ],
        compiler_params=pltpu.CompilerParams(dimension_semantics=("arbitrary",)),
        cost_estimate=pl.CostEstimate(
            flops=4 * 4 * BLK * DIM * vocab, bytes_accessed=2 * DIM * vocab + 6 * BLK * DIM * 4, transcendentals=4 * BLK * vocab
        ),
        name="backward_dn",
    )(offs, kept, ntiles, col0, n_row, aux_row, w)


def gather_kernel(offs_ref, xh_ref, g_ref, aux_ref, n_hbm, aux_hbm, n_ref, auxc_ref, sems):
    b = pl.program_id(0)

    @pl.when(b == 0)
    def _():
        auxc_ref[...] = jnp.zeros_like(auxc_ref)

        def clear(i, carry):
            n_ref[pl.ds(pl.multiple_of(i * BLK, BLK), BLK), :] = jnp.zeros((BLK, DIM), bf16)
            return carry

        lax.fori_loop(0, n_ref.shape[0] // BLK, clear, 0)

    off = pl.multiple_of(offs_ref[b], ALIGN)
    n_ref[pl.ds(off, BLK), :] = (xh_ref[...] * g_ref[...]).astype(bf16)
    auxc_ref[pl.ds(off, BLK), :] = aux_columns(aux_ref[0])

    @pl.when(b == pl.num_programs(0) - 1)
    def _():
        copies = [pltpu.make_async_copy(n_ref, n_hbm, sems.at[0]), pltpu.make_async_copy(auxc_ref, aux_hbm, sems.at[1])]
        for copy in copies:
            copy.start()
        for copy in copies:
            copy.wait()


def gather_tokens(offs, xh_all, g, aux_all):
    blocks = aux_all.shape[0]
    tokens = blocks * BLK
    return pl.pallas_call(
        gather_kernel,
        grid_spec=pltpu.PrefetchScalarGridSpec(
            num_scalar_prefetch=1,
            grid=(blocks,),
            in_specs=[
                pl.BlockSpec((BLK, DIM), lambda b, *_: (b, 0)),
                pl.BlockSpec((1, DIM), lambda b, *_: (0, 0)),
                pl.BlockSpec((1, 8, BLK), lambda b, *_: (b, 0, 0)),
            ],
            out_specs=[pl.BlockSpec(memory_space=pl.ANY), pl.BlockSpec(memory_space=pl.ANY)],
            scratch_shapes=[
                pltpu.VMEM((tokens, DIM), bf16),
                pltpu.VMEM((tokens, 128), f32),
                pltpu.SemaphoreType.DMA((2,)),
            ],
        ),
        out_shape=[
            jax.ShapeDtypeStruct((tokens, DIM), bf16),
            jax.ShapeDtypeStruct((tokens, 128), f32),
        ],
        compiler_params=pltpu.CompilerParams(dimension_semantics=("arbitrary",), vmem_limit_bytes=56 << 20),
        cost_estimate=pl.CostEstimate(flops=2 * tokens * DIM, bytes_accessed=6 * tokens * DIM, transcendentals=0),
        name="gather_tokens",
    )(offs, xh_all, g, aux_all)


def dw_kernel(place_ref, nt_ref, n_hbm, aux_hbm, w_ref, *rest):
    out_ref, all_ref, nbuf, abuf, sems = rest[-5:]
    steps = nt_ref[0]

    def fetch(i, slot):
        rows = pl.ds(pl.multiple_of(i * DW_TOK, DW_TOK), DW_TOK)
        return (
            pltpu.make_async_copy(n_hbm.at[rows, :], nbuf.at[slot], sems.at[slot, 0]),
            pltpu.make_async_copy(aux_hbm.at[rows, :], abuf.at[slot], sems.at[slot, 1]),
        )

    for copy in fetch(0, 0):
        copy.start()
    out_ref[...] = jnp.zeros_like(out_ref)

    def tile(i, carry):
        slot = lax.rem(i, 2)

        @pl.when(i + 1 < steps)
        def _():
            for copy in fetch(i + 1, 1 - slot):
                copy.start()

        for copy in fetch(i, slot):
            copy.wait()
        for u in range(DW_TOK // SUB):
            rows = pl.ds(u * SUB, SUB)
            n = nbuf[slot, rows, :]
            z = jnp.dot(n, w_ref[...], preferred_element_type=f32)
            dz, _ = grad_logits(z, abuf[slot, rows, :], place_ref[1])
            out_ref[...] += lax.dot_general(n, dz, (((0,), (0,)), ((), ())), preferred_element_type=f32)
        return carry

    lax.fori_loop(0, steps, tile, 0)
    all_ref[...] = out_ref[...]


def weight_grad(place, ntiles, n_all, aux_all, w, whole):
    tokens, vocab = n_all.shape[0], w.shape[1]
    column = pl.BlockSpec((DIM, DW_COLS), lambda i, place, nt: (0, place[0]))
    anywhere = pl.BlockSpec(memory_space=pl.ANY)
    held = [] if whole is None else [whole]
    return pl.pallas_call(
        dw_kernel,
        grid_spec=pltpu.PrefetchScalarGridSpec(
            num_scalar_prefetch=2,
            grid=(1,),
            in_specs=[anywhere, anywhere, column] + [anywhere] * len(held),
            out_specs=[pl.BlockSpec((DIM, DW_COLS), lambda i, *_: (0, 0)), column],
            scratch_shapes=[
                pltpu.VMEM((2, DW_TOK, DIM), bf16),
                pltpu.VMEM((2, DW_TOK, 128), f32),
                pltpu.SemaphoreType.DMA((2, 2)),
            ],
        ),
        out_shape=[
            jax.ShapeDtypeStruct((DIM, DW_COLS), f32),
            jax.ShapeDtypeStruct((DIM, vocab), f32),
        ],
        input_output_aliases={5: 1} if held else {},
        compiler_params=pltpu.CompilerParams(dimension_semantics=("arbitrary",)),
        cost_estimate=pl.CostEstimate(
            flops=2 * tokens * DIM * DW_COLS, bytes_accessed=tokens * DIM + 8 * DIM * DW_COLS, transcendentals=tokens * DW_COLS // 2
        ),
        name="weight_grad",
    )(place, ntiles.reshape(1), n_all, aux_all, w, *held)


def solution(mesh):
    dp_count, vp_count = mesh.shape["dp"], mesh.shape["vp"]

    def local_step(hidden, targets, loss_mask, norm_scale, w_head):
        vocab = w_head.shape[1]
        dp, vp = lax.axis_index("dp"), lax.axis_index("vp")
        g = norm_scale.reshape(1, DIM)

        mask = loss_mask[0]
        idx = lax.iota(i32, BLK)
        before = jnp.sum(jnp.where(idx[None, :] < idx[:, None], mask[None, :], 0), axis=1)
        kept = jnp.sum(mask)
        pos = jnp.where(mask == 1, before, kept + idx - before)
        perm = pos[None, :] == idx[:, None]
        x_sorted = jnp.dot(perm.astype(bf16), hidden[0], preferred_element_type=f32)
        t_sorted = jnp.sum(jnp.where(perm, targets[0][None, :], 0), axis=1)
        inv_rms = lax.rsqrt(jnp.mean(x_sorted * x_sorted, axis=-1, keepdims=True) + EPS)
        x_hat = x_sorted * inv_rms

        xh_row = lax.all_gather(x_hat, "vp", axis=0, tiled=True)
        info = jnp.concatenate([t_sorted, jnp.full((BLK,), kept, i32)]).reshape(1, 2 * BLK)
        info = lax.all_gather(info, ("dp", "vp"), axis=0, tiled=True)
        xh_all = lax.all_gather(x_hat, ("dp", "vp"), axis=0, tiled=True)

        t_all, kept_all = info[:, :BLK], info[:, BLK]
        span = (kept_all + ALIGN - 1) // ALIGN * ALIGN
        offs_all = jnp.cumsum(span) - span
        total = jnp.sum(span)
        weight = 1.0 / jnp.sum(kept_all).astype(f32)
        kept_row = lax.dynamic_slice(kept_all, (dp * vp_count,), (vp_count,))
        offs_row = lax.dynamic_slice(offs_all, (dp * vp_count,), (vp_count,))
        span_row = lax.dynamic_slice(span, (dp * vp_count,), (vp_count,))
        offs_row = offs_row - offs_row[0]
        nt_row = ((jnp.sum(span_row) + 255) // 256).reshape(1)
        nt_all = jnp.maximum((total + DW_TOK - 1) // DW_TOK, 1)

        n_row, stats = forward_stats(offs_row, nt_row, xh_row, g, w_head)
        stats = lax.all_gather(stats, "vp", axis=0)
        row_max = jnp.max(stats[:, :, 0], axis=0)
        row_sum = jnp.sum(stats[:, :, 1] * jnp.exp(stats[:, :, 0] - row_max), axis=0)
        lse_row = row_max + jnp.log(row_sum)
        live_row = idx[None, :] < kept_row[:, None]
        lse_row = jnp.where(live_row, lse_row, DROPPED)
        lse_all = lax.all_gather(lse_row, "dp", axis=0, tiled=True)
        live_all = idx[None, :] < kept_all[:, None]
        w_all = jnp.where(live_all, weight, 0.0)
        zeros = jnp.zeros_like(w_all)
        aux_all = jnp.stack([lse_all, w_all, t_all.astype(f32)] + [zeros] * 5, axis=1)
        aux_row = lax.dynamic_slice(aux_all, (dp * vp_count, 0, 0), (vp_count, 8, BLK))

        dn_part, t_part = backward_dn(offs_row, kept_row, nt_row, (vp * vocab).reshape(1), n_row, aux_row, w_head)
        d_normed = lax.psum_scatter(dn_part, "vp", scatter_dimension=0, tiled=True)

        n_all, auxc_all = gather_tokens(offs_all, xh_all, g, aux_all)
        half, quarter = vocab // 2, vocab // 4
        y_pos, z_pos = dp % 2, (dp // 2) % 2
        y_pairs = [(d, d ^ 1) for d in range(dp_count)]
        z_pairs = [(d, d ^ 2) for d in range(dp_count)]
        whole, moved = None, []
        for c in range(quarter // DW_COLS):
            for base, where, pairs in ((0, y_pos, y_pairs), (half, z_pos, z_pairs)):
                col = base + where * quarter + c * DW_COLS
                place = jnp.stack([col // DW_COLS, vp * vocab + col]).astype(i32)
                chunk, whole = weight_grad(place, nt_all, n_all, auxc_all, w_head, whole)
                other = base + (1 - where) * quarter + c * DW_COLS
                moved.append((other, lax.ppermute(chunk, "dp", pairs)))
        for other, chunk in moved:
            whole = lax.dynamic_update_slice(whole, chunk, (0, other))

        d_scale = jnp.sum(d_normed * x_hat, axis=0)
        e = d_normed * norm_scale
        d_x = inv_rms * (e - x_hat * jnp.mean(e * x_hat, axis=-1, keepdims=True))
        back = perm.astype(bf16).T
        d_x = jnp.dot(back, d_x.astype(bf16), preferred_element_type=f32).astype(bf16)

        own = jnp.where(idx < kept, lax.dynamic_slice(lse_row, (vp, 0), (1, BLK))[0], 0.0)
        loss_part = weight * jnp.sum(own) - jnp.sum(t_part)
        parts = jnp.concatenate([d_scale, jnp.full((128,), loss_part, f32)]).reshape(1, DIM + 128)
        parts = jnp.sum(lax.all_gather(parts, ("dp", "vp"), axis=0, tiled=True), axis=0)
        return parts[DIM], d_x[None], whole, parts[:DIM]

    return jax.shard_map(
        local_step,
        mesh=mesh,
        in_specs=(P("dp", "vp", None), P("dp", "vp"), P("dp", "vp"), P(None), P(None, "vp")),
        out_specs=(P(), P("dp", "vp", None), P(None, "vp"), P(None)),
        check_vma=False,
    )
```

time: 1890 us -> 1200 us (0.63)
  waiting for transfers between devices: 1420 us -> 407 us
  Pallas kernels: 0 us -> 513 us
  matrix products: 191 us -> 2.5 us
  other arithmetic: 122 us -> 17.2 us
  blocking collectives: 111 us -> 170 us
    psum x1 -> x0, waiting for transfers between devices: 1420 us -> none  [local_step(): d_w = lax.psum(dw_part, 'dp')]
    pallas_call x0 -> x19, Pallas kernels: none -> 513 us  [the longest x16 380 us: weight_grad(): pl.pallas_call(dw_kernel, grid_spec=pltpu.PrefetchScalarGridSpec(num_scal...]
    dot_general x3 -> x2, matrix products: 191 us -> 2.5 us  [the longest x1 1.83 us: local_step(): jnp.dot(back, d_x.astype(bf16), preferred_element_type=f32).astype(bf16)]
    all_gather x1 -> x2, waiting for transfers between devices: 0.02 us -> 171 us  [the longest x1 171 us: local_step(): xh_all = lax.all_gather(x_hat, ('dp', 'vp'), axis=0, tiled=True)]
    all_gather x2 -> x4, blocking collectives: 12.9 us -> 170 us  [the longest x1 76.8 us: local_step(): lse_all = lax.all_gather(lse_row, 'dp', axis=0, tiled=True)]
    reduce_scatter x1, waiting for transfers between devices: 0.02 us -> 147 us  [local_step(): d_normed = lax.psum_scatter(dn_part, 'vp', scatter_dimension=0, tiled=True)]
    psum x3 -> x0, blocking collectives: 91.8 us -> none  [the longest x1 43 us: local_step(): mask_count = lax.psum(jnp.sum(loss_mask.astype(jnp.float32)), ('dp', 'vp'))]
    ppermute x0 -> x16, waiting for transfers between devices: none -> 87.8 us  [local_step(): moved.append((other, lax.ppermute(chunk, 'dp', pairs)))]
  transfers between devices with their start and end apart: 3 -> 19, of which waited for: 1 -> 9; matrix products, arithmetic and copies ran while one was open for 4% -> 4% of each run, Pallas kernels for 0% -> 30%
where the time goes in v1:
time: 1200 us; the launch traced here: 1190 us
  Pallas kernels  513 us (43%)
  waiting for transfers between devices  407 us (34%)
  blocking collectives  170 us (14%)
  local copies, waits for them, and re-layouts  38.2 us (3%)
  between operations  19.7 us (2%)
  starting transfers between devices  18.9 us (2%)
  other arithmetic  17.2 us (1%)
    pallas_call x16, Pallas kernels, weight_grad(): pl.pallas_call(dw_kernel, grid_spec=pltpu.PrefetchScalarGridSpec(num_scal...  380 us
    all_gather x1, waiting for transfers between devices, local_step(): xh_all = lax.all_gather(x_hat, ('dp', 'vp'), axis=0, tiled=True)  171 us
    reduce_scatter x1, waiting for transfers between devices, local_step(): d_normed = lax.psum_scatter(dn_part, 'vp', scatter_dimension=0, tiled=True)  147 us
    ppermute x16, waiting for transfers between devices, local_step(): moved.append((other, lax.ppermute(chunk, 'dp', pairs)))  87.8 us
    all_gather x1, blocking collectives, local_step(): lse_all = lax.all_gather(lse_row, 'dp', axis=0, tiled=True)  76.8 us
    pallas_call x1, Pallas kernels, backward_dn(): pl.pallas_call(dn_kernel, grid_spec=pltpu.PrefetchScalarGridSpec(num_scal...  56.2 us
    all_gather x1, blocking collectives, local_step(): info = lax.all_gather(info, ('dp', 'vp'), axis=0, tiled=True)  44.3 us
    pallas_call x1, Pallas kernels, gather_tokens(): pl.pallas_call(gather_kernel, grid_spec=pltpu.PrefetchScalarGridSpec(num_...  43.3 us
  transfers between devices with their start and end apart: 19, of which 9 were waited for; matrix products, arithmetic and copies ran while one was open for 4% of the time, Pallas kernels for 30%

profile of v1, /device:TPU:0, one launch (start us, length us, event | category | flops | bytes accessed | tf_op | source)
XLA Modules:
  0.0 1185.7 jit_solution(2797304801050801765)
XLA Ops:
  16.3 44.3 %all-gather = s32[32768]{0:T(1024)S(1)} all-gather(s32[1024]{0:T(1024)S(1)} %concatenate.6), channel_id=2, replica_groups=mesh['dp'=8,'vp'=4] {'dp','vp'}, dimensions={0}, use_global_device_ids=true | all-gather | bytes 135168 | tf_op jit(solution)/shard_map/all_gather | solution.py:321
  65.8 32.9 %fwd_stats.1 = (bf16[2048,768]{1,0:T(8,128)(2,1)}, f32[4,2,512]{2,1,0:T(2,128)}) custom-call(s32[4]{0:T(128)} %broadcast_subtract_fusion.offs_ref, s32[1]{0:T(128)} %bitcast.5.nt_ref, f32[2048,768]{1,0:T(8,128)} %all-gather.8.cloned.1.call-done.xh_ref, f32[1,768]{1,0:T(1,128)} %reshape.131.g_ref, bf16[768,16384]{1,0:T(8,128)(2,1)} %w_ref.35), custom_call_target="tpu_custom_call" | custom-call | flops 51539607552 | bytes 40894464 | tf_op jit(solution)/shard_map/fwd_stats/pallas_call | solution.py:77
  98.7 5.4 all-gather.1
  104.3 76.8 %all-gather.3 = f32[8,4,512]{2,1,0:T(4,128)S(1)} all-gather(f32[1,4,512]{2,1,0:T(4,128)S(1)} %bitcast.66), channel_id=1, replica_groups=mesh['dp'=8,'vp'=4] {'dp'}, dimensions={0}, use_global_device_ids=true | all-gather | bytes 73728 | tf_op jit(solution)/shard_map/all_gather | solution.py:343
  182.6 56.2 %backward_dn.1 = (f32[2048,768]{1,0:T(8,128)}, f32[8,128]{1,0:T(8,128)}) custom-call(s32[4]{0:T(128)} %broadcast_subtract_fusion.offs_ref, s32[4]{0:T(128)} %copy-done.16, s32[1]{0:T(128)} %bitcast.5.nt_ref, s32[1]{0:T(128)} %bitcast.6.col_ref, bf16[2048,768]{1,0:T(8,128)(2,1)} %get-tuple-element.42.n_ref, ...), custom_call_target="tpu_custom_call" | custom-call | flops 103079215104 | bytes 34603008 | tf_op jit(solution)/shard_map/backward_dn/pallas_call | solution.py:148
  248.6 147.2 %reduce-scatter.2.cloned.1.call-done = f32[512,768]{1,0:T(8,128)} async-done(((f32[2048,768]{1,0:T(8,128)}), f32[512,768]{1,0:T(8,128)}) %reduce-scatter.2.cloned.1.call-update) | async-done | bytes 1572880 | tf_op jit(solution)/shard_map/reduce_scatter | solution.py:351
  395.8 2.1 multiply_reduce_fusion
  397.9 43.2 %all-gather.4 = f32[32,1,896]{2,1,0:T(1,128)S(1)} all-gather(f32[1,1,896]{2,1,0:T(1,128)S(1)} %reshape.139), channel_id=4, replica_groups=mesh['dp'=8,'vp'=4] {'dp','vp'}, dimensions={0}, use_global_device_ids=true | all-gather | bytes 118272 | tf_op jit(solution)/shard_map/all_gather | solution.py:378
  441.7 1.8 fusion
  443.6 171.3 %all-gather.10.cloned.1.call-done.xh_ref = f32[16384,768]{1,0:T(8,128)} async-done(((f32[512,768]{1,0:T(8,128)}), f32[16384,768]{1,0:T(8,128)}) %all-gather.10.cloned.1.call-update) | async-done | bytes 50331664 | tf_op jit(solution)/shard_map/all_gather | solution.py:322
  614.8 43.3 %gather_tokens.1 = (bf16[16384,768]{1,0:T(8,128)(2,1)}, f32[16384,128]{1,0:T(8,128)}) custom-call(s32[32]{0:T(128)} %copy-done.14, f32[16384,768]{1,0:T(8,128)} %all-gather.10.cloned.1.call-done.xh_ref, f32[1,768]{1,0:T(1,128)} %reshape.131.g_ref, f32[32,8,512]{2,1,0:T(8,128)} %copy-done.5), custom_call_target="tpu_custom_call" | custom-call | flops 25165824 | bytes 75497472 | tf_op jit(solution)/shard_map/gather_tokens/pallas_call | solution.py:205
  658.2 23.8 %weight_grad.16 = (f32[768,512]{1,0:T(8,128)}, f32[768,16384]{1,0:T(8,128)}) custom-call(s32[2]{0:T(128)} %get-tuple-element.110.place_ref, s32[1]{0:T(128)} %bitcast.16.nt_ref, bf16[16384,768]{1,0:T(8,128)(2,1)} %get-tuple-element.46.n_hbm, f32[16384,128]{1,0:T(8,128)} %get-tuple-element.47.aux_hbm, bf16[768,16384]{1,0:T(8,128)(2,1)} %w_ref.35), custom_call_target="tpu_custom_call" | custom-call | flops 12884901888 | bytes 15728640 | tf_op jit(solution)/shard_map/weight_grad/pallas_call | solution.py:274
  683.5 23.7 %weight_grad.17 = (f32[768,512]{1,0:T(8,128)}, f32[768,16384]{1,0:T(8,128)}) custom-call(s32[2]{0:T(128)} %get-tuple-element.109.place_ref, s32[1]{0:T(128)} %bitcast.16.nt_ref, bf16[16384,768]{1,0:T(8,128)(2,1)} %get-tuple-element.46.n_hbm, f32[16384,128]{1,0:T(8,128)} %get-tuple-element.47.aux_hbm, ...), custom_call_target="tpu_custom_call", output_to_operand_aliasing={{1}: (5, {})} | custom-call | flops 12884901888 | bytes 15728640 | tf_op jit(solution)/shard_map/weight_grad/pallas_call | solution.py:274
  707.3 23.8 %weight_grad.18 = (f32[768,512]{1,0:T(8,128)}, f32[768,16384]{1,0:T(8,128)}) custom-call(s32[2]{0:T(128)} %get-tuple-element.108.place_ref, s32[1]{0:T(128)} %bitcast.16.nt_ref, bf16[16384,768]{1,0:T(8,128)(2,1)} %get-tuple-element.46.n_hbm, f32[16384,128]{1,0:T(8,128)} %get-tuple-element.47.aux_hbm, ...), custom_call_target="tpu_custom_call", output_to_operand_aliasing={{1}: (5, {})} | custom-call | flops 12884901888 | bytes 15728640 | tf_op jit(solution)/shard_map/weight_grad/pallas_call | solution.py:274
  731.7 23.7 %weight_grad.19 = (f32[768,512]{1,0:T(8,128)}, f32[768,16384]{1,0:T(8,128)}) custom-call(s32[2]{0:T(128)} %get-tuple-element.107.place_ref, s32[1]{0:T(128)} %bitcast.16.nt_ref, bf16[16384,768]{1,0:T(8,128)(2,1)} %get-tuple-element.46.n_hbm, f32[16384,128]{1,0:T(8,128)} %get-tuple-element.47.aux_hbm, ...), custom_call_target="tpu_custom_call", output_to_operand_aliasing={{1}: (5, {})} | custom-call | flops 12884901888 | bytes 15728640 | tf_op jit(solution)/shard_map/weight_grad/pallas_call | solution.py:274
  755.5 2.1 collective-permute-start.3
  757.5 23.7 %weight_grad.20 = (f32[768,512]{1,0:T(8,128)}, f32[768,16384]{1,0:T(8,128)}) custom-call(s32[2]{0:T(128)} %get-tuple-element.106.place_ref, s32[1]{0:T(128)} %bitcast.16.nt_ref, bf16[16384,768]{1,0:T(8,128)(2,1)} %get-tuple-element.46.n_hbm, f32[16384,128]{1,0:T(8,128)} %get-tuple-element.47.aux_hbm, ...), custom_call_target="tpu_custom_call", output_to_operand_aliasing={{1}: (5, {})} | custom-call | flops 12884901888 | bytes 15728640 | tf_op jit(solution)/shard_map/weight_grad/pallas_call | solution.py:274
  782.8 23.7 %weight_grad.21 = (f32[768,512]{1,0:T(8,128)}, f32[768,16384]{1,0:T(8,128)}) custom-call(s32[2]{0:T(128)} %get-tuple-element.105.place_ref, s32[1]{0:T(128)} %bitcast.16.nt_ref, bf16[16384,768]{1,0:T(8,128)(2,1)} %get-tuple-element.46.n_hbm, f32[16384,128]{1,0:T(8,128)} %get-tuple-element.47.aux_hbm, ...), custom_call_target="tpu_custom_call", output_to_operand_aliasing={{1}: (5, {})} | custom-call | flops 12884901888 | bytes 15728640 | tf_op jit(solution)/shard_map/weight_grad/pallas_call | solution.py:274
  806.6 23.7 %weight_grad.22 = (f32[768,512]{1,0:T(8,128)}, f32[768,16384]{1,0:T(8,128)}) custom-call(s32[2]{0:T(128)} %get-tuple-element.104.place_ref, s32[1]{0:T(128)} %bitcast.16.nt_ref, bf16[16384,768]{1,0:T(8,128)(2,1)} %get-tuple-element.46.n_hbm, f32[16384,128]{1,0:T(8,128)} %get-tuple-element.47.aux_hbm, ...), custom_call_target="tpu_custom_call", output_to_operand_aliasing={{1}: (5, {})} | custom-call | flops 12884901888 | bytes 15728640 | tf_op jit(solution)/shard_map/weight_grad/pallas_call | solution.py:274
  830.3 23.7 %weight_grad.23 = (f32[768,512]{1,0:T(8,128)}, f32[768,16384]{1,0:T(8,128)}) custom-call(s32[2]{0:T(128)} %get-tuple-element.103.place_ref, s32[1]{0:T(128)} %bitcast.16.nt_ref, bf16[16384,768]{1,0:T(8,128)(2,1)} %get-tuple-element.46.n_hbm, f32[16384,128]{1,0:T(8,128)} %get-tuple-element.47.aux_hbm, ...), custom_call_target="tpu_custom_call", output_to_operand_aliasing={{1}: (5, {})} | custom-call | flops 12884901888 | bytes 15728640 | tf_op jit(solution)/shard_map/weight_grad/pallas_call | solution.py:274
  854.1 23.7 %weight_grad.24 = (f32[768,512]{1,0:T(8,128)}, f32[768,16384]{1,0:T(8,128)}) custom-call(s32[2]{0:T(128)} %get-tuple-element.102.place_ref, s32[1]{0:T(128)} %bitcast.16.nt_ref, bf16[16384,768]{1,0:T(8,128)(2,1)} %get-tuple-element.46.n_hbm, f32[16384,128]{1,0:T(8,128)} %get-tuple-element.47.aux_hbm, ...), custom_call_target="tpu_custom_call", output_to_operand_aliasing={{1}: (5, {})} | custom-call | flops 12884901888 | bytes 15728640 | tf_op jit(solution)/shard_map/weight_grad/pallas_call | solution.py:274
  877.8 23.7 %weight_grad.25 = (f32[768,512]{1,0:T(8,128)}, f32[768,16384]{1,0:T(8,128)}) custom-call(s32[2]{0:T(128)} %get-tuple-element.101.place_ref, s32[1]{0:T(128)} %bitcast.16.nt_ref, bf16[16384,768]{1,0:T(8,128)(2,1)} %get-tuple-element.46.n_hbm, f32[16384,128]{1,0:T(8,128)} %get-tuple-element.47.aux_hbm, ...), custom_call_target="tpu_custom_call", output_to_operand_aliasing={{1}: (5, {})} | custom-call | flops 12884901888 | bytes 15728640 | tf_op jit(solution)/shard_map/weight_grad/pallas_call | solution.py:274
  901.6 23.7 %weight_grad.26 = (f32[768,512]{1,0:T(8,128)}, f32[768,16384]{1,0:T(8,128)}) custom-call(s32[2]{0:T(128)} %get-tuple-element.100.place_ref, s32[1]{0:T(128)} %bitcast.16.nt_ref, bf16[16384,768]{1,0:T(8,128)(2,1)} %get-tuple-element.46.n_hbm, f32[16384,128]{1,0:T(8,128)} %get-tuple-element.47.aux_hbm, ...), custom_call_target="tpu_custom_call", output_to_operand_aliasing={{1}: (5, {})} | custom-call | flops 12884901888 | bytes 15728640 | tf_op jit(solution)/shard_map/weight_grad/pallas_call | solution.py:274
  925.4 23.7 %weight_grad.27 = (f32[768,512]{1,0:T(8,128)}, f32[768,16384]{1,0:T(8,128)}) custom-call(s32[2]{0:T(128)} %get-tuple-element.99.place_ref, s32[1]{0:T(128)} %bitcast.16.nt_ref, bf16[16384,768]{1,0:T(8,128)(2,1)} %get-tuple-element.46.n_hbm, f32[16384,128]{1,0:T(8,128)} %get-tuple-element.47.aux_hbm, ...), custom_call_target="tpu_custom_call", output_to_operand_aliasing={{1}: (5, {})} | custom-call | flops 12884901888 | bytes 15728640 | tf_op jit(solution)/shard_map/weight_grad/pallas_call | solution.py:274
  949.1 23.7 %weight_grad.28 = (f32[768,512]{1,0:T(8,128)}, f32[768,16384]{1,0:T(8,128)}) custom-call(s32[2]{0:T(128)} %get-tuple-element.98.place_ref, s32[1]{0:T(128)} %bitcast.16.nt_ref, bf16[16384,768]{1,0:T(8,128)(2,1)} %get-tuple-element.46.n_hbm, f32[16384,128]{1,0:T(8,128)} %get-tuple-element.47.aux_hbm, ...), custom_call_target="tpu_custom_call", output_to_operand_aliasing={{1}: (5, {})} | custom-call | flops 12884901888 | bytes 15728640 | tf_op jit(solution)/shard_map/weight_grad/pallas_call | solution.py:274
  973.0 23.8 %weight_grad.29 = (f32[768,512]{1,0:T(8,128)}, f32[768,16384]{1,0:T(8,128)}) custom-call(s32[2]{0:T(128)} %get-tuple-element.97.place_ref, s32[1]{0:T(128)} %bitcast.16.nt_ref, bf16[16384,768]{1,0:T(8,128)(2,1)} %get-tuple-element.46.n_hbm, f32[16384,128]{1,0:T(8,128)} %get-tuple-element.47.aux_hbm, ...), custom_call_target="tpu_custom_call", output_to_operand_aliasing={{1}: (5, {})} | custom-call | flops 12884901888 | bytes 15728640 | tf_op jit(solution)/shard_map/weight_grad/pallas_call | solution.py:274
  997.4 2.0 collective-permute-start.7
  1000.8 23.9 %weight_grad.30 = (f32[768,512]{1,0:T(8,128)}, f32[768,16384]{1,0:T(8,128)}) custom-call(s32[2]{0:T(128)} %get-tuple-element.96.place_ref, s32[1]{0:T(128)} %bitcast.16.nt_ref, bf16[16384,768]{1,0:T(8,128)(2,1)} %get-tuple-element.46.n_hbm, f32[16384,128]{1,0:T(8,128)} %get-tuple-element.47.aux_hbm, ...), custom_call_target="tpu_custom_call", output_to_operand_aliasing={{1}: (5, {})} | custom-call | flops 12884901888 | bytes 15728640 | tf_op jit(solution)/shard_map/weight_grad/pallas_call | solution.py:274
  1025.5 23.7 %weight_grad.31 = (f32[768,512]{1,0:T(8,128)}, f32[768,16384]{1,0:T(8,128)}) custom-call(s32[2]{0:T(128)} %get-tuple-element.95.place_ref, s32[1]{0:T(128)} %bitcast.16.nt_ref, bf16[16384,768]{1,0:T(8,128)(2,1)} %get-tuple-element.46.n_hbm, f32[16384,128]{1,0:T(8,128)} %get-tuple-element.47.aux_hbm, ...), custom_call_target="tpu_custom_call", output_to_operand_aliasing={{1}: (5, {})} | custom-call | flops 12884901888 | bytes 15728640 | tf_op jit(solution)/shard_map/weight_grad/pallas_call | solution.py:274
  1049.3 2.0 collective-permute-start.11
  1051.3 2.8 constant_dynamic-update-slice_fusion.15
  1055.6 2.7 constant_dynamic-update-slice_fusion.14
  1058.3 9.8 collective-permute-done.8
  1068.1 2.0 collective-permute-start.13
  1070.1 2.7 constant_dynamic-update-slice_fusion.13
  1072.8 5.2 collective-permute-done.9
  1078.5 2.7 constant_dynamic-update-slice_fusion.12
  1081.2 20.6 %collective-permute-done.10 = f32[768,512]{1,0:T(8,128)} collective-permute-done((f32[768,512]{1,0:T(8,128)}, f32[768,512]{1,0:T(8,128)}, u32[]{:S(2)}, u32[]{:S(2)}) %collective-permute-start.10) | collective-permute-done | bytes 1572896 | tf_op jit(solution)/shard_map/ppermute | solution.py:365
  1101.8 2.0 collective-permute-start.15
  1103.8 2.7 constant_dynamic-update-slice_fusion.11
  1109.0 2.7 constant_dynamic-update-slice_fusion.8
  1111.7 2.7 constant_dynamic-update-slice_fusion.7
  1114.3 2.7 constant_dynamic-update-slice_fusion.6
  1117.0 2.7 constant_dynamic-update-slice_fusion.5
  1120.9 14.5 %collective-permute-done.12 = f32[768,512]{1,0:T(8,128)S(1)} collective-permute-done((f32[768,512]{1,0:T(8,128)S(1)}, f32[768,512]{1,0:T(8,128)S(1)}, u32[]{:S(2)}, u32[]{:S(2)}) %collective-permute-start.12) | collective-permute-done | bytes 1572896 | tf_op jit(solution)/shard_map/ppermute | solution.py:365
  1136.7 8.6 collective-permute-done.13
  1146.5 20.5 %collective-permute-done.14 = f32[768,512]{1,0:T(8,128)S(1)} collective-permute-done((f32[768,512]{1,0:T(8,128)S(1)}, f32[768,512]{1,0:T(8,128)S(1)}, u32[]{:S(2)}, u32[]{:S(2)}) %collective-permute-start.14) | collective-permute-done | bytes 1572896 | tf_op jit(solution)/shard_map/ppermute | solution.py:365
  1168.3 8.6 collective-permute-done.15
  (122 shorter events, 39.3 us)
Async XLA Ops:
  8.0 3.6 copy-start
  8.0 57.8 %all-gather.8.cloned.1.call-start = ((), (), s32[]{:S(2)}) async-start(), calls=%async_computation.1 | async-start | bytes 7864320 | tf_op jit(solution)/shard_map/all_gather | solution.py:319
  11.6 3.2 copy-start.10
  12.3 1.1 copy-start.2
  12.3 2.4 copy-start.6
  14.8 0.7 copy-start.15
  14.8 48.9 %copy-start.8 = (f32[768]{0:T(1024)S(1)}, f32[768]{0:T(1024)}, u32[]{:S(2)}) copy-start(f32[768]{0:T(1024)} %param.8) | copy-start | bytes 9220
  14.8 381.0 %reduce-scatter.2.cloned.1.call-start = ((), (), s32[]{:S(2)}) async-start(), calls=%async_computation.2 | async-start | bytes 7864320 | tf_op jit(solution)/shard_map/reduce_scatter | solution.py:351
  63.4 35.3 %copy-start.14 = (s32[32]{0:T(128)}, s32[32]{0:T(128)S(1)}, u32[]{:S(2)}) copy-start(s32[32]{0:T(128)S(1)} %sub.139.offs_ref) | copy-start | bytes 388
  63.6 40.6 %copy-start.16 = (s32[4]{0:T(128)}, s32[4]{0:T(128)S(1)}, u32[]{:S(2)}) copy-start(s32[4]{0:T(128)S(1)} %fusion.15.kept_ref) | copy-start | bytes 52
  181.9 56.9 %copy-start.5 = (f32[32,8,512]{2,1,0:T(8,128)}, f32[32,8,512]{2,1,0:T(8,128)S(1)}, u32[]{:S(2)}) copy-start(f32[32,8,512]{2,1,0:T(8,128)S(1)} %stack.160.aux_ref) | copy-start | bytes 1572868
  238.8 8.5 copy-start.12
  238.8 157.0 %copy-start.3 = (f32[512,768]{1,0:T(8,128)S(1)}, f32[512,768]{1,0:T(8,128)}, u32[]{:S(2)}) copy-start(f32[512,768]{1,0:T(8,128)} %copy-done.2) | copy-start | bytes 4718596
  238.8 157.0 %copy-start.7 = (f32[512]{0:T(512)S(1)}, f32[512]{0:T(512)}, u32[]{:S(2)}) copy-start(f32[512]{0:T(512)} %copy-done.6) | copy-start | bytes 6148
  238.8 157.0 %copy-start.9 = (f32[768]{0:T(1024)S(1)}, f32[768]{0:T(1024)}, u32[]{:S(2)}) copy-start(f32[768]{0:T(1024)} %param.8) | copy-start | bytes 9220
  238.8 376.0 %all-gather.10.cloned.1.call-start = ((), (), s32[]{:S(2)}) async-start(), calls=%async_computation.3 | async-start | bytes 51904512 | tf_op jit(solution)/shard_map/all_gather | solution.py:322
  248.6 193.1 %copy-start.11 = (s32[1,512]{1,0:T(1,128)S(1)}, s32[1,512]{1,0:T(1,128)}, u32[]{:S(2)}) copy-start(s32[1,512]{1,0:T(1,128)} %copy-done.10) | copy-start | bytes 6148
  395.8 45.9 %copy-start.4 = (f32[512,768]{1,0:T(8,128)S(1)}, f32[512,768]{1,0:T(8,128)}, u32[]{:S(2)}) copy-start(f32[512,768]{1,0:T(8,128)} %reduce-scatter.2.cloned.1.call-done) | copy-start | bytes 4718596
  441.2 2.4 copy-start.13
  682.0 290.9 %collective-permute-start = (f32[768,512]{1,0:T(8,128)}, f32[768,512]{1,0:T(8,128)}, u32[]{:S(2)}, u32[]{:S(2)}) collective-permute-start(f32[768,512]{1,0:T(8,128)} %get-tuple-element.64), channel_id=1, source_target_pairs={{0,4},{4,0},{8,12},{12,8},{16,20},{20,16},{24,28},{28,24},{1,5},{5... | collective-permute-start | bytes 4718600 | tf_op jit(solution)/shard_map/ppermute | solution.py:365
  707.2 289.5 %collective-permute-start.1 = (f32[768,512]{1,0:T(8,128)}, f32[768,512]{1,0:T(8,128)}, u32[]{:S(2)}, u32[]{:S(2)}) collective-permute-start(f32[768,512]{1,0:T(8,128)} %get-tuple-element.65), channel_id=1, source_target_pairs={{0,8},{4,12},{8,0},{12,4},{16,24},{20,28},{24,16},{28,20},{1,9},{5... | collective-permute-start | bytes 4718600 | tf_op jit(solution)/shard_map/ppermute | solution.py:365
  731.1 266.3 %collective-permute-start.2 = (f32[768,512]{1,0:T(8,128)}, f32[768,512]{1,0:T(8,128)}, u32[]{:S(2)}, u32[]{:S(2)}) collective-permute-start(f32[768,512]{1,0:T(8,128)} %get-tuple-element.66), channel_id=1, source_target_pairs={{0,4},{4,0},{8,12},{12,8},{16,20},{20,16},{24,28},{28,24},{1,5},{5... | collective-permute-start | bytes 4718600 | tf_op jit(solution)/shard_map/ppermute | solution.py:365
  755.5 243.9 %collective-permute-start.3 = (f32[768,512]{1,0:T(8,128)}, f32[768,512]{1,0:T(8,128)}, u32[]{:S(2)}, u32[]{:S(2)}) collective-permute-start(f32[768,512]{1,0:T(8,128)} %get-tuple-element.67), channel_id=1, source_target_pairs={{0,8},{4,12},{8,0},{12,4},{16,24},{20,28},{24,16},{28,20},{1,9},{5... | collective-permute-start | bytes 4718600 | tf_op jit(solution)/shard_map/ppermute | solution.py:365
  781.3 243.5 %collective-permute-start.4 = (f32[768,512]{1,0:T(8,128)}, f32[768,512]{1,0:T(8,128)}, u32[]{:S(2)}, u32[]{:S(2)}) collective-permute-start(f32[768,512]{1,0:T(8,128)} %get-tuple-element.68), channel_id=1, source_target_pairs={{0,4},{4,0},{8,12},{12,8},{16,20},{20,16},{24,28},{28,24},{1,5},{5... | collective-permute-start | bytes 4718600 | tf_op jit(solution)/shard_map/ppermute | solution.py:365
  972.9 52.0 %collective-permute-start.5 = (f32[768,512]{1,0:T(8,128)}, f32[768,512]{1,0:T(8,128)S(1)}, u32[]{:S(2)}, u32[]{:S(2)}) collective-permute-start(f32[768,512]{1,0:T(8,128)} %get-tuple-element.69), channel_id=1, source_target_pairs={{0,8},{4,12},{8,0},{12,4},{16,24},{20,28},{24,16},{28,20},{1,9},{5... | collective-permute-start | bytes 4718600 | tf_op jit(solution)/shard_map/ppermute | solution.py:365
  996.7 52.5 %collective-permute-start.6 = (f32[768,512]{1,0:T(8,128)}, f32[768,512]{1,0:T(8,128)S(1)}, u32[]{:S(2)}, u32[]{:S(2)}) collective-permute-start(f32[768,512]{1,0:T(8,128)} %get-tuple-element.70), channel_id=1, source_target_pairs={{0,4},{4,0},{8,12},{12,8},{16,20},{20,16},{24,28},{28,24},{1,5},{5... | collective-permute-start | bytes 4718600 | tf_op jit(solution)/shard_map/ppermute | solution.py:365
  997.4 56.7 %collective-permute-start.7 = (f32[768,512]{1,0:T(8,128)}, f32[768,512]{1,0:T(8,128)}, u32[]{:S(2)}, u32[]{:S(2)}) collective-permute-start(f32[768,512]{1,0:T(8,128)} %get-tuple-element.71), channel_id=1, source_target_pairs={{0,8},{4,12},{8,0},{12,4},{16,24},{20,28},{24,16},{28,20},{1,9},{5... | collective-permute-start | bytes 4718600 | tf_op jit(solution)/shard_map/ppermute | solution.py:365
  999.4 68.7 %collective-permute-start.8 = (f32[768,512]{1,0:T(8,128)}, f32[768,512]{1,0:T(8,128)}, u32[]{:S(2)}, u32[]{:S(2)}) collective-permute-start(f32[768,512]{1,0:T(8,128)} %get-tuple-element.72), channel_id=1, source_target_pairs={{0,4},{4,0},{8,12},{12,8},{16,20},{20,16},{24,28},{28,24},{1,5},{5... | collective-permute-start | bytes 4718600 | tf_op jit(solution)/shard_map/ppermute | solution.py:365
  1024.8 53.2 %collective-permute-start.9 = (f32[768,512]{1,0:T(8,128)}, f32[768,512]{1,0:T(8,128)}, u32[]{:S(2)}, u32[]{:S(2)}) collective-permute-start(f32[768,512]{1,0:T(8,128)} %get-tuple-element.73), channel_id=1, source_target_pairs={{0,8},{4,12},{8,0},{12,4},{16,24},{20,28},{24,16},{28,20},{1,9},{5... | collective-permute-start | bytes 4718600 | tf_op jit(solution)/shard_map/ppermute | solution.py:365
  1024.9 76.9 %collective-permute-start.10 = (f32[768,512]{1,0:T(8,128)}, f32[768,512]{1,0:T(8,128)}, u32[]{:S(2)}, u32[]{:S(2)}) collective-permute-start(f32[768,512]{1,0:T(8,128)} %get-tuple-element.74), channel_id=1, source_target_pairs={{0,4},{4,0},{8,12},{12,8},{16,20},{20,16},{24,28},{28,24},{1,5},{5... | collective-permute-start | bytes 4718600 | tf_op jit(solution)/shard_map/ppermute | solution.py:365
  1049.3 70.4 %collective-permute-start.11 = (f32[768,512]{1,0:T(8,128)}, f32[768,512]{1,0:T(8,128)S(1)}, u32[]{:S(2)}, u32[]{:S(2)}) collective-permute-start(f32[768,512]{1,0:T(8,128)} %get-tuple-element.75), channel_id=1, source_target_pairs={{0,8},{4,12},{8,0},{12,4},{16,24},{20,28},{24,16},{28,20},{1,9},{5... | collective-permute-start | bytes 4718600 | tf_op jit(solution)/shard_map/ppermute | solution.py:365
  1051.3 2.8 copy-start.17
  1054.1 14.0 %copy-start.18 = (f32[768,512]{1,0:T(8,128)S(1)}, f32[768,512]{1,0:T(8,128)}, u32[]{:S(2)}) copy-start(f32[768,512]{1,0:T(8,128)} %get-tuple-element.77) | copy-start | bytes 4718596
  1054.1 81.3 %collective-permute-start.12 = (f32[768,512]{1,0:T(8,128)S(1)}, f32[768,512]{1,0:T(8,128)S(1)}, u32[]{:S(2)}, u32[]{:S(2)}) collective-permute-start(f32[768,512]{1,0:T(8,128)S(1)} %copy-done.17), channel_id=1, source_target_pairs={{0,4},{4,0},{8,12},{12,8},{16,20},{20,16},{24,28},{28,24},{1,5},{5... | collective-permute-start | bytes 4718600 | tf_op jit(solution)/shard_map/ppermute | solution.py:365
  1068.1 9.8 copy-start.19
  1068.1 77.1 %collective-permute-start.13 = (f32[768,512]{1,0:T(8,128)S(1)}, f32[768,512]{1,0:T(8,128)S(1)}, u32[]{:S(2)}, u32[]{:S(2)}) collective-permute-start(f32[768,512]{1,0:T(8,128)S(1)} %copy-done.18), channel_id=1, source_target_pairs={{0,8},{4,12},{8,0},{12,4},{16,24},{20,28},{24,16},{28,20},{1,9},{5... | collective-permute-start | bytes 4718600 | tf_op jit(solution)/shard_map/ppermute | solution.py:365
  1077.9 23.9 %copy-start.20 = (f32[768,512]{1,0:T(8,128)S(1)}, f32[768,512]{1,0:T(8,128)}, u32[]{:S(2)}) copy-start(f32[768,512]{1,0:T(8,128)} %get-tuple-element.79) | copy-start | bytes 4718596
  1077.9 89.1 %collective-permute-start.14 = (f32[768,512]{1,0:T(8,128)S(1)}, f32[768,512]{1,0:T(8,128)S(1)}, u32[]{:S(2)}, u32[]{:S(2)}) collective-permute-start(f32[768,512]{1,0:T(8,128)S(1)} %copy-done.19), channel_id=1, source_target_pairs={{0,4},{4,0},{8,12},{12,8},{16,20},{20,16},{24,28},{28,24},{1,5},{5... | collective-permute-start | bytes 4718600 | tf_op jit(solution)/shard_map/ppermute | solution.py:365
  1101.8 75.0 %collective-permute-start.15 = (f32[768,512]{1,0:T(8,128)S(1)}, f32[768,512]{1,0:T(8,128)S(1)}, u32[]{:S(2)}, u32[]{:S(2)}) collective-permute-start(f32[768,512]{1,0:T(8,128)S(1)} %copy-done.20), channel_id=1, source_target_pairs={{0,8},{4,12},{8,0},{12,4},{16,24},{20,28},{24,16},{28,20},{1,9},{5... | collective-permute-start | bytes 4718600 | tf_op jit(solution)/shard_map/ppermute | solution.py:365
  1167.0 11.1 copy-start.1
Sparse Core Ops, SparseCore 0:
  14.9 50.1 all-gather.7
  238.9 156.8 reduce-scatter.1
Sparse Core Ops, SparseCore 1:
  242.2 372.6 all-gather.9

commit v2 on v1

v2 whole, which is shorter than its diff:
```python
import functools

import jax
import jax.numpy as jnp
from jax import lax
from jax.experimental import pallas as pl
from jax.experimental.pallas import tpu as pltpu
from jax.sharding import PartitionSpec as P


EPS = 1e-5
BLK = 512
DIM = 768
ALIGN = 16
FWD_COLS = 1024
DN_COLS = 2048
DW_COLS = 512
DW_STEPS = 2
DW_TOK = 1024
SUB = 256
LAG = 3
DROPPED = 1e30


f32, bf16, i32 = jnp.float32, jnp.bfloat16, jnp.int32


def tiny_gather_kernel(dp_count, vp_count, x_ref, out_ref, send_sems, recv_sems):
    count = dp_count * vp_count
    me = lax.axis_index("dp") * vp_count + lax.axis_index("vp")
    barrier = pltpu.get_barrier_semaphore()

    def peer(k):
        other = lax.rem(me + k, count)
        return (other // vp_count, lax.rem(other, vp_count))

    for k in range(1, count):
        pl.semaphore_signal(barrier, inc=1, device_id=peer(k), device_id_type=pl.DeviceIdType.MESH)
    pl.semaphore_wait(barrier, count - 1)
    copies = [
        pltpu.make_async_remote_copy(
            src_ref=x_ref,
            dst_ref=out_ref.at[me],
            send_sem=send_sems.at[k - 1],
            recv_sem=recv_sems.at[k - 1],
            device_id=peer(k),
            device_id_type=pl.DeviceIdType.MESH,
        )
        for k in range(1, count)
    ]
    for copy in copies:
        copy.start()
    out_ref[me] = x_ref[...]
    for copy in copies:
        copy.wait()


def tiny_gather(x, mesh_shape, collective_id):
    dp_count, vp_count = mesh_shape
    count = dp_count * vp_count
    return pl.pallas_call(
        functools.partial(tiny_gather_kernel, dp_count, vp_count),
        out_shape=jax.ShapeDtypeStruct((count, 8, 128), f32),
        in_specs=[pl.BlockSpec(memory_space=pltpu.VMEM)],
        out_specs=pl.BlockSpec(memory_space=pltpu.VMEM),
        scratch_shapes=[pltpu.SemaphoreType.DMA((count - 1,)), pltpu.SemaphoreType.DMA((count - 1,))],
        compiler_params=pltpu.CompilerParams(collective_id=collective_id, has_side_effects=True),
        name="tiny_gather",
    )(x)


def place_masked(dst, off, span, new):
    rows = pl.ds(pl.multiple_of(off, ALIGN), BLK)
    live = lax.broadcasted_iota(i32, (BLK, 1), 0) < span
    dst[rows, :] = jnp.where(live, new, dst[rows, :].astype(f32)).astype(dst.dtype)


def aux_columns(aux):
    pad = jnp.zeros((120, BLK), f32)
    return jnp.concatenate([aux, pad], axis=0).T


def fwd_kernel(offs_ref, span_ref, nt_ref, xa, xb, xc, xd, g_ref, w_ref, n_ref, st_ref, m_ref, s_ref, z_ref):
    j = pl.program_id(0)
    steps = nt_ref[0]

    @pl.when(j == 0)
    def _():
        n_ref[...] = jnp.zeros_like(n_ref)
        m_ref[...] = jnp.full_like(m_ref, -DROPPED)
        s_ref[...] = jnp.zeros_like(s_ref)
        for k, x_ref in enumerate((xa, xb, xc, xd)):
            place_masked(n_ref, offs_ref[k], span_ref[k], x_ref[...] * g_ref[...])

    def absorb(rows, z):
        parts = [z[:, k * 128 : (k + 1) * 128] for k in range(FWD_COLS // 128)]
        m_old = m_ref[rows, :]
        m_new = functools.reduce(jnp.maximum, parts, m_old)
        total = s_ref[rows, :] * jnp.exp(m_old - m_new)
        for part in parts:
            total += jnp.exp(part - m_new)
        m_ref[rows, :] = m_new
        s_ref[rows, :] = total

    def rows_of(i, u):
        return pl.ds(pl.multiple_of(i * BLK, BLK) + u * SUB, SUB)

    z_ref[...] = jnp.full_like(z_ref, -DROPPED)

    def tile(i, carry):
        z = jnp.dot(n_ref[rows_of(i, 0), :], w_ref[...], preferred_element_type=f32)
        absorb(rows_of(jnp.maximum(i - 1, 0), 1), z_ref[...])
        z_ref[...] = jnp.dot(n_ref[rows_of(i, 1), :], w_ref[...], preferred_element_type=f32)
        absorb(rows_of(i, 0), z)
        return carry

    lax.fori_loop(0, steps, tile, 0)
    absorb(rows_of(jnp.maximum(steps - 1, 0), 1), z_ref[...])

    @pl.when(j == pl.num_programs(0) - 1)
    def _():
        for k in range(4):
            rows = pl.ds(pl.multiple_of(offs_ref[k], ALIGN), BLK)
            m_lane = m_ref[rows, :]
            m = jnp.max(m_lane, axis=1, keepdims=True)
            s = jnp.sum(s_ref[rows, :] * jnp.exp(m_lane - m), axis=1, keepdims=True)
            st_ref[k, 0:1, :] = jnp.broadcast_to(m, (BLK, 128)).T[0:1, :]
            st_ref[k, 1:2, :] = jnp.broadcast_to(s, (BLK, 128)).T[0:1, :]


def forward_stats(offs, span, ntiles, blocks, g, w):
    vocab = w.shape[1]
    return pl.pallas_call(
        fwd_kernel,
        grid_spec=pltpu.PrefetchScalarGridSpec(
            num_scalar_prefetch=3,
            grid=(vocab // FWD_COLS,),
            in_specs=[pl.BlockSpec((BLK, DIM), lambda j, *_: (0, 0))] * 4
            + [
                pl.BlockSpec((1, DIM), lambda j, *_: (0, 0)),
                pl.BlockSpec((DIM, FWD_COLS), lambda j, *_: (0, j)),
            ],
            out_specs=[
                pl.BlockSpec((4 * BLK, DIM), lambda j, *_: (0, 0)),
                pl.BlockSpec((4, 2, BLK), lambda j, *_: (0, 0, 0)),
            ],
            scratch_shapes=[
                pltpu.VMEM((4 * BLK, 128), f32),
                pltpu.VMEM((4 * BLK, 128), f32),
                pltpu.VMEM((SUB, FWD_COLS), f32),
            ],
        ),
        out_shape=[
            jax.ShapeDtypeStruct((4 * BLK, DIM), bf16),
            jax.ShapeDtypeStruct((4, 2, BLK), f32),
        ],
        compiler_params=pltpu.CompilerParams(dimension_semantics=("arbitrary",)),
        cost_estimate=pl.CostEstimate(
            flops=2 * 4 * BLK * DIM * vocab, bytes_accessed=2 * DIM * vocab + 10 * BLK * DIM * 4, transcendentals=4 * BLK * vocab
        ),
        name="fwd_stats",
    )(offs, span, ntiles, *blocks, g, w)


def grad_logits(z, aux, col0):
    target = aux[:, 2:3].astype(i32) - col0
    hot = lax.broadcasted_iota(i32, z.shape, 1) == target
    p = jnp.exp(z - aux[:, 0:1])
    dz = (jnp.where(hot, p - 1.0, p) * aux[:, 1:2]).astype(bf16)
    return dz, hot


def dn_kernel(offs_ref, span_ref, kept_ref, nt_ref, col_ref, n_ref, aux_ref, w_ref, dn_ref, tl_ref, acc_ref, auxc_ref, dz_ref):
    j = pl.program_id(0)

    @pl.when(j == 0)
    def _():
        acc_ref[...] = jnp.zeros_like(acc_ref)
        auxc_ref[...] = jnp.zeros_like(auxc_ref)
        tl_ref[...] = jnp.zeros_like(tl_ref)
        for b in range(4):
            place_masked(auxc_ref, offs_ref[b], span_ref[b], aux_columns(aux_ref[b]))

    col0 = col_ref[0] + j * DN_COLS

    def tile(i, carry):
        rows = pl.ds(pl.multiple_of(i * BLK, BLK), BLK)
        aux = auxc_ref[rows, :]
        n = n_ref[rows, :]
        found = jnp.zeros((BLK, 128), f32)
        for c in range(DN_COLS // 512):
            z = jnp.dot(n, w_ref[:, c * 512 : (c + 1) * 512], preferred_element_type=f32)
            dz, hot = grad_logits(z, aux, col0 + c * 512)
            dz_ref[:, c * 512 : (c + 1) * 512] = dz
            picked = jnp.where(hot, z, 0.0)
            for k in range(4):
                found += picked[:, k * 128 : (k + 1) * 128]
        tl_ref[...] += jnp.sum((found * aux[:, 1:2]).reshape(BLK // 8, 8, 128), axis=0)
        acc_ref[rows, :] += lax.dot_general(dz_ref[...], w_ref[...], (((1,), (1,)), ((), ())), preferred_element_type=f32)
        return carry

    lax.fori_loop(0, nt_ref[0], tile, 0)

    @pl.when(j == pl.num_programs(0) - 1)
    def _():
        for b in range(4):
            got = acc_ref[pl.ds(pl.multiple_of(offs_ref[b], ALIGN), BLK), :]
            live = lax.broadcasted_iota(i32, (BLK, 1), 0) < kept_ref[b]
            dn_ref[pl.ds(b * BLK, BLK), :] = jnp.where(live, got, 0.0)


def backward_dn(offs, span, kept, ntiles, col0, n_row, aux_row, w):
    vocab = w.shape[1]
    return pl.pallas_call(
        dn_kernel,
        grid_spec=pltpu.PrefetchScalarGridSpec(
            num_scalar_prefetch=5,
            grid=(vocab // DN_COLS,),
            in_specs=[
                pl.BlockSpec((4 * BLK, DIM), lambda j, *_: (0, 0)),
                pl.BlockSpec((4, 8, BLK), lambda j, *_: (0, 0, 0)),
                pl.BlockSpec((DIM, DN_COLS), lambda j, *_: (0, j)),
            ],
            out_specs=[
                pl.BlockSpec((4 * BLK, DIM), lambda j, *_: (0, 0)),
                pl.BlockSpec((8, 128), lambda j, *_: (0, 0)),
            ],
            scratch_shapes=[
                pltpu.VMEM((4 * BLK, DIM), f32),
                pltpu.VMEM((4 * BLK, 128), f32),
                pltpu.VMEM((BLK, DN_COLS), bf16),
            ],
        ),
        out_shape=[
            jax.ShapeDtypeStruct((4 * BLK, DIM), f32),
            jax.ShapeDtypeStruct((8, 128), f32),
        ],
        compiler_params=pltpu.CompilerParams(dimension_semantics=("arbitrary",)),
        cost_estimate=pl.CostEstimate(
            flops=4 * 4 * BLK * DIM * vocab, bytes_accessed=2 * DIM * vocab + 6 * BLK * DIM * 4, transcendentals=4 * BLK * vocab
        ),
        name="backward_dn",
    )(offs, span, kept, ntiles, col0, n_row, aux_row, w)


def gather_kernel(offs_ref, xh_ref, g_ref, aux_ref, n_hbm, aux_hbm, n_ref, auxc_ref, sems):
    step = pl.program_id(0)
    last = pl.num_programs(0) - 1
    tokens = n_ref.shape[0]
    chunks = tokens // DW_TOK

    @pl.when(step == 0)
    def _():
        def clear(i, carry):
            rows = pl.ds(pl.multiple_of(i * BLK, BLK), BLK)
            n_ref[rows, :] = jnp.zeros((BLK, DIM), bf16)
            auxc_ref[rows, :] = jnp.zeros((BLK, 128), f32)
            return carry

        lax.fori_loop(0, tokens // BLK, clear, 0)

    def copies(q):
        rows = pl.ds(q * DW_TOK, DW_TOK)
        return (
            pltpu.make_async_copy(n_ref.at[rows, :], n_hbm.at[rows, :], sems.at[q, 0]),
            pltpu.make_async_copy(auxc_ref.at[rows, :], aux_hbm.at[rows, :], sems.at[q, 1]),
        )

    def block(k, carry):
        off = pl.multiple_of(offs_ref[step * 4 + k], ALIGN)
        src = pl.ds(pl.multiple_of(k * BLK, BLK), BLK)
        n_ref[pl.ds(off, BLK), :] = (xh_ref[src, :] * g_ref[...]).astype(bf16)
        auxc_ref[pl.ds(off, BLK), :] = aux_columns(aux_ref[k])
        return carry

    lax.fori_loop(0, 4, block, 0)
    before, after = offs_ref[step * 4], offs_ref[step * 4 + 4]
    reach = jnp.where(step == last, after + DW_TOK - 1, after)
    for q in range(chunks):
        end = (q + 1) * DW_TOK

        @pl.when((end <= reach) & (end > before))
        def _():
            for copy in copies(q):
                copy.start()

    @pl.when(step == last)
    def _():
        for q in range(chunks):

            @pl.when(q * DW_TOK < after)
            def _():
                for copy in copies(q):
                    copy.wait()


def gather_tokens(offs, xh_all, g, aux_all):
    blocks = aux_all.shape[0]
    tokens = blocks * BLK
    anywhere = pl.BlockSpec(memory_space=pl.ANY)
    return pl.pallas_call(
        gather_kernel,
        grid_spec=pltpu.PrefetchScalarGridSpec(
            num_scalar_prefetch=1,
            grid=(blocks // 4,),
            in_specs=[
                pl.BlockSpec((4 * BLK, DIM), lambda b, *_: (b, 0)),
                pl.BlockSpec((1, DIM), lambda b, *_: (0, 0)),
                pl.BlockSpec((4, 8, BLK), lambda b, *_: (b, 0, 0)),
            ],
            out_specs=[anywhere, anywhere],
            scratch_shapes=[
                pltpu.VMEM((tokens, DIM), bf16),
                pltpu.VMEM((tokens, 128), f32),
                pltpu.SemaphoreType.DMA((tokens // DW_TOK, 2)),
            ],
        ),
        out_shape=[
            jax.ShapeDtypeStruct((tokens, DIM), bf16),
            jax.ShapeDtypeStruct((tokens, 128), f32),
        ],
        compiler_params=pltpu.CompilerParams(dimension_semantics=("arbitrary",), vmem_limit_bytes=56 << 20),
        cost_estimate=pl.CostEstimate(flops=2 * tokens * DIM, bytes_accessed=6 * tokens * DIM, transcendentals=0),
        name="gather_tokens",
    )(offs, xh_all, g, aux_all)


def dw_kernel(merge, place_ref, nt_ref, n_hbm, aux_hbm, w_ref, *rest):
    out_ref, all_hbm, nbuf, abuf, dz_ref, sems, own_sems = rest[-7 - 2 * merge : len(rest) - 2 * merge]
    s = pl.program_id(0)
    steps = nt_ref[0]

    def fetch(i, slot):
        rows = pl.ds(pl.multiple_of(i * DW_TOK, DW_TOK), DW_TOK)
        return (
            pltpu.make_async_copy(n_hbm.at[rows, :], nbuf.at[slot], sems.at[slot, 0]),
            pltpu.make_async_copy(aux_hbm.at[rows, :], abuf.at[slot], sems.at[slot, 1]),
        )

    def keep(step):
        cols = pl.ds(pl.multiple_of((place_ref[0] + step) * DW_COLS, DW_COLS), DW_COLS)
        return pltpu.make_async_copy(out_ref, all_hbm.at[:, cols], own_sems.at[step])

    if merge:
        recv_hbm, (mbuf, msems) = rest[-10], rest[-2:]
        cols = pl.ds(pl.multiple_of(place_ref[2], DW_COLS), DW_COLS * DW_STEPS)
        merge_in = pltpu.make_async_copy(recv_hbm, mbuf, msems.at[0])
        merge_out = pltpu.make_async_copy(mbuf, all_hbm.at[:, cols], msems.at[1])

    @pl.when(s == 0)
    def _():
        for copy in fetch(0, 0):
            copy.start()
        if merge:
            merge_in.start()

    out_ref[...] = jnp.zeros_like(out_ref)
    col0 = place_ref[1] + s * DW_COLS

    def tile(i, carry):
        g = s * steps + i
        slot = lax.rem(g, 2)

        @pl.when(g + 1 < DW_STEPS * steps)
        def _():
            for copy in fetch(jnp.where(i + 1 < steps, i + 1, 0), 1 - slot):
                copy.start()

        for copy in fetch(i, slot):
            copy.wait()
        for u in range(DW_TOK // SUB):
            rows = pl.ds(u * SUB, SUB)
            z = jnp.dot(nbuf[slot, rows, :], w_ref[...], preferred_element_type=f32)
            dz_ref[rows, :], _ = grad_logits(z, abuf[slot, rows, :], col0)
        out_ref[...] += lax.dot_general(nbuf[slot], dz_ref[...], (((0,), (0,)), ((), ())), preferred_element_type=f32)
        return carry

    lax.fori_loop(0, steps, tile, 0)
    for step in range(DW_STEPS):

        @pl.when(s == step)
        def _():
            keep(step).start()
            if merge and step == 0:
                merge_in.wait()
                merge_out.start()
            if step == DW_STEPS - 1:
                for done in range(DW_STEPS):
                    keep(done).wait()
                if merge:
                    merge_out.wait()


def weight_grad(place, ntiles, n_all, aux_all, w, whole, recv):
    tokens, vocab = n_all.shape[0], w.shape[1]
    width = DW_COLS * DW_STEPS
    anywhere = pl.BlockSpec(memory_space=pl.ANY)
    held = [a for a in (whole, recv) if a is not None]
    merge = recv is not None
    scratch = [
        pltpu.VMEM((2, DW_TOK, DIM), bf16),
        pltpu.VMEM((2, DW_TOK, 128), f32),
        pltpu.VMEM((DW_TOK, DW_COLS), bf16),
        pltpu.SemaphoreType.DMA((2, 2)),
        pltpu.SemaphoreType.DMA((DW_STEPS,)),
    ]
    if merge:
        scratch += [pltpu.VMEM((DIM, width), f32), pltpu.SemaphoreType.DMA((2,))]
    return pl.pallas_call(
        functools.partial(dw_kernel, merge),
        grid_spec=pltpu.PrefetchScalarGridSpec(
            num_scalar_prefetch=2,
            grid=(DW_STEPS,),
            in_specs=[anywhere, anywhere, pl.BlockSpec((DIM, DW_COLS), lambda s, place, nt: (0, place[0] + s))]
            + [anywhere] * len(held),
            out_specs=[pl.BlockSpec((DIM, DW_COLS), lambda s, *_: (0, s)), anywhere],
            scratch_shapes=scratch,
        ),
        out_shape=[
            jax.ShapeDtypeStruct((DIM, width), f32),
            jax.ShapeDtypeStruct((DIM, vocab), f32),
        ],
        input_output_aliases={} if whole is None else {5: 1},
        compiler_params=pltpu.CompilerParams(dimension_semantics=("arbitrary",)),
        cost_estimate=pl.CostEstimate(
            flops=2 * tokens * DIM * width, bytes_accessed=2 * tokens * DIM + 8 * DIM * width, transcendentals=tokens * width // 2
        ),
        name="weight_grad",
    )(place, ntiles.reshape(1), n_all, aux_all, w, *held)


def solution(mesh):
    dp_count, vp_count = mesh.shape["dp"], mesh.shape["vp"]
    everyone = (dp_count, vp_count)

    def local_step(hidden, targets, loss_mask, norm_scale, w_head):
        vocab = w_head.shape[1]
        dp, vp = lax.axis_index("dp"), lax.axis_index("vp")
        g = norm_scale.reshape(1, DIM)

        mask = loss_mask[0]
        idx = lax.iota(i32, BLK)
        before = jnp.sum(jnp.where(idx[None, :] < idx[:, None], mask[None, :], 0), axis=1)
        kept = jnp.sum(mask)
        pos = jnp.where(mask == 1, before, kept + idx - before)
        perm = pos[None, :] == idx[:, None]
        x_sorted = jnp.dot(perm.astype(bf16), hidden[0], preferred_element_type=f32)
        t_sorted = jnp.sum(jnp.where(perm, targets[0][None, :], 0), axis=1)
        inv_rms = lax.rsqrt(jnp.mean(x_sorted * x_sorted, axis=-1, keepdims=True) + EPS)
        x_hat = x_sorted * inv_rms

        core_pairs = [(v, v ^ 1) for v in range(vp_count)]
        x_pairs = [(v, v ^ 2) for v in range(vp_count)]
        from_x = lax.ppermute(x_hat, "vp", x_pairs)
        from_core = lax.ppermute(x_hat, "vp", core_pairs)
        xh_all = lax.all_gather(x_hat, ("dp", "vp"), axis=0, tiled=True)
        info = jnp.concatenate([t_sorted.astype(f32).reshape(4, 128), jnp.full((4, 128), kept.astype(f32))])
        info = tiny_gather(info, everyone, 1)
        from_x_core = lax.ppermute(from_x, "vp", core_pairs)
        blocks = (x_hat, from_core, from_x, from_x_core)

        t_all = info[:, :4].reshape(dp_count * vp_count, BLK)
        kept_all = info[:, 4, 0].astype(i32)
        span = (kept_all + ALIGN - 1) // ALIGN * ALIGN
        ends = jnp.cumsum(span)
        offs_all = jnp.concatenate([jnp.zeros((1,), i32), ends])
        total = ends[-1]
        weight = 1.0 / jnp.sum(kept_all).astype(f32)
        first = dp * vp_count
        kept_row = lax.dynamic_slice(kept_all, (first,), (vp_count,))
        offs_row = lax.dynamic_slice(offs_all, (first,), (vp_count,))
        span_row = lax.dynamic_slice(span, (first,), (vp_count,))
        offs_row = offs_row - offs_row[0]
        nt_row = ((jnp.sum(span_row) + BLK - 1) // BLK).reshape(1)
        nt_all = jnp.maximum((total + DW_TOK - 1) // DW_TOK, 1)

        table = jnp.stack([jnp.arange(vp_count) ^ v for v in range(vp_count)])
        mine = lax.dynamic_slice(table, (vp, 0), (1, vp_count))[0]
        pick = (mine[:, None] == jnp.arange(vp_count)[None, :]).astype(i32)
        offs_mine = jnp.sum(pick * offs_row[None, :], axis=1)
        span_mine = jnp.sum(pick * span_row[None, :], axis=1)

        n_row, stats = forward_stats(offs_mine, span_mine, nt_row, blocks, g, w_head)
        stats = lax.all_gather(stats, "vp", axis=0)
        stats = jnp.stack([jnp.stack([stats[v, b ^ v] for b in range(vp_count)]) for v in range(vp_count)])
        row_max = jnp.max(stats[:, :, 0], axis=0)
        row_sum = jnp.sum(stats[:, :, 1] * jnp.exp(stats[:, :, 0] - row_max), axis=0)
        lse_row = row_max + jnp.log(row_sum)
        lse_row = jnp.where(idx[None, :] < kept_row[:, None], lse_row, DROPPED)
        w_row = jnp.where(idx[None, :] < kept_row[:, None], weight, 0.0)
        t_row = lax.dynamic_slice(t_all, (first, 0), (vp_count, BLK))
        none = jnp.zeros_like(w_row)
        aux_row = jnp.stack([lse_row, w_row, t_row] + [none] * 5, axis=1)

        dn_part, t_part = backward_dn(
            offs_row, span_row, kept_row, nt_row, (vp * vocab).reshape(1), n_row, aux_row, w_head
        )
        d_normed = lax.psum_scatter(dn_part, "vp", scatter_dimension=0, tiled=True)

        lse_own = lax.dynamic_slice(lse_row, (vp, 0), (1, BLK))[0]
        lse_own, t_part = lax.optimization_barrier((lse_own, t_part))
        lse_all = tiny_gather(jnp.concatenate([lse_own.reshape(4, 128), jnp.zeros((4, 128), f32)]), everyone, 2)
        lse_all = lse_all[:, :4].reshape(dp_count * vp_count, BLK)
        w_all = jnp.where(idx[None, :] < kept_all[:, None], weight, 0.0)
        none = jnp.zeros_like(w_all)
        aux_all = jnp.stack([lse_all, w_all, t_all] + [none] * 5, axis=1)
        n_all, auxc_all = gather_tokens(offs_all, xh_all, g, aux_all)

        d_scale = jnp.sum(d_normed * x_hat, axis=0)
        e = d_normed * norm_scale
        d_x = inv_rms * (e - x_hat * jnp.mean(e * x_hat, axis=-1, keepdims=True))
        back = perm.astype(bf16).T
        d_x = jnp.dot(back, d_x.astype(bf16), preferred_element_type=f32).astype(bf16)
        loss_part = weight * jnp.sum(jnp.where(idx < kept, lse_own, 0.0)) - jnp.sum(t_part)
        parts = jnp.concatenate([d_scale.reshape(6, 128), jnp.full((2, 128), loss_part, f32)])
        parts = jnp.sum(tiny_gather(parts, everyone, 3), axis=0)

        half, quarter, width = vocab // 2, vocab // 4, DW_COLS * DW_STEPS
        y_pos, z_pos = dp % 2, (dp // 2) % 2
        y_pairs = [(d, d ^ 1) for d in range(dp_count)]
        z_pairs = [(d, d ^ 2) for d in range(dp_count)]
        jobs = [
            (base + where * quarter + c * width, base + (1 - where) * quarter + c * width, pairs)
            for c in range(quarter // width)
            for base, where, pairs in ((0, y_pos, y_pairs), (half, z_pos, z_pairs))
        ]
        whole, moved = None, []
        for k, (col, other, pairs) in enumerate(jobs):
            if k == len(jobs) - 2:
                n_all, parts, d_x = lax.optimization_barrier((n_all, parts, d_x))
            ahead = moved[k - LAG] if k >= LAG else (0, None)
            place = jnp.stack([col // DW_COLS, vp * vocab + col, ahead[0]]).astype(i32)
            chunk, whole = weight_grad(place, nt_all, n_all, auxc_all, w_head, whole, ahead[1])
            moved.append((other, lax.ppermute(chunk, "dp", pairs)))
        for other, chunk in moved[-LAG:]:
            whole = lax.dynamic_update_slice(whole, chunk, (0, other))
        return parts[6, 0], d_x[None], whole, parts[:6].reshape(DIM)

    return jax.shard_map(
        local_step,
        mesh=mesh,
        in_specs=(P("dp", "vp", None), P("dp", "vp"), P("dp", "vp"), P(None), P(None, "vp")),
        out_specs=(P(), P("dp", "vp", None), P(None, "vp"), P(None)),
        check_vma=False,
    )
```

time: 1200 us -> 926 us (0.77); the launches traced: 1190 us -> 925 us
  blocking collectives: 170 us -> 5.63 us
  waiting for transfers between devices: 407 us -> 300 us
  Pallas kernels: 513 us -> 542 us
  local copies, waits for them, and re-layouts: 38.2 us -> 22.7 us
    all_gather x3 -> x0, blocking collectives: 164 us -> none  [the longest x1 76.8 us: local_step(): lse_all = lax.all_gather(lse_row, 'dp', axis=0, tiled=True)]
    reduce_scatter x1, waiting for transfers between devices: 147 us -> 38.2 us  [local_step(): d_normed = lax.psum_scatter(dn_part, 'vp', scatter_dimension=0, tiled=True)]
    pallas_call x16 -> x11, Pallas kernels: 380 us -> 440 us  [the longest x8 272 us: weight_grad(): pl.pallas_call(functools.partial(dw_kernel, merge), grid_spec=pltpu.Prefe...]
    all_gather x1, waiting for transfers between devices: 171 us -> 202 us  [local_step(): xh_all = lax.all_gather(x_hat, ('dp', 'vp'), axis=0, tiled=True)]
    ppermute x16 -> x8, waiting for transfers between devices: 87.8 us -> 59.9 us  [local_step(): moved.append((other, lax.ppermute(chunk, 'dp', pairs)))]
    dynamic_update_slice x16 -> x3, local copies, waits for them, and re-layouts: 33 us -> 12 us  [local_step(): whole = lax.dynamic_update_slice(whole, chunk, (0, other))]
    pallas_call x1, Pallas kernels: 43.3 us -> 26.8 us  [gather_tokens(): pl.pallas_call(gather_kernel, grid_spec=pltpu.PrefetchScalarGridSpec(num_...]
    pallas_call x1, Pallas kernels: 56.2 us -> 39.9 us  [backward_dn(): pl.pallas_call(dn_kernel, grid_spec=pltpu.PrefetchScalarGridSpec(num_scal...]
  transfers between devices with their start and end apart: 19 -> 13, of which waited for: 9 -> 5; matrix products, arithmetic and copies ran while one was open for 4% -> 4% of each run, Pallas kernels for 30% -> 44%
where the time goes in v2:
time: 926 us; the launch traced here: 925 us
  Pallas kernels  542 us (59%)
  waiting for transfers between devices  300 us (32%)
  local copies, waits for them, and re-layouts  22.7 us (2%)
  between operations  20.1 us (2%)
  other arithmetic  20 us (2%)
  starting transfers between devices  10.8 us (1%)
    pallas_call x8, Pallas kernels, weight_grad(): pl.pallas_call(functools.partial(dw_kernel, merge), grid_spec=pltpu.Prefe...  272 us
    all_gather x1, waiting for transfers between devices, local_step(): xh_all = lax.all_gather(x_hat, ('dp', 'vp'), axis=0, tiled=True)  202 us
    pallas_call x3, Pallas kernels, tiny_gather(): pl.pallas_call(functools.partial(tiny_gather_kernel, dp_count, vp_count),...  168 us
    ppermute x8, waiting for transfers between devices, local_step(): moved.append((other, lax.ppermute(chunk, 'dp', pairs)))  59.9 us
    pallas_call x1, Pallas kernels, backward_dn(): pl.pallas_call(dn_kernel, grid_spec=pltpu.PrefetchScalarGridSpec(num_scal...  39.9 us
    reduce_scatter x1, waiting for transfers between devices, local_step(): d_normed = lax.psum_scatter(dn_part, 'vp', scatter_dimension=0, tiled=True)  38.2 us
    pallas_call x1, Pallas kernels, forward_stats(): pl.pallas_call(fwd_kernel, grid_spec=pltpu.PrefetchScalarGridSpec(num_sca...  35.7 us
    pallas_call x1, Pallas kernels, gather_tokens(): pl.pallas_call(gather_kernel, grid_spec=pltpu.PrefetchScalarGridSpec(num_...  26.8 us
  transfers between devices with their start and end apart: 13, of which 5 were waited for; matrix products, arithmetic and copies ran while one was open for 4% of the time, Pallas kernels for 44%

profile of v2, /device:TPU:0, one launch (start us, length us, event | category | flops | bytes accessed | tf_op | source)
XLA Modules:
  0.0 924.5 jit_solution(8746148142744432634)
XLA Ops:
  8.1 0.9 select_reduce_fusion.1
  9.0 1.3 reduce_sum.130
  10.3 1.3 compare_select_fusion.4
  11.6 0.7 multiply_reduce_fusion.2
  12.3 1.1 copy-done.2
  13.6 3.0 collective-permute-start.1
  18.1 36.6 %tiny_gather.3 = f32[32,8,128]{2,1,0:T(8,128)} custom-call(f32[8,128]{1,0:T(8,128)} %concatenate.12.x_ref), custom_call_target="tpu_custom_call" | custom-call | tf_op jit(solution)/shard_map/tiny_gather/pallas_call | solution.py:61
  54.8 2.8 fusion.14
  58.1 0.7 fusion.16
  59.5 0.9 slice.97
  61.9 0.9 slice_convert_fusion
  63.0 0.7 select_reduce_fusion.3
  63.7 35.7 %fwd_stats.1 = (bf16[2048,768]{1,0:T(8,128)(2,1)}, f32[4,2,512]{2,1,0:T(2,128)}) custom-call(s32[4]{0:T(128)} %get-tuple-element.64.offs_ref, s32[4]{0:T(128)} %get-tuple-element.63.span_ref, s32[1]{0:T(128)} %bitcast.8.nt_ref, f32[512,768]{1,0:T(8,128)} %copy-done.5, f32[512,768]{1,0:T(8,128)} %collective-permute-done.xb, f32[512,768]{1,0:T(8,128)} %copy-done.25, ...), custom_call_target="tpu_custom_call" | custom-call | flops 51539607552 | bytes 40894464 | tf_op jit(solution)/shard_map/fwd_stats/pallas_call | solution.py:133
  99.5 5.6 all-gather
  105.5 0.7 stack.151.aux_ref
  106.2 39.9 %backward_dn.1 = (f32[2048,768]{1,0:T(8,128)}, f32[8,128]{1,0:T(8,128)}) custom-call(s32[4]{0:T(128)} %copy-done.24, s32[4]{0:T(128)} %copy-done.23, s32[4]{0:T(128)} %copy-done.21, s32[1]{0:T(128)} %bitcast.8.nt_ref, s32[1]{0:T(128)} %bitcast.32.col_ref, bf16[2048,768]{1,0:T(8,128)(2,1)} %get-tuple-element.32.n_ref, f32[4,8,512]{2,1,0:T(8,128)} %stack.151.aux_ref, ...), custom_call_target="tpu_custom_call" | custom-call | flops 103079215104 | bytes 34603008 | tf_op jit(solution)/shard_map/backward_dn/pallas_call | solution.py:214
  147.4 1.2 slice.120
  153.7 0.7 compare_select_fusion.3
  155.0 119.3 %tiny_gather.4 = f32[32,8,128]{2,1,0:T(8,128)} custom-call(f32[8,128]{1,0:T(8,128)} %concatenate.14.x_ref), custom_call_target="tpu_custom_call" | custom-call | tf_op jit(solution)/shard_map/tiny_gather/pallas_call | solution.py:61
  274.3 0.9 slice.98
  275.2 1.3 select_reduce_fusion.2
  278.5 1.2 stack.153.aux_ref
  279.7 38.2 %reduce-scatter.2.cloned.1.call-done = f32[512,768]{1,0:T(8,128)} async-done(((f32[2048,768]{1,0:T(8,128)}), f32[512,768]{1,0:T(8,128)}) %reduce-scatter.2.cloned.1.call-update) | async-done | bytes 1572880 | tf_op jit(solution)/shard_map/reduce_scatter | solution.py:498
  317.9 2.0 multiply_reduce_fusion
  320.5 11.9 %tiny_gather.5 = f32[32,8,128]{2,1,0:T(8,128)} custom-call(f32[8,128]{1,0:T(8,128)} %concatenate.15.x_ref), custom_call_target="tpu_custom_call" | custom-call | tf_op jit(solution)/shard_map/tiny_gather/pallas_call | solution.py:61
  332.4 1.5 reduce_sum.141
  333.9 1.8 convolution_convert_fusion
  335.7 202.0 %all-gather.3.cloned.1.call-done.xh_ref = f32[16384,768]{1,0:T(8,128)} async-done(((f32[512,768]{1,0:T(8,128)}), f32[16384,768]{1,0:T(8,128)}) %all-gather.3.cloned.1.call-update) | async-done | bytes 50331664 | tf_op jit(solution)/shard_map/all_gather | solution.py:456
  537.7 26.8 %gather_tokens.1 = (bf16[16384,768]{1,0:T(8,128)(2,1)}, f32[16384,128]{1,0:T(8,128)}) custom-call(s32[33]{0:T(128)} %copy-done.19, f32[16384,768]{1,0:T(8,128)} %all-gather.3.cloned.1.call-done.xh_ref, f32[1,768]{1,0:T(1,128)} %reshape.269.g_ref, f32[32,8,512]{2,1,0:T(8,128)} %stack.153.aux_ref), custom_call_target="tpu_custom_call" | custom-call | flops 25165824 | bytes 75497472 | tf_op jit(solution)/shard_map/gather_tokens/pallas_call | solution.py:301
  564.6 33.6 %weight_grad.8 = (f32[768,1024]{1,0:T(8,128)}, f32[768,16384]{1,0:T(8,128)}) custom-call(s32[3]{0:T(128)} %get-tuple-element.90.place_ref, s32[1]{0:T(128)} %bitcast.43.nt_ref, bf16[16384,768]{1,0:T(8,128)(2,1)} %get-tuple-element.40.n_hbm, f32[16384,128]{1,0:T(8,128)} %get-tuple-element.41.aux_hbm, bf16[768,16384]{1,0:T(8,128)(2,1)} %w_ref.19), custom_call_target="tpu_custom_call" | custom-call | flops 25769803776 | bytes 31457280 | tf_op jit(solution)/shard_map/weight_grad/pallas_call | solution.py:409
  598.2 1.5 collective-permute-start.3
  599.7 33.5 %weight_grad.9 = (f32[768,1024]{1,0:T(8,128)}, f32[768,16384]{1,0:T(8,128)}) custom-call(s32[3]{0:T(128)} %get-tuple-element.91.place_ref, s32[1]{0:T(128)} %bitcast.43.nt_ref, bf16[16384,768]{1,0:T(8,128)(2,1)} %get-tuple-element.40.n_hbm, f32[16384,128]{1,0:T(8,128)} %get-tuple-element.41.aux_hbm, ...), custom_call_target="tpu_custom_call", output_to_operand_aliasing={{1}: (5, {})} | custom-call | flops 25769803776 | bytes 31457280 | tf_op jit(solution)/shard_map/weight_grad/pallas_call | solution.py:409
  633.3 33.6 %weight_grad.10 = (f32[768,1024]{1,0:T(8,128)}, f32[768,16384]{1,0:T(8,128)}) custom-call(s32[3]{0:T(128)} %pad_add_fusion.3.place_ref, s32[1]{0:T(128)} %bitcast.43.nt_ref, bf16[16384,768]{1,0:T(8,128)(2,1)} %get-tuple-element.40.n_hbm, f32[16384,128]{1,0:T(8,128)} %get-tuple-element.41.aux_hbm, ...), custom_call_target="tpu_custom_call", output_to_operand_aliasing={{1}: (5, {})} | custom-call | flops 25769803776 | bytes 31457280 | tf_op jit(solution)/shard_map/weight_grad/pallas_call | solution.py:409
  667.6 1.2 collective-permute-done.3.rest_1_
  668.8 34.2 %weight_grad.11 = (f32[768,1024]{1,0:T(8,128)}, f32[768,16384]{1,0:T(8,128)}) custom-call(s32[3]{0:T(128)} %pad_add_fusion.9.place_ref, s32[1]{0:T(128)} %bitcast.43.nt_ref, bf16[16384,768]{1,0:T(8,128)(2,1)} %get-tuple-element.40.n_hbm, f32[16384,128]{1,0:T(8,128)} %get-tuple-element.41.aux_hbm, ...), custom_call_target="tpu_custom_call", output_to_operand_aliasing={{1}: (5, {})} | custom-call | flops 25769803776 | bytes 31457280 | tf_op jit(solution)/shard_map/weight_grad/pallas_call | solution.py:409
  703.0 0.8 collective-permute-start.6
  703.9 34.4 %weight_grad.12 = (f32[768,1024]{1,0:T(8,128)}, f32[768,16384]{1,0:T(8,128)}) custom-call(s32[3]{0:T(128)} %pad_add_fusion.8.place_ref, s32[1]{0:T(128)} %bitcast.43.nt_ref, bf16[16384,768]{1,0:T(8,128)(2,1)} %get-tuple-element.40.n_hbm, f32[16384,128]{1,0:T(8,128)} %get-tuple-element.41.aux_hbm, ...), custom_call_target="tpu_custom_call", output_to_operand_aliasing={{1}: (5, {})} | custom-call | flops 25769803776 | bytes 31457280 | tf_op jit(solution)/shard_map/weight_grad/pallas_call | solution.py:409
  738.3 1.5 collective-permute-start.7
  739.8 34.2 %weight_grad.13 = (f32[768,1024]{1,0:T(8,128)}, f32[768,16384]{1,0:T(8,128)}) custom-call(s32[3]{0:T(128)} %pad_add_fusion.7.place_ref, s32[1]{0:T(128)} %bitcast.43.nt_ref, bf16[16384,768]{1,0:T(8,128)(2,1)} %get-tuple-element.40.n_hbm, f32[16384,128]{1,0:T(8,128)} %get-tuple-element.41.aux_hbm, ...), custom_call_target="tpu_custom_call", output_to_operand_aliasing={{1}: (5, {})} | custom-call | flops 25769803776 | bytes 31457280 | tf_op jit(solution)/shard_map/weight_grad/pallas_call | solution.py:409
  774.0 1.3 collective-permute-start.8
  775.3 34.2 %weight_grad.14 = (f32[768,1024]{1,0:T(8,128)}, f32[768,16384]{1,0:T(8,128)}) custom-call(s32[3]{0:T(128)} %pad_add_fusion.6.place_ref, s32[1]{0:T(128)} %bitcast.43.nt_ref, bf16[16384,768]{1,0:T(8,128)(2,1)} %get-tuple-element.40.n_hbm, f32[16384,128]{1,0:T(8,128)} %get-tuple-element.41.aux_hbm, ...), custom_call_target="tpu_custom_call", output_to_operand_aliasing={{1}: (5, {})} | custom-call | flops 25769803776 | bytes 31457280 | tf_op jit(solution)/shard_map/weight_grad/pallas_call | solution.py:409
  810.2 34.3 %weight_grad.15 = (f32[768,1024]{1,0:T(8,128)}, f32[768,16384]{1,0:T(8,128)}) custom-call(s32[3]{0:T(128)} %pad_add_fusion.5.place_ref, s32[1]{0:T(128)} %bitcast.43.nt_ref, bf16[16384,768]{1,0:T(8,128)(2,1)} %get-tuple-element.40.n_hbm, f32[16384,128]{1,0:T(8,128)} %get-tuple-element.41.aux_hbm, ...), custom_call_target="tpu_custom_call", output_to_operand_aliasing={{1}: (5, {})} | custom-call | flops 25769803776 | bytes 31457280 | tf_op jit(solution)/shard_map/weight_grad/pallas_call | solution.py:409
  844.5 0.8 collective-permute-start.10
  846.4 4.0 constant_dynamic-update-slice_fusion.2
  850.4 28.1 %collective-permute-done.9 = f32[768,1024]{1,0:T(8,128)} collective-permute-done((f32[768,1024]{1,0:T(8,128)}, f32[768,1024]{1,0:T(8,128)}, u32[]{:S(2)}, u32[]{:S(2)}) %collective-permute-start.9) | collective-permute-done | bytes 3145760 | tf_op jit(solution)/shard_map/ppermute | solution.py:534
  878.5 4.0 constant_dynamic-update-slice_fusion.1
  882.5 30.6 %collective-permute-done.10 = f32[768,1024]{1,0:T(8,128)} collective-permute-done((f32[768,1024]{1,0:T(8,128)}, f32[768,1024]{1,0:T(8,128)}, u32[]{:S(2)}, u32[]{:S(2)}) %collective-permute-start.10) | collective-permute-done | bytes 3145760 | tf_op jit(solution)/shard_map/ppermute | solution.py:534
  913.1 4.0 constant_dynamic-update-slice_fusion
  (119 shorter events, 12.7 us)
Async XLA Ops:
  8.0 3.6 copy-start
  8.0 9.3 %copy-start.20 = (s32[1,512]{1,0:T(1,128)S(1)}, s32[1,512]{1,0:T(1,128)}, u32[]{:S(2)}) copy-start(s32[1,512]{1,0:T(1,128)} %param.6) | copy-start | bytes 6148
  8.0 52.4 %copy-start.11 = (f32[768]{0:T(1024)S(1)}, f32[768]{0:T(1024)}, u32[]{:S(2)}) copy-start(f32[768]{0:T(1024)} %param.8) | copy-start | bytes 9220
  8.0 309.8 %reduce-scatter.2.cloned.1.call-start = ((), (), s32[]{:S(2)}) async-start(), calls=%async_computation.2 | async-start | bytes 7864320 | tf_op jit(solution)/shard_map/reduce_scatter | solution.py:498
  11.6 46.0 %copy-start.13 = (s32[1,512]{1,0:T(1,128)}, s32[1,512]{1,0:T(1,128)S(1)}, u32[]{:S(2)}) copy-start(s32[1,512]{1,0:T(1,128)S(1)} %compare_select_fusion.4) | copy-start | bytes 6148
  12.3 1.1 copy-start.2
  12.3 45.3 %copy-start.9 = (f32[512]{0:T(512)}, f32[512]{0:T(512)S(1)}, u32[]{:S(2)}) copy-start(f32[512]{0:T(512)S(1)} %add_rsqrt_fusion) | copy-start | bytes 6148
  13.6 50.1 %copy-start.5 = (f32[512,768]{1,0:T(8,128)}, f32[512,768]{1,0:T(8,128)S(1)}, u32[]{:S(2)}) copy-start(f32[512,768]{1,0:T(8,128)S(1)} %broadcast_multiply_fusion.xa) | copy-start | bytes 4718596
  13.6 43.9 %collective-permute-start.1 = (f32[512,768]{1,0:T(8,128)S(1)}, f32[512,768]{1,0:T(8,128)S(1)}, u32[]{:S(2)}, u32[]{:S(2)}) collective-permute-start(f32[512,768]{1,0:T(8,128)S(1)} %broadcast_multiply_fusion.xa), channel_id=1, source_target_pairs={{0,2},{1,3},{2,0},{3,1},{4,6},{5,7},{6,4},{7,5},{8,10},{9,11},{10,... | collective-permute-start | bytes 4718600 | tf_op jit(solution)/shard_map/ppermute | solution.py:454
  16.7 47.0 %collective-permute-start = (f32[512,768]{1,0:T(8,128)S(1)}, f32[512,768]{1,0:T(8,128)}, u32[]{:S(2)}, u32[]{:S(2)}) collective-permute-start(f32[512,768]{1,0:T(8,128)S(1)} %broadcast_multiply_fusion.xa), channel_id=1, source_target_pairs={{0,1},{1,0},{2,3},{3,2},{4,5},{5,4},{6,7},{7,6},{8,9},{9,8},{10,11... | collective-permute-start | bytes 4718600 | tf_op jit(solution)/shard_map/ppermute | solution.py:455
  57.5 2.0 copy-start.17
  57.5 6.2 copy-start.25
  57.5 6.2 collective-permute-start.2
  57.8 1.7 copy-start.8
  58.0 1.5 copy-start.19
  58.8 40.6 %copy-start.23 = (s32[4]{0:T(128)}, s32[4]{0:T(128)S(1)}, u32[]{:S(2)}) copy-start(s32[4]{0:T(128)S(1)} %get-tuple-element.66.span_ref) | copy-start | bytes 52
  58.9 40.6 %copy-start.24 = (s32[4]{0:T(128)}, s32[4]{0:T(128)S(1)}, u32[]{:S(2)}) copy-start(s32[4]{0:T(128)S(1)} %get-tuple-element.94.offs_ref) | copy-start | bytes 52
  60.5 39.0 %copy-start.6 = (f32[32,4,128]{2,1,0:T(4,128)}, f32[32,4,128]{2,1,0:T(4,128)S(1)}, u32[]{:S(2)}) copy-start(f32[32,4,128]{2,1,0:T(4,128)S(1)} %slice.97) | copy-start | bytes 196612
  63.0 42.4 %copy-start.21 = (s32[4]{0:T(128)}, s32[4]{0:T(128)S(1)}, u32[]{:S(2)}) copy-start(s32[4]{0:T(128)S(1)} %dynamic-slice_reduce_fusion.kept_ref) | copy-start | bytes 52
  146.1 0.7 copy-start.22
  146.1 7.5 copy-start.18
  146.1 131.0 %copy-start.16 = (f32[8,128]{1,0:T(8,128)S(1)}, f32[8,128]{1,0:T(8,128)}, u32[]{:S(2)}) copy-start(f32[8,128]{1,0:T(8,128)} %get-tuple-element.37) | copy-start | bytes 12292
  146.1 132.4 %copy-start.7 = (f32[32,4,128]{2,1,0:T(4,128)S(1)}, f32[32,4,128]{2,1,0:T(4,128)}, u32[]{:S(2)}) copy-start(f32[32,4,128]{2,1,0:T(4,128)} %copy-done.6) | copy-start | bytes 196612
  146.2 171.7 %copy-start.3 = (f32[512,768]{1,0:T(8,128)S(1)}, f32[512,768]{1,0:T(8,128)}, u32[]{:S(2)}) copy-start(f32[512,768]{1,0:T(8,128)} %copy-done.2) | copy-start | bytes 4718596
  146.2 171.7 %copy-start.10 = (f32[512]{0:T(512)S(1)}, f32[512]{0:T(512)}, u32[]{:S(2)}) copy-start(f32[512]{0:T(512)} %copy-done.9) | copy-start | bytes 6148
  146.2 171.7 %copy-start.12 = (f32[768]{0:T(1024)S(1)}, f32[768]{0:T(1024)}, u32[]{:S(2)}) copy-start(f32[768]{0:T(1024)} %param.8) | copy-start | bytes 9220
  146.2 391.5 %all-gather.3.cloned.1.call-start = ((), (), s32[]{:S(2)}) async-start(), calls=%async_computation.1 | async-start | bytes 51904512 | tf_op jit(solution)/shard_map/all_gather | solution.py:456
  146.8 187.1 %copy-start.14 = (s32[1,512]{1,0:T(1,128)S(1)}, s32[1,512]{1,0:T(1,128)}, u32[]{:S(2)}) copy-start(s32[1,512]{1,0:T(1,128)} %copy-done.13) | copy-start | bytes 6148
  317.9 16.1 %copy-start.4 = (f32[512,768]{1,0:T(8,128)S(1)}, f32[512,768]{1,0:T(8,128)}, u32[]{:S(2)}) copy-start(f32[512,768]{1,0:T(8,128)} %reduce-scatter.2.cloned.1.call-done) | copy-start | bytes 4718596
  598.2 70.6 %collective-permute-start.3 = (f32[768,1024]{1,0:T(8,128)}, f32[768,1024]{1,0:T(8,128)}, u32[]{:S(2)}, u32[]{:S(2)}) collective-permute-start(f32[768,1024]{1,0:T(8,128)} %get-tuple-element.45), channel_id=1, source_target_pairs={{0,4},{4,0},{8,12},{12,8},{16,20},{20,16},{24,28},{28,24},{1,5},{5... | collective-permute-start | bytes 9437192 | tf_op jit(solution)/shard_map/ppermute | solution.py:534
  633.3 70.6 %collective-permute-start.4 = (f32[768,1024]{1,0:T(8,128)}, f32[768,1024]{1,0:T(8,128)}, u32[]{:S(2)}, u32[]{:S(2)}) collective-permute-start(f32[768,1024]{1,0:T(8,128)} %get-tuple-element.47), channel_id=1, source_target_pairs={{0,8},{4,12},{8,0},{12,4},{16,24},{20,28},{24,16},{28,20},{1,9},{5... | collective-permute-start | bytes 9437192 | tf_op jit(solution)/shard_map/ppermute | solution.py:534
  666.9 72.9 %collective-permute-start.5 = (f32[768,1024]{1,0:T(8,128)}, f32[768,1024]{1,0:T(8,128)}, u32[]{:S(2)}, u32[]{:S(2)}) collective-permute-start(f32[768,1024]{1,0:T(8,128)} %get-tuple-element.49), channel_id=1, source_target_pairs={{0,4},{4,0},{8,12},{12,8},{16,20},{20,16},{24,28},{28,24},{1,5},{5... | collective-permute-start | bytes 9437192 | tf_op jit(solution)/shard_map/ppermute | solution.py:534
  703.0 72.3 %collective-permute-start.6 = (f32[768,1024]{1,0:T(8,128)}, f32[768,1024]{1,0:T(8,128)}, u32[]{:S(2)}, u32[]{:S(2)}) collective-permute-start(f32[768,1024]{1,0:T(8,128)} %get-tuple-element.51), channel_id=1, source_target_pairs={{0,8},{4,12},{8,0},{12,4},{16,24},{20,28},{24,16},{28,20},{1,9},{5... | collective-permute-start | bytes 9437192 | tf_op jit(solution)/shard_map/ppermute | solution.py:534
  738.3 71.9 %collective-permute-start.7 = (f32[768,1024]{1,0:T(8,128)}, f32[768,1024]{1,0:T(8,128)}, u32[]{:S(2)}, u32[]{:S(2)}) collective-permute-start(f32[768,1024]{1,0:T(8,128)} %get-tuple-element.53), channel_id=1, source_target_pairs={{0,4},{4,0},{8,12},{12,8},{16,20},{20,16},{24,28},{28,24},{1,5},{5... | collective-permute-start | bytes 9437192 | tf_op jit(solution)/shard_map/ppermute | solution.py:534
  774.0 72.4 %collective-permute-start.8 = (f32[768,1024]{1,0:T(8,128)}, f32[768,1024]{1,0:T(8,128)}, u32[]{:S(2)}, u32[]{:S(2)}) collective-permute-start(f32[768,1024]{1,0:T(8,128)} %get-tuple-element.55), channel_id=1, source_target_pairs={{0,8},{4,12},{8,0},{12,4},{16,24},{20,28},{24,16},{28,20},{1,9},{5... | collective-permute-start | bytes 9437192 | tf_op jit(solution)/shard_map/ppermute | solution.py:534
  809.5 68.9 %collective-permute-start.9 = (f32[768,1024]{1,0:T(8,128)}, f32[768,1024]{1,0:T(8,128)}, u32[]{:S(2)}, u32[]{:S(2)}) collective-permute-start(f32[768,1024]{1,0:T(8,128)} %get-tuple-element.56), channel_id=1, source_target_pairs={{0,4},{4,0},{8,12},{12,8},{16,20},{20,16},{24,28},{28,24},{1,5},{5... | collective-permute-start | bytes 9437192 | tf_op jit(solution)/shard_map/ppermute | solution.py:534
  810.2 35.1 %copy-start.15 = (f32[8,128]{1,0:T(8,128)S(1)}, f32[8,128]{1,0:T(8,128)}, u32[]{:S(2)}) copy-start(f32[8,128]{1,0:T(8,128)} %reduce_sum.141) | copy-start | bytes 12292
  844.5 68.6 %collective-permute-start.10 = (f32[768,1024]{1,0:T(8,128)}, f32[768,1024]{1,0:T(8,128)}, u32[]{:S(2)}, u32[]{:S(2)}) collective-permute-start(f32[768,1024]{1,0:T(8,128)} %get-tuple-element.57), channel_id=1, source_target_pairs={{0,8},{4,12},{8,0},{12,4},{16,24},{20,28},{24,16},{28,20},{1,9},{5... | collective-permute-start | bytes 9437192 | tf_op jit(solution)/shard_map/ppermute | solution.py:534
  878.5 38.6 %copy-start.1 = (bf16[1,512,768]{2,1,0:T(8,128)(2,1)S(1)}, bf16[1,512,768]{2,1,0:T(8,128)(2,1)}, u32[]{:S(2)}) copy-start(bf16[1,512,768]{2,1,0:T(8,128)(2,1)} %param.5) | copy-start | bytes 2359300
Sparse Core Ops, SparseCore 0:
  146.3 171.5 reduce-scatter.1
Sparse Core Ops, SparseCore 1:
  149.6 388.1 all-gather.2

commit v3 on v2

v3 whole, which is shorter than its diff:
```python
import functools

import jax
import jax.numpy as jnp
from jax import lax
from jax.experimental import pallas as pl
from jax.experimental.pallas import tpu as pltpu
from jax.sharding import PartitionSpec as P


EPS = 1e-5
BLK = 512
DIM = 768
ALIGN = 16
FWD_COLS = 2048
FWD_GROUP = 512
DN_COLS = 2048
DW_TOK = 1024
DW_GROUP = 1024
SUB = 256
Y_WIDTHS = (1024, 1024, 1024, 512, 512)
Z_WIDTHS = (1024, 1024, 1024, 512, 256, 256)
LAG = 4
DROPPED = 1e30
LOG2E = 1.4426950408889634


f32, bf16, i32 = jnp.float32, jnp.bfloat16, jnp.int32


def tiny_gather_kernel(dp_count, vp_count, x_ref, out_ref, send_sems, recv_sems):
    count = dp_count * vp_count
    me = lax.axis_index("dp") * vp_count + lax.axis_index("vp")
    barrier = pltpu.get_barrier_semaphore()

    def peer(k):
        other = lax.rem(me + k, count)
        return (other // vp_count, lax.rem(other, vp_count))

    for k in range(1, count):
        pl.semaphore_signal(barrier, inc=1, device_id=peer(k), device_id_type=pl.DeviceIdType.MESH)
    pl.semaphore_wait(barrier, count - 1)
    copies = [
        pltpu.make_async_remote_copy(
            src_ref=x_ref,
            dst_ref=out_ref.at[me],
            send_sem=send_sems.at[k - 1],
            recv_sem=recv_sems.at[k - 1],
            device_id=peer(k),
            device_id_type=pl.DeviceIdType.MESH,
        )
        for k in range(1, count)
    ]
    for copy in copies:
        copy.start()
    out_ref[me] = x_ref[...]
    for copy in copies:
        copy.wait()


def tiny_gather(x, mesh_shape, collective_id):
    dp_count, vp_count = mesh_shape
    count = dp_count * vp_count
    return pl.pallas_call(
        functools.partial(tiny_gather_kernel, dp_count, vp_count),
        out_shape=jax.ShapeDtypeStruct((count, 8, 128), f32),
        in_specs=[pl.BlockSpec(memory_space=pltpu.VMEM)],
        out_specs=pl.BlockSpec(memory_space=pltpu.VMEM),
        scratch_shapes=[pltpu.SemaphoreType.DMA((count - 1,)), pltpu.SemaphoreType.DMA((count - 1,))],
        compiler_params=pltpu.CompilerParams(collective_id=collective_id, has_side_effects=True),
        name="tiny_gather",
    )(x)


def place_masked(dst, off, span, new):
    rows = pl.ds(pl.multiple_of(off, ALIGN), BLK)
    live = lax.broadcasted_iota(i32, (BLK, 1), 0) < span
    dst[rows, :] = jnp.where(live, new, dst[rows, :].astype(f32)).astype(dst.dtype)


def aux_columns(aux):
    pad = jnp.zeros((120, aux.shape[1]), f32)
    return jnp.concatenate([aux, pad], axis=0).T


def fwd_kernel(xa, xb, g_ref, w_ref, n_ref, st_ref, m_ref, s_ref, za_ref, zb_ref):
    j = pl.program_id(0)
    groups = FWD_COLS // FWD_GROUP
    bufs = (za_ref, zb_ref)

    @pl.when(j == 0)
    def _():
        m_ref[...] = jnp.full_like(m_ref, -DROPPED)
        s_ref[...] = jnp.zeros_like(s_ref)
        zb_ref[...] = jnp.full_like(zb_ref, -DROPPED)
        for k, x_ref in enumerate((xa, xb)):
            n_ref[pl.ds(k * BLK, BLK), :] = (x_ref[...] * g_ref[...]).astype(bf16)

    def absorb(row, z_ref):
        for r in range(0, BLK, 8):
            rows = pl.ds(pl.multiple_of(row + r, 8), 8)
            parts = [z_ref[r : r + 8, k * 128 : (k + 1) * 128] for k in range(FWD_GROUP // 128)]
            m_old = m_ref[rows, :]
            m_new = jnp.maximum(functools.reduce(jnp.maximum, parts), m_old)
            total = functools.reduce(jnp.add, [jnp.exp(part - m_new) for part in parts])
            s_ref[rows, :] = s_ref[rows, :] * jnp.exp(m_old - m_new) + total
            m_ref[rows, :] = m_new

    def tile(i, carry):
        row = pl.multiple_of(i * BLK, BLK)
        n = n_ref[pl.ds(row, BLK), :]
        for c in range(groups):
            cols = pl.ds(c * FWD_GROUP, FWD_GROUP)
            bufs[c % 2][...] = jnp.dot(n, w_ref[:, cols], preferred_element_type=f32)
            absorb(row if c else pl.multiple_of((1 - i) * BLK, BLK), bufs[(c + 1) % 2])
        return carry

    lax.fori_loop(0, 2, tile, 0)

    @pl.when(j == pl.num_programs(0) - 1)
    def _():
        absorb(BLK, zb_ref)
        for k in range(2):
            rows = pl.ds(k * BLK, BLK)
            m_lane = m_ref[rows, :]
            m = jnp.max(m_lane, axis=1, keepdims=True)
            s = jnp.sum(s_ref[rows, :] * jnp.exp(m_lane - m), axis=1, keepdims=True)
            st_ref[k, 0:1, :] = jnp.broadcast_to(m, (BLK, 128)).T[0:1, :]
            st_ref[k, 1:2, :] = jnp.broadcast_to(s, (BLK, 128)).T[0:1, :]


def forward_stats(xa, xb, g, w):
    vocab = w.shape[1]
    return pl.pallas_call(
        fwd_kernel,
        grid=(vocab // FWD_COLS,),
        in_specs=[pl.BlockSpec((BLK, DIM), lambda j: (0, 0))] * 2
        + [
            pl.BlockSpec((1, DIM), lambda j: (0, 0)),
            pl.BlockSpec((DIM, FWD_COLS), lambda j: (0, j)),
        ],
        out_specs=[
            pl.BlockSpec((2 * BLK, DIM), lambda j: (0, 0)),
            pl.BlockSpec((2, 2, BLK), lambda j: (0, 0, 0)),
        ],
        scratch_shapes=[
            pltpu.VMEM((2 * BLK, 128), f32),
            pltpu.VMEM((2 * BLK, 128), f32),
            pltpu.VMEM((BLK, FWD_GROUP), f32),
            pltpu.VMEM((BLK, FWD_GROUP), f32),
        ],
        out_shape=[
            jax.ShapeDtypeStruct((2 * BLK, DIM), bf16),
            jax.ShapeDtypeStruct((2, 2, BLK), f32),
        ],
        compiler_params=pltpu.CompilerParams(dimension_semantics=("arbitrary",)),
        cost_estimate=pl.CostEstimate(
            flops=2 * 2 * BLK * DIM * vocab, bytes_accessed=2 * DIM * vocab + 5 * BLK * DIM * 4, transcendentals=2 * BLK * vocab
        ),
        name="fwd_stats",
    )(xa, xb, g, w)


def grad_logits(z, aux, col0):
    target = aux[:, 2:3].astype(i32) - col0
    hot = lax.broadcasted_iota(i32, z.shape, 1) == target
    p = jnp.exp2(z * LOG2E - aux[:, 0:1])
    return jnp.where(hot, p - aux[:, 1:2], p).astype(bf16), hot


def dn_kernel(
    offs_ref, span_ref, kept_ref, mine_ref, nt_ref, col_ref, na_ref, nb_ref, aux_ref, w_ref, dn_ref, tl_ref, acc_ref, auxc_ref, n_ref, dz_ref
):
    j = pl.program_id(0)

    @pl.when(j == 0)
    def _():
        acc_ref[...] = jnp.zeros_like(acc_ref)
        auxc_ref[...] = jnp.zeros_like(auxc_ref)
        tl_ref[...] = jnp.zeros_like(tl_ref)
        n_ref[...] = jnp.zeros_like(n_ref)
        for b in range(4):
            place_masked(auxc_ref, offs_ref[b], span_ref[b], aux_columns(aux_ref[b]))
            src = (na_ref, na_ref, nb_ref, nb_ref)[b][pl.ds(b % 2 * BLK, BLK), :].astype(f32)
            place_masked(n_ref, offs_ref[mine_ref[b]], span_ref[mine_ref[b]], src)

    col0 = col_ref[0] + j * DN_COLS

    def tile(i, carry):
        rows = pl.ds(pl.multiple_of(i * BLK, BLK), BLK)
        aux = auxc_ref[rows, :]
        n = n_ref[rows, :]
        found = jnp.zeros((BLK, 128), f32)
        for c in range(DN_COLS // 512):
            z = jnp.dot(n, w_ref[:, c * 512 : (c + 1) * 512], preferred_element_type=f32)
            dz, hot = grad_logits(z, aux, col0 + c * 512)
            dz_ref[:, c * 512 : (c + 1) * 512] = dz
            picked = jnp.where(hot, z, 0.0)
            for k in range(4):
                found += picked[:, k * 128 : (k + 1) * 128]
        tl_ref[...] += jnp.sum((found * aux[:, 1:2]).reshape(BLK // 8, 8, 128), axis=0)
        acc_ref[rows, :] += lax.dot_general(dz_ref[...], w_ref[...], (((1,), (1,)), ((), ())), preferred_element_type=f32)
        return carry

    lax.fori_loop(0, nt_ref[0], tile, 0)

    @pl.when(j == pl.num_programs(0) - 1)
    def _():
        for b in range(4):
            got = acc_ref[pl.ds(pl.multiple_of(offs_ref[b], ALIGN), BLK), :]
            live = lax.broadcasted_iota(i32, (BLK, 1), 0) < kept_ref[b]
            dn_ref[pl.ds(b * BLK, BLK), :] = jnp.where(live, got, 0.0)


def backward_dn(offs, span, kept, mine, ntiles, col0, n_near, n_far, aux_row, w):
    vocab = w.shape[1]
    return pl.pallas_call(
        dn_kernel,
        grid_spec=pltpu.PrefetchScalarGridSpec(
            num_scalar_prefetch=6,
            grid=(vocab // DN_COLS,),
            in_specs=[
                pl.BlockSpec((2 * BLK, DIM), lambda j, *_: (0, 0)),
                pl.BlockSpec((2 * BLK, DIM), lambda j, *_: (0, 0)),
                pl.BlockSpec((4, 8, BLK), lambda j, *_: (0, 0, 0)),
                pl.BlockSpec((DIM, DN_COLS), lambda j, *_: (0, j)),
            ],
            out_specs=[
                pl.BlockSpec((4 * BLK, DIM), lambda j, *_: (0, 0)),
                pl.BlockSpec((8, 128), lambda j, *_: (0, 0)),
            ],
            scratch_shapes=[
                pltpu.VMEM((4 * BLK, DIM), f32),
                pltpu.VMEM((4 * BLK, 128), f32),
                pltpu.VMEM((4 * BLK, DIM), bf16),
                pltpu.VMEM((BLK, DN_COLS), bf16),
            ],
        ),
        out_shape=[
            jax.ShapeDtypeStruct((4 * BLK, DIM), f32),
            jax.ShapeDtypeStruct((8, 128), f32),
        ],
        compiler_params=pltpu.CompilerParams(dimension_semantics=("arbitrary",)),
        cost_estimate=pl.CostEstimate(
            flops=4 * 4 * BLK * DIM * vocab, bytes_accessed=2 * DIM * vocab + 6 * BLK * DIM * 4, transcendentals=4 * BLK * vocab
        ),
        name="backward_dn",
    )(offs, span, kept, mine, ntiles, col0, n_near, n_far, aux_row, w)


def dw_tile(load, aux, w_ref, dz_ref, acc_ref, col0):
    width = acc_ref.shape[1]
    group = min(width, DW_GROUP)
    sub = SUB if width > 256 else 2 * SUB
    for c in range(width // group):
        cols = pl.ds(c * group, group)
        for u in range(DW_TOK // sub):
            rows = pl.ds(u * sub, sub)
            z = jnp.dot(load(u * sub, sub), w_ref[:, cols], preferred_element_type=f32)
            dz_ref[rows, cols], _ = grad_logits(z, aux(u * sub, sub), col0 + c * group)
        acc_ref[:, cols] += lax.dot_general(
            load(0, DW_TOK), dz_ref[:, cols], (((0,), (0,)), ((), ())), preferred_element_type=f32
        )


def first_kernel(final, offs_ref, place_ref, xh_ref, aux_ref, g_ref, w_ref, *rest):
    n_hbm, aux_hbm, acc_ref, n_img, aux_img, dz_ref, sems = rest[-7:]
    step = pl.program_id(0)
    last = pl.num_programs(0) - 1
    half = BLK // 2
    base = offs_ref[0] // DW_TOK
    end = offs_ref[offs_ref.shape[0] - 1]

    def images(t):
        rows = pl.ds(pl.multiple_of((t - base) * DW_TOK, DW_TOK), DW_TOK)
        return n_img.at[rows, :], aux_img.at[rows, :]

    def places(t):
        rows = pl.ds(pl.multiple_of(t * DW_TOK, DW_TOK), DW_TOK)
        return n_hbm.at[rows, :], aux_hbm.at[rows, :]

    def copies(t):
        return [pltpu.make_async_copy(a, b, sems.at[k]) for k, (a, b) in enumerate(zip(images(t), places(t)))]

    @pl.when(step == 0)
    def _():
        if final:
            acc_ref[...] = rest[2][...]
            loads = [pltpu.make_async_copy(b, a, sems.at[k]) for k, (a, b) in enumerate(zip(images(base), places(base)))]
            for copy in loads:
                copy.start()
            for copy in loads:
                copy.wait()
        else:
            acc_ref[...] = jnp.zeros_like(acc_ref)

    for k in range(4):
        off = pl.multiple_of(offs_ref[step * 4 + k] - base * DW_TOK, ALIGN)
        n_img[pl.ds(off, half), :] = (xh_ref[k] * g_ref[...]).astype(bf16)
        aux_img[pl.ds(off, half), :] = aux_columns(aux_ref[k])

    @pl.when(step == last)
    def _():
        rows = pl.ds(pl.multiple_of(end - base * DW_TOK, ALIGN), DW_TOK)
        n_img[rows, :] = jnp.zeros((DW_TOK, DIM), bf16)
        aux_img[rows, :] = jnp.zeros((DW_TOK, 128), f32)

    full = offs_ref[step * 4 + 4] // DW_TOK
    stop = jnp.where(step == last, (end + DW_TOK - 1) // DW_TOK, full) if final else full

    def tile(t, carry):
        for copy in copies(t):
            copy.start()
        row = (t - base) * DW_TOK

        def rows(start, size):
            return pl.ds(pl.multiple_of(row, DW_TOK) + start, size)

        dw_tile(
            lambda *r: n_img[rows(*r), :], lambda *r: aux_img[rows(*r), :], w_ref, dz_ref, acc_ref, place_ref[1]
        )
        return carry

    lax.fori_loop(offs_ref[step * 4] // DW_TOK, stop, tile, 0)

    @pl.when(step == last)
    def _():
        if not final:
            for copy in copies(full):
                copy.start()

        def drain(t, carry):
            for copy in copies(t):
                copy.wait()
            return carry

        lax.fori_loop(base, stop if final else full + 1, drain, 0)


def first_columns(half, offs, place, xh_half, aux_all, g, w, before):
    blocks = aux_all.shape[0]
    tokens = blocks * BLK
    image = tokens // 2 + 2 * DW_TOK
    width = Y_WIDTHS[0]
    anywhere = pl.BlockSpec(memory_space=pl.ANY)
    whole_chunk = pl.BlockSpec((DIM, width), lambda b, *_: (0, 0))
    final = before is not None
    return pl.pallas_call(
        functools.partial(first_kernel, final),
        grid_spec=pltpu.PrefetchScalarGridSpec(
            num_scalar_prefetch=2,
            grid=(blocks // 4,),
            in_specs=[
                pl.BlockSpec((4, BLK // 2, DIM), lambda b, *_: (b, 0, 0)),
                pl.BlockSpec((4, 8, BLK // 2), lambda b, *_: (b, 0, half)),
                pl.BlockSpec((1, DIM), lambda b, *_: (0, 0)),
                pl.BlockSpec((DIM, width), lambda b, offs, place: (0, place[0])),
            ]
            + ([anywhere, anywhere, whole_chunk] if final else []),
            out_specs=[anywhere, anywhere, whole_chunk],
            scratch_shapes=[
                pltpu.VMEM((image, DIM), bf16),
                pltpu.VMEM((image, 128), f32),
                pltpu.VMEM((DW_TOK, width), bf16),
                pltpu.SemaphoreType.DMA((2,)),
            ],
        ),
        out_shape=[
            jax.ShapeDtypeStruct((tokens, DIM), bf16),
            jax.ShapeDtypeStruct((tokens, 128), f32),
            jax.ShapeDtypeStruct((DIM, width), f32),
        ],
        input_output_aliases={6: 0, 7: 1} if final else {},
        compiler_params=pltpu.CompilerParams(dimension_semantics=("arbitrary",), vmem_limit_bytes=60 << 20),
        cost_estimate=pl.CostEstimate(
            flops=tokens * DIM * width, bytes_accessed=4 * tokens * DIM, transcendentals=tokens * width // 4
        ),
        name="first_columns",
    )(offs, place, xh_half.reshape(blocks, BLK // 2, DIM), aux_all, g, w, *(before or ()))


def dw_kernel(merges, place_ref, nt_ref, n_hbm, aux_hbm, w_ref, *rest):
    inputs, rest = rest[: -(6 + merges + 1)], rest[-(6 + merges + 1) :]
    out_ref, all_hbm, nbuf, abuf, dz_ref, sems = rest[:6]
    mbufs, out_sems = rest[6:-1], rest[-1]
    steps = nt_ref[0]

    def fetch(i, slot):
        rows = pl.ds(pl.multiple_of(i * DW_TOK, DW_TOK), DW_TOK)
        return (
            pltpu.make_async_copy(n_hbm.at[rows, :], nbuf.at[slot], sems.at[slot, 0]),
            pltpu.make_async_copy(aux_hbm.at[rows, :], abuf.at[slot], sems.at[slot, 1]),
        )

    def put(ref, col, sem):
        return pltpu.make_async_copy(ref, all_hbm.at[:, pl.ds(pl.multiple_of(col, 128), ref.shape[1])], sem)

    for copy in fetch(0, 0):
        copy.start()
    moves_in = [pltpu.make_async_copy(src, mbuf, out_sems.at[k, 0]) for k, (src, mbuf) in enumerate(zip(inputs[-merges:], mbufs))]
    moves_out = [put(mbuf, place_ref[3 + k], out_sems.at[k, 1]) for k, mbuf in enumerate(mbufs)]
    for copy in moves_in:
        copy.start()
    out_ref[...] = jnp.zeros_like(out_ref)

    def tile(i, carry):
        slot = lax.rem(i, 2)

        @pl.when(i + 1 < steps)
        def _():
            for copy in fetch(i + 1, 1 - slot):
                copy.start()

        for copy in fetch(i, slot):
            copy.wait()
        dw_tile(
            lambda start, size: nbuf[slot, pl.ds(start, size), :],
            lambda start, size: abuf[slot, pl.ds(start, size), :],
            w_ref,
            dz_ref,
            out_ref,
            place_ref[1],
        )
        return carry

    lax.fori_loop(0, steps, tile, 0)
    own = put(out_ref, place_ref[2], out_sems.at[merges, 0])
    own.start()
    for copy in moves_in:
        copy.wait()
    for copy in moves_out:
        copy.start()
    for copy in (own, *moves_out):
        copy.wait()


def weight_grad(width, col, vocab_col, ntiles, n_all, aux_all, w, whole, merges):
    tokens, vocab = n_all.shape[0], w.shape[1]
    anywhere = pl.BlockSpec(memory_space=pl.ANY)
    chunks = [chunk for chunk, _ in merges]
    held = ([] if whole is None else [whole]) + chunks
    place = jnp.stack([col // width, vocab_col, col] + [c for _, c in merges]).astype(i32)
    return pl.pallas_call(
        functools.partial(dw_kernel, len(merges)),
        grid_spec=pltpu.PrefetchScalarGridSpec(
            num_scalar_prefetch=2,
            grid=(1,),
            in_specs=[anywhere, anywhere, pl.BlockSpec((DIM, width), lambda s, place, nt: (0, place[0]))]
            + [anywhere] * len(held),
            out_specs=[pl.BlockSpec((DIM, width), lambda s, *_: (0, 0)), anywhere],
            scratch_shapes=[
                pltpu.VMEM((2, DW_TOK, DIM), bf16),
                pltpu.VMEM((2, DW_TOK, 128), f32),
                pltpu.VMEM((DW_TOK, width), bf16),
                pltpu.SemaphoreType.DMA((2, 2)),
                *(pltpu.VMEM(chunk.shape, f32) for chunk in chunks),
                pltpu.SemaphoreType.DMA((len(merges) + 1, 2)),
            ],
        ),
        out_shape=[
            jax.ShapeDtypeStruct((DIM, width), f32),
            jax.ShapeDtypeStruct((DIM, vocab), f32),
        ],
        input_output_aliases={} if whole is None else {5: 1},
        compiler_params=pltpu.CompilerParams(dimension_semantics=("arbitrary",)),
        cost_estimate=pl.CostEstimate(
            flops=2 * tokens * DIM * width, bytes_accessed=2 * tokens * DIM + 8 * DIM * width, transcendentals=tokens * width // 2
        ),
        name="weight_grad",
    )(place, ntiles, n_all, aux_all, w, *held)


def solution(mesh):
    dp_count, vp_count = mesh.shape["dp"], mesh.shape["vp"]
    everyone = (dp_count, vp_count)

    def local_step(hidden, targets, loss_mask, norm_scale, w_head):
        vocab = w_head.shape[1]
        dp, vp = lax.axis_index("dp"), lax.axis_index("vp")
        g = norm_scale.reshape(1, DIM)

        mask = loss_mask[0]
        idx = lax.iota(i32, BLK)
        before = jnp.sum(jnp.where(idx[None, :] < idx[:, None], mask[None, :], 0), axis=1)
        kept = jnp.sum(mask)
        pos = jnp.where(mask == 1, before, kept + idx - before)
        perm = pos[None, :] == idx[:, None]
        x_sorted = jnp.dot(perm.astype(bf16), hidden[0], preferred_element_type=f32)
        t_sorted = jnp.sum(jnp.where(perm, targets[0][None, :], 0), axis=1)
        inv_rms = lax.rsqrt(jnp.mean(x_sorted * x_sorted, axis=-1, keepdims=True) + EPS)
        x_hat = x_sorted * inv_rms

        core_pairs = [(v, v ^ 1) for v in range(vp_count)]
        x_pairs = [(v, v ^ 2) for v in range(vp_count)]
        from_core = lax.ppermute(x_hat, "vp", core_pairs)
        from_x = lax.ppermute(x_hat, "vp", x_pairs)
        xh_a = lax.all_gather(x_hat[: BLK // 2], ("dp", "vp"), axis=0, tiled=True)
        xh_b = lax.all_gather(x_hat[BLK // 2 :], ("dp", "vp"), axis=0, tiled=True)
        n_near, st_near = forward_stats(x_hat, from_core, g, w_head)
        from_x_core = lax.ppermute(from_x, "vp", core_pairs)
        n_far, st_far = forward_stats(from_x, from_x_core, g, w_head)

        info = jnp.stack([t_sorted.astype(f32), jnp.full((BLK,), kept.astype(f32))])[None]
        near = lax.all_gather(jnp.concatenate([st_near, st_far, info]), "vp", axis=0)
        stats = jnp.stack([jnp.stack([near[v, b ^ v] for b in range(vp_count)]) for v in range(vp_count)])
        row_max = jnp.max(stats[:, :, 0], axis=0)
        row_sum = jnp.sum(stats[:, :, 1] * jnp.exp(stats[:, :, 0] - row_max), axis=0)
        lse_row = row_max + jnp.log(row_sum)
        info_row = near[:, vp_count]
        lse_row = jnp.where(idx[None, :].astype(f32) < info_row[:, 1], lse_row, DROPPED)
        info_all = lax.all_gather(jnp.concatenate([lse_row[:, None], info_row], axis=1), "dp", axis=0, tiled=True)
        lse_all, t_all, kept_all = info_all[:, 0], info_all[:, 1], info_all[:, 2, 0].astype(i32)

        weight = 1.0 / jnp.sum(kept_all).astype(f32)
        live = idx[None, :] < kept_all[:, None]
        w_all = jnp.where(live, weight, 0.0)
        lse_all = jnp.where(live, lse_all * LOG2E - jnp.log2(weight), DROPPED)
        none = jnp.zeros_like(w_all)
        aux_all = jnp.stack([lse_all, w_all, t_all] + [none] * 5, axis=1)

        span = (kept_all + ALIGN - 1) // ALIGN * ALIGN
        span_a = jnp.minimum(span, BLK // 2)
        ends = jnp.cumsum(jnp.concatenate([span_a, span - span_a]))
        offs = jnp.concatenate([jnp.zeros((1,), i32), ends])
        count = dp_count * vp_count
        nt_all = ((ends[-1:] + DW_TOK - 1) // DW_TOK).astype(i32)

        first = dp * vp_count
        kept_row = lax.dynamic_slice(kept_all, (first,), (vp_count,))
        span_row = lax.dynamic_slice(span, (first,), (vp_count,))
        aux_row = lax.dynamic_slice(aux_all, (first, 0, 0), (vp_count, 8, BLK))
        offs_row = jnp.cumsum(span_row) - span_row
        nt_row = ((jnp.sum(span_row) + BLK - 1) // BLK).reshape(1)
        mine = jnp.bitwise_xor(jnp.arange(vp_count, dtype=i32), vp)
        dn_part, t_part = backward_dn(
            offs_row, span_row, kept_row, mine, nt_row, (vp * vocab).reshape(1), n_near, n_far, aux_row, w_head
        )
        d_normed = lax.psum_scatter(dn_part, "vp", scatter_dimension=0, tiled=True)

        d_scale = jnp.sum(d_normed * x_hat, axis=0)
        e = d_normed * norm_scale
        d_x = inv_rms * (e - x_hat * jnp.mean(e * x_hat, axis=-1, keepdims=True))
        back = perm.astype(bf16).T
        d_x = jnp.dot(back, d_x.astype(bf16), preferred_element_type=f32).astype(bf16)
        lse_own = lax.dynamic_slice(lse_row, (vp, 0), (1, BLK))[0]
        loss_part = weight * jnp.sum(jnp.where(idx < kept, lse_own, 0.0)) - jnp.sum(t_part)
        parts = jnp.concatenate([d_scale.reshape(6, 128), jnp.full((2, 128), loss_part, f32)])

        half, quarter = vocab // 2, vocab // 4
        y_pairs = [(d, d ^ 1) for d in range(dp_count)]
        z_pairs = [(d, d ^ 2) for d in range(dp_count)]

        def jobs_of(widths, base, where, pairs):
            starts = [sum(widths[:c]) for c in range(len(widths))]
            return [(n, base + where * quarter + c, base + (1 - where) * quarter + c, pairs) for n, c in zip(widths, starts)]

        y_jobs = jobs_of(Y_WIDTHS, 0, dp % 2, y_pairs)
        z_jobs = jobs_of(Z_WIDTHS, half, (dp // 2) % 2, z_pairs)
        jobs = [job for pair in zip(y_jobs, z_jobs) for job in pair] + z_jobs[len(y_jobs) :]

        width, col, other, pairs = jobs[0]
        place = jnp.stack([col // width, vp * vocab + col]).astype(i32)
        before = first_columns(0, offs[: count + 1], place, xh_a, aux_all, g, w_head, None)
        n_all, auxc_all, chunk = first_columns(1, offs[count:], place, xh_b, aux_all, g, w_head, before)
        moved = [(lax.ppermute(chunk, "dp", pairs), other)]
        whole = None
        for k, (width, col, other, pairs) in enumerate(jobs):
            if k == 0:
                own = (chunk, col)
                continue
            merges = [own] if k == 1 else [moved[k - LAG]] if k >= LAG else []
            chunk, whole = weight_grad(width, col, vp * vocab + col, nt_all, n_all, auxc_all, w_head, whole, merges)
            if k == len(jobs) - 1:
                chunk, parts = lax.optimization_barrier((chunk, parts))
            moved.append((lax.ppermute(chunk, "dp", pairs), other))
        parts = jnp.sum(tiny_gather(parts, everyone, 1), axis=0)
        for chunk, other in moved[-LAG:]:
            whole = lax.dynamic_update_slice(whole, chunk, (0, other))
        return parts[6, 0], d_x[None], whole, parts[:6].reshape(DIM)

    return jax.shard_map(
        local_step,
        mesh=mesh,
        in_specs=(P("dp", "vp", None), P("dp", "vp"), P("dp", "vp"), P(None), P(None, "vp")),
        out_specs=(P(), P("dp", "vp", None), P(None, "vp"), P(None)),
        check_vma=False,
    )
```

time: 926 us -> 985 us (1.064)
  waiting for transfers between devices: 300 us -> 402 us
  Pallas kernels: 542 us -> 463 us
  blocking collectives: 5.63 us -> 37.3 us
    pallas_call x3 -> x1, Pallas kernels: 168 us -> 32.2 us  [tiny_gather(): pl.pallas_call(functools.partial(tiny_gather_kernel, dp_count, vp_count),...]
    reduce_scatter x1, waiting for transfers between devices: 38.2 us -> 106 us  [local_step(): d_normed = lax.psum_scatter(dn_part, 'vp', scatter_dimension=0, tiled=True)]
    pallas_call x10 -> x14, Pallas kernels: 335 us -> 390 us  [the longest x10 258 us: weight_grad(): pl.pallas_call(functools.partial(dw_kernel, len(merges)), grid_spec=pltpu...]
    all_gather x1 -> x2, waiting for transfers between devices: 202 us -> 236 us  [the longest x1 124 us: local_step(): xh_b = lax.all_gather(x_hat[BLK // 2:], ('dp', 'vp'), axis=0, tiled=True)]
    ppermute x8 -> x11, waiting for transfers between devices: 59.9 us -> 27 us  [the longest x10 27 us: local_step(): moved.append((lax.ppermute(chunk, 'dp', pairs), other))]
    ppermute x1, waiting for transfers between devices: 0.01 us -> 32.4 us  [local_step(): from_x = lax.ppermute(x_hat, 'vp', x_pairs)]
    all_gather x1 -> x2, blocking collectives: 5.63 us -> 37.3 us  [the longest x1 31.8 us: local_step(): lax.all_gather(jnp.concatenate([lse_row[:, None], info_row], axis=1), 'dp...]
  transfers between devices with their start and end apart: 13 -> 17, of which waited for: 5 -> 6; matrix products, arithmetic and copies ran while one was open for 4% -> 3% of each run, Pallas kernels for 44% -> 37%
where the time goes in v3:
time: 985 us; the launch traced here: 978 us
  Pallas kernels  463 us (47%)
  waiting for transfers between devices  402 us (41%)
  blocking collectives  37.3 us (4%)
  other arithmetic  20.6 us (2%)
  between operations  20.2 us (2%)
  local copies, waits for them, and re-layouts  18.7 us (2%)
  starting transfers between devices  12.6 us (1%)
    pallas_call x10, Pallas kernels, weight_grad(): pl.pallas_call(functools.partial(dw_kernel, len(merges)), grid_spec=pltpu...  258 us
    all_gather x1, waiting for transfers between devices, local_step(): xh_b = lax.all_gather(x_hat[BLK // 2:], ('dp', 'vp'), axis=0, tiled=True)  124 us
    all_gather x1, waiting for transfers between devices, local_step(): xh_a = lax.all_gather(x_hat[:BLK // 2], ('dp', 'vp'), axis=0, tiled=True)  112 us
    reduce_scatter x1, waiting for transfers between devices, local_step(): d_normed = lax.psum_scatter(dn_part, 'vp', scatter_dimension=0, tiled=True)  106 us
    pallas_call x2, Pallas kernels, forward_stats(): pl.pallas_call(fwd_kernel, grid=(vocab // FWD_COLS,), in_specs=[pl.BlockS...  78.1 us
    pallas_call x2, Pallas kernels, first_columns(): pl.pallas_call(functools.partial(first_kernel, final), grid_spec=pltpu.Pr...  53.9 us
    pallas_call x1, Pallas kernels, backward_dn(): pl.pallas_call(dn_kernel, grid_spec=pltpu.PrefetchScalarGridSpec(num_scal...  40.6 us
    ppermute x1, waiting for transfers between devices, local_step(): from_x = lax.ppermute(x_hat, 'vp', x_pairs)  32.4 us
  transfers between devices with their start and end apart: 17, of which 6 were waited for; matrix products, arithmetic and copies ran while one was open for 3% of the time, Pallas kernels for 37%

profile of v3, /device:TPU:0, one launch (start us, length us, event | category | flops | bytes accessed | tf_op | source)
XLA Modules:
  0.0 978.1 jit_solution(9870986647340378709)
XLA Ops:
  8.1 1.4 reduce_sum.112
  9.4 0.8 select_reduce_fusion.1
  10.3 1.3 compare_select_fusion.3
  12.5 1.0 copy-done.2
  13.5 3.0 collective-permute-start.1
  18.5 32.4 %collective-permute-done.1.xa = f32[512,768]{1,0:T(8,128)} collective-permute-done((f32[512,768]{1,0:T(8,128)S(1)}, f32[512,768]{1,0:T(8,128)}, u32[]{:S(2)}, u32[]{:S(2)}) %collective-permute-start.1) | collective-permute-done | bytes 1572896 | tf_op jit(solution)/shard_map/ppermute | solution.py:496
  51.0 39.0 %fwd_stats.2 = (bf16[1024,768]{1,0:T(8,128)(2,1)}, f32[2,2,512]{2,1,0:T(2,128)}) custom-call(f32[512,768]{1,0:T(8,128)} %copy-done.5, f32[512,768]{1,0:T(8,128)} %collective-permute-done.xb, f32[1,768]{1,0:T(1,128)} %reshape.190.g_ref, bf16[768,16384]{1,0:T(8,128)(2,1)} %w_ref.29), custom_call_target="tpu_custom_call" | custom-call | flops 25769803776 | bytes 33030144 | tf_op jit(solution)/shard_map/fwd_stats/pallas_call | solution.py:134
  90.0 39.0 %fwd_stats.3 = (bf16[1024,768]{1,0:T(8,128)(2,1)}, f32[2,2,512]{2,1,0:T(2,128)}) custom-call(f32[512,768]{1,0:T(8,128)} %collective-permute-done.1.xa, f32[512,768]{1,0:T(8,128)} %collective-permute-done.2.xb, f32[1,768]{1,0:T(1,128)} %reshape.190.g_ref, bf16[768,16384]{1,0:T(8,128)(2,1)} %w_ref.29), custom_call_target="tpu_custom_call" | custom-call | flops 25769803776 | bytes 33030144 | tf_op jit(solution)/shard_map/fwd_stats/pallas_call | solution.py:134
  129.0 0.7 pad_maximum_fusion.2
  129.7 5.5 all-gather
  135.6 31.8 %all_gather.17 = f32[32,3,512]{2,1,0:T(4,128)S(1)} all-gather(f32[4,3,512]{2,1,0:T(4,128)S(1)} %pad_maximum_fusion.1), channel_id=1, replica_groups=mesh['dp'=8,'vp'=4] {'dp'}, dimensions={0}, use_global_device_ids=true | all-gather | bytes 221184 | tf_op jit(solution)/shard_map/all_gather | solution.py:511
  167.4 1.2 fusion.15
  168.6 1.2 fusion.17
  172.2 0.7 dynamic-slice_reduce_fusion.kept_ref
  174.2 40.6 %backward_dn.1 = (f32[2048,768]{1,0:T(8,128)}, f32[8,128]{1,0:T(8,128)}) custom-call(s32[4]{0:T(128)} %bitcast_subtract_fusion.offs_ref, s32[4]{0:T(128)} %copy-done.21, s32[4]{0:T(128)} %dynamic-slice_reduce_fusion.kept_ref, s32[4]{0:T(128)} %iota_xor_fusion.mine_ref, s32[1]{0:T(128)} %bitcast.76.nt_ref, s32[1]{0:T(128)} %bitcast.77.col_ref, ...), custom_call_target="tpu_custom_call" | custom-call | flops 103079215104 | bytes 34603008 | tf_op jit(solution)/shard_map/backward_dn/pallas_call | solution.py:217
  215.0 1.3 copy-done.6
  216.3 1.2 fusion.19
  225.3 1.3 select_reduce_fusion.2
  229.8 105.7 %reduce-scatter.2.cloned.1.call-done = f32[512,768]{1,0:T(8,128)} async-done(((f32[2048,768]{1,0:T(8,128)}), f32[512,768]{1,0:T(8,128)}) %reduce-scatter.2.cloned.1.call-update) | async-done | bytes 1572880 | tf_op jit(solution)/shard_map/reduce_scatter | solution.py:538
  335.5 1.9 multiply_reduce_fusion
  338.6 111.9 %all-gather.6.cloned.1.call-done = f32[8192,768]{1,0:T(8,128)} async-done(((f32[256,768]{1,0:T(8,128)}), f32[8192,768]{1,0:T(8,128)}) %all-gather.6.cloned.1.call-update) | async-done | bytes 25165840 | tf_op jit(solution)/shard_map/all_gather | solution.py:497
  450.6 30.4 %first_columns.2 = (bf16[16384,768]{1,0:T(8,128)(2,1)}, f32[16384,128]{1,0:T(8,128)}, f32[768,1024]{1,0:T(8,128)}) custom-call(s32[33]{0:T(128)} %bitcast.142, s32[2]{0:T(128)} %pad_add_fusion.1.place_ref, f32[32,256,768]{2,1,0:T(8,128)} %bitcast.128, f32[32,8,512]{2,1,0:T(8,128)} %copy-done.7, f32[1,768]{1,0:T(1,128)} %reshape.190.g_ref, ...), custom_call_target="tpu_custom_call" | custom-call | flops 12884901888 | bytes 50331648 | tf_op jit(solution)/shard_map/first_columns/pallas_call | solution.py:348
  480.9 124.2 %all-gather.4.cloned.1.call-done = f32[8192,768]{1,0:T(8,128)} async-done(((f32[256,768]{1,0:T(8,128)}), f32[8192,768]{1,0:T(8,128)}) %all-gather.4.cloned.1.call-update) | async-done | bytes 25165840 | tf_op jit(solution)/shard_map/all_gather | solution.py:498
  605.2 23.5 %first_columns.3 = (bf16[16384,768]{1,0:T(8,128)(2,1)}, f32[16384,128]{1,0:T(8,128)}, f32[768,1024]{1,0:T(8,128)}) custom-call(s32[33]{0:T(128)} %slice_reduce_fusion.offs_ref, s32[2]{0:T(128)} %pad_add_fusion.1.place_ref, f32[32,256,768]{2,1,0:T(8,128)} %bitcast.129, f32[32,8,512]{2,1,0:T(8,128)} %copy-done.7, ...), custom_call_target="tpu_custom_call", output_to_operand_aliasing={{0}: (6, {}), {1}: (7, {})} | custom-call | flops 12884901888 | bytes 50331648 | tf_op jit(solution)/shard_map/first_columns/pallas_call | solution.py:348
  628.7 1.5 collective-permute-start.3
  630.2 33.5 %weight_grad.10 = (f32[768,1024]{1,0:T(8,128)}, f32[768,16384]{1,0:T(8,128)}) custom-call(s32[4]{0:T(128)} %get-tuple-element.108.place_ref, s32[1]{0:T(128)S(6)} %select_n.129.nt_ref, bf16[16384,768]{1,0:T(8,128)(2,1)} %get-tuple-element.43.n_hbm, f32[16384,128]{1,0:T(8,128)} %get-tuple-element.44.aux_hbm, bf16[768,16384]{1,0:T(8,128)(2,1)} %w_ref.29, ...), custom_call_target="tpu_custom_call" | custom-call | flops 25769803776 | bytes 31457280 | tf_op jit(solution)/shard_map/weight_grad/pallas_call | solution.py:443
  663.8 32.4 %weight_grad.11 = (f32[768,1024]{1,0:T(8,128)}, f32[768,16384]{1,0:T(8,128)}) custom-call(s32[3]{0:T(128)} %get-tuple-element.107.place_ref, s32[1]{0:T(128)S(6)} %select_n.129.nt_ref, bf16[16384,768]{1,0:T(8,128)(2,1)} %get-tuple-element.43.n_hbm, f32[16384,128]{1,0:T(8,128)} %get-tuple-element.44.aux_hbm, ...), custom_call_target="tpu_custom_call", output_to_operand_aliasing={{1}: (5, {})} | custom-call | flops 25769803776 | bytes 31457280 | tf_op jit(solution)/shard_map/weight_grad/pallas_call | solution.py:443
  696.2 32.4 %weight_grad.12 = (f32[768,1024]{1,0:T(8,128)}, f32[768,16384]{1,0:T(8,128)}) custom-call(s32[3]{0:T(128)} %get-tuple-element.106.place_ref, s32[1]{0:T(128)S(6)} %select_n.129.nt_ref, bf16[16384,768]{1,0:T(8,128)(2,1)} %get-tuple-element.43.n_hbm, f32[16384,128]{1,0:T(8,128)} %get-tuple-element.44.aux_hbm, ...), custom_call_target="tpu_custom_call", output_to_operand_aliasing={{1}: (5, {})} | custom-call | flops 25769803776 | bytes 31457280 | tf_op jit(solution)/shard_map/weight_grad/pallas_call | solution.py:443
  728.7 2.1 collective-permute-start.6
  731.3 33.6 %weight_grad.13 = (f32[768,1024]{1,0:T(8,128)}, f32[768,16384]{1,0:T(8,128)}) custom-call(s32[4]{0:T(128)} %pad_add_fusion.8.place_ref, s32[1]{0:T(128)S(6)} %select_n.129.nt_ref, bf16[16384,768]{1,0:T(8,128)(2,1)} %get-tuple-element.43.n_hbm, f32[16384,128]{1,0:T(8,128)} %get-tuple-element.44.aux_hbm, ...), custom_call_target="tpu_custom_call", output_to_operand_aliasing={{1}: (5, {})} | custom-call | flops 25769803776 | bytes 31457280 | tf_op jit(solution)/shard_map/weight_grad/pallas_call | solution.py:443
  765.0 1.5 collective-permute-start.7
  766.5 33.5 %weight_grad.14 = (f32[768,1024]{1,0:T(8,128)}, f32[768,16384]{1,0:T(8,128)}) custom-call(s32[4]{0:T(128)} %pad_add_fusion.7.place_ref, s32[1]{0:T(128)S(6)} %select_n.129.nt_ref, bf16[16384,768]{1,0:T(8,128)(2,1)} %get-tuple-element.43.n_hbm, f32[16384,128]{1,0:T(8,128)} %get-tuple-element.44.aux_hbm, ...), custom_call_target="tpu_custom_call", output_to_operand_aliasing={{1}: (5, {})} | custom-call | flops 25769803776 | bytes 31457280 | tf_op jit(solution)/shard_map/weight_grad/pallas_call | solution.py:443
  800.1 1.9 collective-permute-done.5.rest_1_
  802.1 20.8 %weight_grad.15 = (f32[768,512]{1,0:T(8,128)}, f32[768,16384]{1,0:T(8,128)}) custom-call(s32[4]{0:T(128)} %pad_add_fusion.6.place_ref, s32[1]{0:T(128)S(6)} %select_n.129.nt_ref, bf16[16384,768]{1,0:T(8,128)(2,1)} %get-tuple-element.43.n_hbm, f32[16384,128]{1,0:T(8,128)} %get-tuple-element.44.aux_hbm, ...), custom_call_target="tpu_custom_call", output_to_operand_aliasing={{1}: (5, {})} | custom-call | flops 12884901888 | bytes 28311552 | tf_op jit(solution)/shard_map/weight_grad/pallas_call | solution.py:443
  822.9 20.8 %weight_grad.16 = (f32[768,512]{1,0:T(8,128)}, f32[768,16384]{1,0:T(8,128)}) custom-call(s32[4]{0:T(128)} %pad_add_fusion.5.place_ref, s32[1]{0:T(128)S(6)} %select_n.129.nt_ref, bf16[16384,768]{1,0:T(8,128)(2,1)} %get-tuple-element.43.n_hbm, f32[16384,128]{1,0:T(8,128)} %get-tuple-element.44.aux_hbm, ...), custom_call_target="tpu_custom_call", output_to_operand_aliasing={{1}: (5, {})} | custom-call | flops 12884901888 | bytes 28311552 | tf_op jit(solution)/shard_map/weight_grad/pallas_call | solution.py:443
  844.4 25.1 %collective-permute-done.7.rest_1_ = f32[768,1024]{1,0:T(8,128)} collective-permute-done((f32[768,1024]{1,0:T(8,128)}, f32[768,1024]{1,0:T(8,128)}, u32[]{:S(2)}, u32[]{:S(2)}) %collective-permute-start.7) | collective-permute-done | bytes 3145760 | tf_op jit(solution)/shard_map/ppermute | solution.py:575
  869.5 20.8 %weight_grad.17 = (f32[768,512]{1,0:T(8,128)}, f32[768,16384]{1,0:T(8,128)}) custom-call(s32[4]{0:T(128)} %pad_add_fusion.4.place_ref, s32[1]{0:T(128)S(6)} %select_n.129.nt_ref, bf16[16384,768]{1,0:T(8,128)(2,1)} %get-tuple-element.43.n_hbm, f32[16384,128]{1,0:T(8,128)} %get-tuple-element.44.aux_hbm, ...), custom_call_target="tpu_custom_call", output_to_operand_aliasing={{1}: (5, {})} | custom-call | flops 12884901888 | bytes 28311552 | tf_op jit(solution)/shard_map/weight_grad/pallas_call | solution.py:443
  890.9 15.5 %weight_grad.18 = (f32[768,256]{1,0:T(8,128)}, f32[768,16384]{1,0:T(8,128)}) custom-call(s32[4]{0:T(128)} %pad_add_fusion.3.place_ref, s32[1]{0:T(128)S(6)} %select_n.129.nt_ref, bf16[16384,768]{1,0:T(8,128)(2,1)} %get-tuple-element.43.n_hbm, f32[16384,128]{1,0:T(8,128)} %get-tuple-element.44.aux_hbm, ...), custom_call_target="tpu_custom_call", output_to_operand_aliasing={{1}: (5, {})} | custom-call | flops 6442450944 | bytes 26738688 | tf_op jit(solution)/shard_map/weight_grad/pallas_call | solution.py:443
  906.5 1.1 copy-done.8
  907.6 14.8 %weight_grad.19 = (f32[768,256]{1,0:T(8,128)}, f32[768,16384]{1,0:T(8,128)}) custom-call(s32[4]{0:T(128)} %pad_add_fusion.place_ref, s32[1]{0:T(128)S(6)} %select_n.129.nt_ref, bf16[16384,768]{1,0:T(8,128)(2,1)} %get-tuple-element.43.n_hbm, f32[16384,128]{1,0:T(8,128)} %get-tuple-element.44.aux_hbm, ...), custom_call_target="tpu_custom_call", output_to_operand_aliasing={{1}: (5, {})} | custom-call | flops 6442450944 | bytes 26738688 | tf_op jit(solution)/shard_map/weight_grad/pallas_call | solution.py:443
  922.6 2.0 collective-permute-start.12
  924.6 3.2 fusion
  927.8 32.2 %tiny_gather.1 = f32[32,8,128]{2,1,0:T(8,128)} custom-call(f32[8,128]{1,0:T(8,128)} %concatenate.19.x_ref), custom_call_target="tpu_custom_call" | custom-call | tf_op jit(solution)/shard_map/tiny_gather/pallas_call | solution.py:64
  960.0 0.9 reduce_sum.121
  961.5 2.7 constant_dynamic-update-slice_fusion.3
  964.8 2.7 constant_dynamic-update-slice_fusion.2
  967.5 2.1 constant_dynamic-update-slice_fusion.1
  969.6 0.9 constant_dynamic-update-slice_fusion
  (123 shorter events, 18.3 us)
Async XLA Ops:
  8.0 3.6 copy-start
  8.0 327.5 %reduce-scatter.2.cloned.1.call-start = ((), (), s32[]{:S(2)}) async-start(), calls=%async_computation.3 | async-start | bytes 7864320 | tf_op jit(solution)/shard_map/reduce_scatter | solution.py:538
  11.6 5.5 copy-start.15
  12.3 1.2 copy-start.2
  12.3 1.2 copy-start.9
  12.3 4.8 copy-start.20
  12.3 5.0 copy-start.12
  13.5 37.5 %copy-start.5 = (f32[512,768]{1,0:T(8,128)}, f32[512,768]{1,0:T(8,128)S(1)}, u32[]{:S(2)}) copy-start(f32[512,768]{1,0:T(8,128)S(1)} %broadcast_multiply_fusion.xa) | copy-start | bytes 4718596
  13.5 37.5 %collective-permute-start.1 = (f32[512,768]{1,0:T(8,128)S(1)}, f32[512,768]{1,0:T(8,128)}, u32[]{:S(2)}, u32[]{:S(2)}) collective-permute-start(f32[512,768]{1,0:T(8,128)S(1)} %broadcast_multiply_fusion.xa), channel_id=1, source_target_pairs={{0,2},{1,3},{2,0},{3,1},{4,6},{5,7},{6,4},{7,5},{8,10},{9,11},{10,... | collective-permute-start | bytes 4718600 | tf_op jit(solution)/shard_map/ppermute | solution.py:496
  16.4 34.5 %collective-permute-start = (f32[512,768]{1,0:T(8,128)S(1)}, f32[512,768]{1,0:T(8,128)}, u32[]{:S(2)}, u32[]{:S(2)}) collective-permute-start(f32[512,768]{1,0:T(8,128)S(1)} %broadcast_multiply_fusion.xa), channel_id=1, source_target_pairs={{0,1},{1,0},{2,3},{3,2},{4,5},{5,4},{6,7},{7,6},{8,9},{9,8},{10,11... | collective-permute-start | bytes 4718600 | tf_op jit(solution)/shard_map/ppermute | solution.py:495
  51.0 39.0 %collective-permute-start.2 = (f32[512,768]{1,0:T(8,128)}, f32[512,768]{1,0:T(8,128)}, u32[]{:S(2)}, u32[]{:S(2)}) collective-permute-start(f32[512,768]{1,0:T(8,128)} %collective-permute-done.1.xa), channel_id=1, source_target_pairs={{0,1},{1,0},{2,3},{3,2},{4,5},{5,4},{6,7},{7,6},{8,9},{9,8},{10,11... | collective-permute-start | bytes 4718600 | tf_op jit(solution)/shard_map/ppermute | solution.py:500
  90.0 39.0 %copy-start.18 = (f32[2,2,512]{2,1,0:T(2,128)S(1)}, f32[2,2,512]{2,1,0:T(2,128)}, u32[]{:S(2)}) copy-start(f32[2,2,512]{2,1,0:T(2,128)} %get-tuple-element.38) | copy-start | bytes 24580
  169.8 4.4 copy-start.21
  173.5 41.3 %copy-start.7 = (f32[32,8,512]{2,1,0:T(8,128)}, f32[32,8,512]{2,1,0:T(8,128)S(1)}, u32[]{:S(2)}) copy-start(f32[32,8,512]{2,1,0:T(8,128)S(1)} %stack.211.aux_ref) | copy-start | bytes 1572868
  214.9 1.4 copy-start.6
  214.9 235.7 %all-gather.6.cloned.1.call-start = ((), (), s32[]{:S(2)}) async-start(), calls=%async_computation.2 | async-start | bytes 25952256 | tf_op jit(solution)/shard_map/all_gather | solution.py:497
  217.5 9.8 %copy-start.19 = (f32[8,128]{1,0:T(8,128)S(1)}, f32[8,128]{1,0:T(8,128)}, u32[]{:S(2)}) copy-start(f32[8,128]{1,0:T(8,128)} %get-tuple-element.65) | copy-start | bytes 12292
  217.5 118.0 %copy-start.3 = (f32[512,768]{1,0:T(8,128)S(1)}, f32[512,768]{1,0:T(8,128)}, u32[]{:S(2)}) copy-start(f32[512,768]{1,0:T(8,128)} %copy-done.2) | copy-start | bytes 4718596
  217.5 118.0 %copy-start.10 = (f32[512]{0:T(512)S(1)}, f32[512]{0:T(512)}, u32[]{:S(2)}) copy-start(f32[512]{0:T(512)} %copy-done.9) | copy-start | bytes 6148
  217.5 118.0 %copy-start.13 = (f32[768]{0:T(1024)S(1)}, f32[768]{0:T(1024)}, u32[]{:S(2)}) copy-start(f32[768]{0:T(1024)} %param.8) | copy-start | bytes 9220
  217.6 387.6 %all-gather.4.cloned.1.call-start = ((), (), s32[]{:S(2)}) async-start(), calls=%async_computation.1 | async-start | bytes 25952256 | tf_op jit(solution)/shard_map/all_gather | solution.py:498
  628.7 102.6 %collective-permute-start.3 = (f32[768,1024]{1,0:T(8,128)}, f32[768,1024]{1,0:T(8,128)}, u32[]{:S(2)}, u32[]{:S(2)}) collective-permute-start(f32[768,1024]{1,0:T(8,128)} %get-tuple-element.45.rest_0_), channel_id=1, source_target_pairs={{0,4},{4,0},{8,12},{12,8},{16,20},{20,16},{24,28},{28,24},{1,5},{5... | collective-permute-start | bytes 9437192 | tf_op jit(solution)/shard_map/ppermute | solution.py:565
  663.7 102.8 %collective-permute-start.4 = (f32[768,1024]{1,0:T(8,128)}, f32[768,1024]{1,0:T(8,128)}, u32[]{:S(2)}, u32[]{:S(2)}) collective-permute-start(f32[768,1024]{1,0:T(8,128)} %get-tuple-element.50), channel_id=1, source_target_pairs={{0,8},{4,12},{8,0},{12,4},{16,24},{20,28},{24,16},{28,20},{1,9},{5... | collective-permute-start | bytes 9437192 | tf_op jit(solution)/shard_map/ppermute | solution.py:575
  728.7 94.2 %collective-permute-start.6 = (f32[768,1024]{1,0:T(8,128)}, f32[768,1024]{1,0:T(8,128)}, u32[]{:S(2)}, u32[]{:S(2)}) collective-permute-start(f32[768,1024]{1,0:T(8,128)} %get-tuple-element.54), channel_id=1, source_target_pairs={{0,8},{4,12},{8,0},{12,4},{16,24},{20,28},{24,16},{28,20},{1,9},{5... | collective-permute-start | bytes 9437192 | tf_op jit(solution)/shard_map/ppermute | solution.py:575
  730.8 71.3 %collective-permute-start.5 = (f32[768,1024]{1,0:T(8,128)}, f32[768,1024]{1,0:T(8,128)}, u32[]{:S(2)}, u32[]{:S(2)}) collective-permute-start(f32[768,1024]{1,0:T(8,128)} %get-tuple-element.52), channel_id=1, source_target_pairs={{0,4},{4,0},{8,12},{12,8},{16,20},{20,16},{24,28},{28,24},{1,5},{5... | collective-permute-start | bytes 9437192 | tf_op jit(solution)/shard_map/ppermute | solution.py:575
  765.0 104.5 %collective-permute-start.7 = (f32[768,1024]{1,0:T(8,128)}, f32[768,1024]{1,0:T(8,128)}, u32[]{:S(2)}, u32[]{:S(2)}) collective-permute-start(f32[768,1024]{1,0:T(8,128)} %get-tuple-element.56), channel_id=1, source_target_pairs={{0,4},{4,0},{8,12},{12,8},{16,20},{20,16},{24,28},{28,24},{1,5},{5... | collective-permute-start | bytes 9437192 | tf_op jit(solution)/shard_map/ppermute | solution.py:575
  800.0 90.9 %collective-permute-start.8 = (f32[768,1024]{1,0:T(8,128)}, f32[768,1024]{1,0:T(8,128)}, u32[]{:S(2)}, u32[]{:S(2)}) collective-permute-start(f32[768,1024]{1,0:T(8,128)} %get-tuple-element.58), channel_id=1, source_target_pairs={{0,8},{4,12},{8,0},{12,4},{16,24},{20,28},{24,16},{28,20},{1,9},{5... | collective-permute-start | bytes 9437192 | tf_op jit(solution)/shard_map/ppermute | solution.py:575
  843.7 117.8 %collective-permute-start.10 = (f32[768,512]{1,0:T(8,128)}, f32[768,512]{1,0:T(8,128)}, u32[]{:S(2)}, u32[]{:S(2)}) collective-permute-start(f32[768,512]{1,0:T(8,128)} %get-tuple-element.68), channel_id=1, source_target_pairs={{0,8},{4,12},{8,0},{12,4},{16,24},{20,28},{24,16},{28,20},{1,9},{5... | collective-permute-start | bytes 4718600 | tf_op jit(solution)/shard_map/ppermute | solution.py:575
  843.9 62.6 %collective-permute-start.9 = (f32[768,512]{1,0:T(8,128)}, f32[768,512]{1,0:T(8,128)S(1)}, u32[]{:S(2)}, u32[]{:S(2)}) collective-permute-start(f32[768,512]{1,0:T(8,128)} %get-tuple-element.60), channel_id=1, source_target_pairs={{0,4},{4,0},{8,12},{12,8},{16,20},{20,16},{24,28},{28,24},{1,5},{5... | collective-permute-start | bytes 4718600 | tf_op jit(solution)/shard_map/ppermute | solution.py:575
  890.3 74.5 %collective-permute-start.11 = (f32[768,512]{1,0:T(8,128)}, f32[768,512]{1,0:T(8,128)}, u32[]{:S(2)}, u32[]{:S(2)}) collective-permute-start(f32[768,512]{1,0:T(8,128)} %get-tuple-element.69), channel_id=1, source_target_pairs={{0,4},{4,0},{8,12},{12,8},{16,20},{20,16},{24,28},{28,24},{1,5},{5... | collective-permute-start | bytes 4718600 | tf_op jit(solution)/shard_map/ppermute | solution.py:575
  906.5 1.1 copy-start.8
  907.6 17.0 %copy-start.4 = (f32[512,768]{1,0:T(8,128)S(1)}, f32[512,768]{1,0:T(8,128)}, u32[]{:S(2)}) copy-start(f32[512,768]{1,0:T(8,128)} %copy-done.2) | copy-start | bytes 4718596
  907.6 17.0 %copy-start.11 = (f32[512]{0:T(512)S(1)}, f32[512]{0:T(512)}, u32[]{:S(2)}) copy-start(f32[512]{0:T(512)} %copy-done.9) | copy-start | bytes 6148
  907.6 17.0 %copy-start.14 = (f32[768]{0:T(1024)S(1)}, f32[768]{0:T(1024)}, u32[]{:S(2)}) copy-start(f32[768]{0:T(1024)} %param.8) | copy-start | bytes 9220
  907.6 17.0 %copy-start.16 = (s32[1,512]{1,0:T(1,128)S(1)}, s32[1,512]{1,0:T(1,128)}, u32[]{:S(2)}) copy-start(s32[1,512]{1,0:T(1,128)} %copy-done.15) | copy-start | bytes 6148
  907.6 17.0 %copy-start.17 = (f32[512]{0:T(512)S(1)}, f32[512]{0:T(512)}, u32[]{:S(2)}) copy-start(f32[512]{0:T(512)} %broadcast_multiply_fusion.1) | copy-start | bytes 6148
  922.5 47.1 %collective-permute-start.13 = (f32[768,256]{1,0:T(8,128)}, f32[768,256]{1,0:T(8,128)S(1)}, u32[]{:S(2)}, u32[]{:S(2)}) collective-permute-start(f32[768,256]{1,0:T(8,128)} %get-tuple-element.71), channel_id=1, source_target_pairs={{0,8},{4,12},{8,0},{12,4},{16,24},{20,28},{24,16},{28,20},{1,9},{5... | collective-permute-start | bytes 2359304 | tf_op jit(solution)/shard_map/ppermute | solution.py:575
  922.6 44.9 %collective-permute-start.12 = (f32[768,256]{1,0:T(8,128)}, f32[768,256]{1,0:T(8,128)}, u32[]{:S(2)}, u32[]{:S(2)}) collective-permute-start(f32[768,256]{1,0:T(8,128)} %get-tuple-element.70), channel_id=1, source_target_pairs={{0,8},{4,12},{8,0},{12,4},{16,24},{20,28},{24,16},{28,20},{1,9},{5... | collective-permute-start | bytes 2359304 | tf_op jit(solution)/shard_map/ppermute | solution.py:575
  964.8 5.7 copy-start.1
Sparse Core Ops, SparseCore 0:
  215.0 120.4 reduce-scatter.1
Sparse Core Ops, SparseCore 1:
  218.8 231.7 all-gather.5
  453.3 151.8 all-gather.3

commit v4 on v3

--- a/solution.py
+++ b/solution.py
@@ -13,13 +13,14 @@
 DIM = 768
 ALIGN = 16
 FWD_COLS = 2048
-FWD_GROUP = 512
+FWD_GROUPS = (256, 1024)
 DN_COLS = 2048
 DW_TOK = 1024
 DW_GROUP = 1024
 SUB = 256
-Y_WIDTHS = (1024, 1024, 1024, 512, 512)
-Z_WIDTHS = (1024, 1024, 1024, 512, 256, 256)
+Y_WIDTHS = (1024, 1024, 1024, 1024)
+Z_WIDTHS = (1024, 1024, 1024, 512)
+OWN_WIDTHS = (1024,)
 LAG = 4
 DROPPED = 1e30
 LOG2E = 1.4426950408889634
@@ -83,9 +84,9 @@
     return jnp.concatenate([aux, pad], axis=0).T
 
 
-def fwd_kernel(xa, xb, g_ref, w_ref, n_ref, st_ref, m_ref, s_ref, za_ref, zb_ref):
+def fwd_kernel(group, xa, xb, g_ref, w_ref, n_ref, st_ref, m_ref, s_ref, za_ref, zb_ref):
     j = pl.program_id(0)
-    groups = FWD_COLS // FWD_GROUP
+    groups = FWD_COLS // group
     bufs = (za_ref, zb_ref)
 
     @pl.when(j == 0)
@@ -99,7 +100,7 @@
     def absorb(row, z_ref):
         for r in range(0, BLK, 8):
             rows = pl.ds(pl.multiple_of(row + r, 8), 8)
-            parts = [z_ref[r : r + 8, k * 128 : (k + 1) * 128] for k in range(FWD_GROUP // 128)]
+            parts = [z_ref[r : r + 8, k * 128 : (k + 1) * 128] for k in range(group // 128)]
             m_old = m_ref[rows, :]
             m_new = jnp.maximum(functools.reduce(jnp.maximum, parts), m_old)
             total = functools.reduce(jnp.add, [jnp.exp(part - m_new) for part in parts])
@@ -110,7 +111,7 @@
         row = pl.multiple_of(i * BLK, BLK)
         n = n_ref[pl.ds(row, BLK), :]
         for c in range(groups):
-            cols = pl.ds(c * FWD_GROUP, FWD_GROUP)
+            cols = pl.ds(c * group, group)
             bufs[c % 2][...] = jnp.dot(n, w_ref[:, cols], preferred_element_type=f32)
             absorb(row if c else pl.multiple_of((1 - i) * BLK, BLK), bufs[(c + 1) % 2])
         return carry
@@ -129,10 +130,10 @@
             st_ref[k, 1:2, :] = jnp.broadcast_to(s, (BLK, 128)).T[0:1, :]
 
 
-def forward_stats(xa, xb, g, w):
+def forward_stats(group, xa, xb, g, w):
     vocab = w.shape[1]
     return pl.pallas_call(
-        fwd_kernel,
+        functools.partial(fwd_kernel, group),
         grid=(vocab // FWD_COLS,),
         in_specs=[pl.BlockSpec((BLK, DIM), lambda j: (0, 0))] * 2
         + [
@@ -146,8 +147,8 @@
         scratch_shapes=[
             pltpu.VMEM((2 * BLK, 128), f32),
             pltpu.VMEM((2 * BLK, 128), f32),
-            pltpu.VMEM((BLK, FWD_GROUP), f32),
-            pltpu.VMEM((BLK, FWD_GROUP), f32),
+            pltpu.VMEM((BLK, group), f32),
+            pltpu.VMEM((BLK, group), f32),
         ],
         out_shape=[
             jax.ShapeDtypeStruct((2 * BLK, DIM), bf16),
@@ -263,104 +264,84 @@
         )
 
 
-def first_kernel(final, offs_ref, place_ref, xh_ref, aux_ref, g_ref, w_ref, *rest):
-    n_hbm, aux_hbm, acc_ref, n_img, aux_img, dz_ref, sems = rest[-7:]
+def first_kernel(offs_ref, table_ref, xh_ref, aux_ref, g_ref, w_ref, n_hbm, aux_hbm, acc_ref, n_img, aux_img, dz_ref, sems):
     step = pl.program_id(0)
     last = pl.num_programs(0) - 1
-    half = BLK // 2
-    base = offs_ref[0] // DW_TOK
     end = offs_ref[offs_ref.shape[0] - 1]
 
-    def images(t):
-        rows = pl.ds(pl.multiple_of((t - base) * DW_TOK, DW_TOK), DW_TOK)
-        return n_img.at[rows, :], aux_img.at[rows, :]
-
-    def places(t):
+    def copies(t):
         rows = pl.ds(pl.multiple_of(t * DW_TOK, DW_TOK), DW_TOK)
-        return n_hbm.at[rows, :], aux_hbm.at[rows, :]
-
-    def copies(t):
-        return [pltpu.make_async_copy(a, b, sems.at[k]) for k, (a, b) in enumerate(zip(images(t), places(t)))]
+        return (
+            pltpu.make_async_copy(n_img.at[rows, :], n_hbm.at[rows, :], sems.at[0]),
+            pltpu.make_async_copy(aux_img.at[rows, :], aux_hbm.at[rows, :], sems.at[1]),
+        )
 
     @pl.when(step == 0)
     def _():
-        if final:
-            acc_ref[...] = rest[2][...]
-            loads = [pltpu.make_async_copy(b, a, sems.at[k]) for k, (a, b) in enumerate(zip(images(base), places(base)))]
-            for copy in loads:
-                copy.start()
-            for copy in loads:
-                copy.wait()
-        else:
-            acc_ref[...] = jnp.zeros_like(acc_ref)
-
-    for k in range(4):
-        off = pl.multiple_of(offs_ref[step * 4 + k] - base * DW_TOK, ALIGN)
-        n_img[pl.ds(off, half), :] = (xh_ref[k] * g_ref[...]).astype(bf16)
-        aux_img[pl.ds(off, half), :] = aux_columns(aux_ref[k])
+        acc_ref[...] = jnp.zeros_like(acc_ref)
+
+    for k in range(xh_ref.shape[0]):
+        off = pl.multiple_of(offs_ref[step * xh_ref.shape[0] + k], ALIGN)
+        n_img[pl.ds(off, BLK), :] = (xh_ref[k] * g_ref[...]).astype(bf16)
+        aux_img[pl.ds(off, BLK), :] = aux_columns(aux_ref[k])
 
     @pl.when(step == last)
     def _():
-        rows = pl.ds(pl.multiple_of(end - base * DW_TOK, ALIGN), DW_TOK)
+        rows = pl.ds(pl.multiple_of(end, ALIGN), DW_TOK)
         n_img[rows, :] = jnp.zeros((DW_TOK, DIM), bf16)
         aux_img[rows, :] = jnp.zeros((DW_TOK, 128), f32)
 
-    full = offs_ref[step * 4 + 4] // DW_TOK
-    stop = jnp.where(step == last, (end + DW_TOK - 1) // DW_TOK, full) if final else full
+    start = offs_ref[step * xh_ref.shape[0]] // DW_TOK
+    stop = offs_ref[(step + 1) * xh_ref.shape[0]] // DW_TOK
+    stop = jnp.where(step == last, (end + DW_TOK - 1) // DW_TOK, stop)
 
     def tile(t, carry):
         for copy in copies(t):
             copy.start()
-        row = (t - base) * DW_TOK
-
-        def rows(start, size):
-            return pl.ds(pl.multiple_of(row, DW_TOK) + start, size)
-
+        row = pl.multiple_of(t * DW_TOK, DW_TOK)
         dw_tile(
-            lambda *r: n_img[rows(*r), :], lambda *r: aux_img[rows(*r), :], w_ref, dz_ref, acc_ref, place_ref[1]
+            lambda at, size: n_img[pl.ds(row + at, size), :],
+            lambda at, size: aux_img[pl.ds(row + at, size), :],
+            w_ref,
+            dz_ref,
+            acc_ref,
+            table_ref[1],
         )
         return carry
 
-    lax.fori_loop(offs_ref[step * 4] // DW_TOK, stop, tile, 0)
+    lax.fori_loop(start, stop, tile, 0)
 
     @pl.when(step == last)
     def _():
-        if not final:
-            for copy in copies(full):
-                copy.start()
-
         def drain(t, carry):
             for copy in copies(t):
                 copy.wait()
             return carry
 
-        lax.fori_loop(base, stop if final else full + 1, drain, 0)
-
-
-def first_columns(half, offs, place, xh_half, aux_all, g, w, before):
+        lax.fori_loop(0, stop, drain, 0)
+
+
+def first_columns(offs, table, xh_all, aux_all, g, w):
     blocks = aux_all.shape[0]
     tokens = blocks * BLK
-    image = tokens // 2 + 2 * DW_TOK
     width = Y_WIDTHS[0]
+    each = 2
     anywhere = pl.BlockSpec(memory_space=pl.ANY)
-    whole_chunk = pl.BlockSpec((DIM, width), lambda b, *_: (0, 0))
-    final = before is not None
     return pl.pallas_call(
-        functools.partial(first_kernel, final),
+        first_kernel,
         grid_spec=pltpu.PrefetchScalarGridSpec(
             num_scalar_prefetch=2,
-            grid=(blocks // 4,),
+            grid=(blocks // each,),
             in_specs=[
-                pl.BlockSpec((4, BLK // 2, DIM), lambda b, *_: (b, 0, 0)),
-                pl.BlockSpec((4, 8, BLK // 2), lambda b, *_: (b, 0, half)),
+                pl.BlockSpec((each, BLK, DIM), lambda b, *_: (b, 0, 0)),
+                pl.BlockSpec((each, 8, BLK), lambda b, *_: (b, 0, 0)),
                 pl.BlockSpec((1, DIM), lambda b, *_: (0, 0)),
-                pl.BlockSpec((DIM, width), lambda b, offs, place: (0, place[0])),
-            ]
-            + ([anywhere, anywhere, whole_chunk] if final else []),
-            out_specs=[anywhere, anywhere, whole_chunk],
+                pl.BlockSpec((DIM, width), lambda b, offs, table: (0, table[0])),
+            ],
+            out_specs=[anywhere, anywhere, pl.BlockSpec((DIM, width), lambda b, *_: (0, 0))],
             scratch_shapes=[
-                pltpu.VMEM((image, DIM), bf16),
-                pltpu.VMEM((image, 128), f32),
+                pltpu.VMEM((tokens + DW_TOK, DIM), bf16),
+                pltpu.VMEM((tokens + DW_TOK, 128), f32),
                 pltpu.VMEM((DW_TOK, width), bf16),
                 pltpu.SemaphoreType.DMA((2,)),
             ],
@@ -370,16 +351,16 @@
             jax.ShapeDtypeStruct((tokens, 128), f32),
             jax.ShapeDtypeStruct((DIM, width), f32),
         ],
-        input_output_aliases={6: 0, 7: 1} if final else {},
         compiler_params=pltpu.CompilerParams(dimension_semantics=("arbitrary",), vmem_limit_bytes=60 << 20),
         cost_estimate=pl.CostEstimate(
-            flops=tokens * DIM * width, bytes_accessed=4 * tokens * DIM, transcendentals=tokens * width // 4
+            flops=2 * tokens * DIM * width, bytes_accessed=6 * tokens * DIM, transcendentals=tokens * width // 2
         ),
         name="first_columns",
-    )(offs, place, xh_half.reshape(blocks, BLK // 2, DIM), aux_all, g, w, *(before or ()))
-
-
-def dw_kernel(merges, place_ref, nt_ref, n_hbm, aux_hbm, w_ref, *rest):
+    )(offs, table, xh_all.reshape(blocks, BLK, DIM), aux_all, g, w)
+
+
+def dw_kernel(job, places, table_ref, nt_ref, n_hbm, aux_hbm, w_ref, *rest):
+    merges = len(places)
     inputs, rest = rest[: -(6 + merges + 1)], rest[-(6 + merges + 1) :]
     out_ref, all_hbm, nbuf, abuf, dz_ref, sems = rest[:6]
     mbufs, out_sems = rest[6:-1], rest[-1]
@@ -398,7 +379,7 @@
     for copy in fetch(0, 0):
         copy.start()
     moves_in = [pltpu.make_async_copy(src, mbuf, out_sems.at[k, 0]) for k, (src, mbuf) in enumerate(zip(inputs[-merges:], mbufs))]
-    moves_out = [put(mbuf, place_ref[3 + k], out_sems.at[k, 1]) for k, mbuf in enumerate(mbufs)]
+    moves_out = [put(mbuf, table_ref[places[k]], out_sems.at[k, 1]) for k, mbuf in enumerate(mbufs)]
     for copy in moves_in:
         copy.start()
     out_ref[...] = jnp.zeros_like(out_ref)
@@ -419,12 +400,12 @@
             w_ref,
             dz_ref,
             out_ref,
-            place_ref[1],
+            table_ref[4 * job + 1],
         )
         return carry
 
     lax.fori_loop(0, steps, tile, 0)
-    own = put(out_ref, place_ref[2], out_sems.at[merges, 0])
+    own = put(out_ref, table_ref[4 * job + 2], out_sems.at[merges, 0])
     own.start()
     for copy in moves_in:
         copy.wait()
@@ -434,18 +415,17 @@
         copy.wait()
 
 
-def weight_grad(width, col, vocab_col, ntiles, n_all, aux_all, w, whole, merges):
+def weight_grad(job, width, table, ntiles, n_all, aux_all, w, whole, merges):
     tokens, vocab = n_all.shape[0], w.shape[1]
     anywhere = pl.BlockSpec(memory_space=pl.ANY)
     chunks = [chunk for chunk, _ in merges]
     held = ([] if whole is None else [whole]) + chunks
-    place = jnp.stack([col // width, vocab_col, col] + [c for _, c in merges]).astype(i32)
     return pl.pallas_call(
-        functools.partial(dw_kernel, len(merges)),
+        functools.partial(dw_kernel, job, [at for _, at in merges]),
         grid_spec=pltpu.PrefetchScalarGridSpec(
             num_scalar_prefetch=2,
             grid=(1,),
-            in_specs=[anywhere, anywhere, pl.BlockSpec((DIM, width), lambda s, place, nt: (0, place[0]))]
+            in_specs=[anywhere, anywhere, pl.BlockSpec((DIM, width), lambda s, table, nt: (0, table[4 * job]))]
             + [anywhere] * len(held),
             out_specs=[pl.BlockSpec((DIM, width), lambda s, *_: (0, 0)), anywhere],
             scratch_shapes=[
@@ -467,7 +447,7 @@
             flops=2 * tokens * DIM * width, bytes_accessed=2 * tokens * DIM + 8 * DIM * width, transcendentals=tokens * width // 2
         ),
         name="weight_grad",
-    )(place, ntiles, n_all, aux_all, w, *held)
+    )(table, ntiles, n_all, aux_all, w, *held)
 
 
 def solution(mesh):
@@ -494,11 +474,10 @@
         x_pairs = [(v, v ^ 2) for v in range(vp_count)]
         from_core = lax.ppermute(x_hat, "vp", core_pairs)
         from_x = lax.ppermute(x_hat, "vp", x_pairs)
-        xh_a = lax.all_gather(x_hat[: BLK // 2], ("dp", "vp"), axis=0, tiled=True)
-        xh_b = lax.all_gather(x_hat[BLK // 2 :], ("dp", "vp"), axis=0, tiled=True)
-        n_near, st_near = forward_stats(x_hat, from_core, g, w_head)
+        xh_all = lax.all_gather(x_hat, ("dp", "vp"), axis=0, tiled=True)
+        n_near, st_near = forward_stats(FWD_GROUPS[0], x_hat, from_core, g, w_head)
         from_x_core = lax.ppermute(from_x, "vp", core_pairs)
-        n_far, st_far = forward_stats(from_x, from_x_core, g, w_head)
+        n_far, st_far = forward_stats(FWD_GROUPS[1], from_x, from_x_core, g, w_head)
 
         info = jnp.stack([t_sorted.astype(f32), jnp.full((BLK,), kept.astype(f32))])[None]
         near = lax.all_gather(jnp.concatenate([st_near, st_far, info]), "vp", axis=0)
@@ -519,10 +498,8 @@
         aux_all = jnp.stack([lse_all, w_all, t_all] + [none] * 5, axis=1)
 
         span = (kept_all + ALIGN - 1) // ALIGN * ALIGN
-        span_a = jnp.minimum(span, BLK // 2)
-        ends = jnp.cumsum(jnp.concatenate([span_a, span - span_a]))
+        ends = jnp.cumsum(span)
         offs = jnp.concatenate([jnp.zeros((1,), i32), ends])
-        count = dp_count * vp_count
         nt_all = ((ends[-1:] + DW_TOK - 1) // DW_TOK).astype(i32)
 
         first = dp * vp_count
@@ -546,36 +523,42 @@
         loss_part = weight * jnp.sum(jnp.where(idx < kept, lse_own, 0.0)) - jnp.sum(t_part)
         parts = jnp.concatenate([d_scale.reshape(6, 128), jnp.full((2, 128), loss_part, f32)])
 
-        half, quarter = vocab // 2, vocab // 4
         y_pairs = [(d, d ^ 1) for d in range(dp_count)]
         z_pairs = [(d, d ^ 2) for d in range(dp_count)]
-
-        def jobs_of(widths, base, where, pairs):
-            starts = [sum(widths[:c]) for c in range(len(widths))]
-            return [(n, base + where * quarter + c, base + (1 - where) * quarter + c, pairs) for n, c in zip(widths, starts)]
-
-        y_jobs = jobs_of(Y_WIDTHS, 0, dp % 2, y_pairs)
-        z_jobs = jobs_of(Z_WIDTHS, half, (dp // 2) % 2, z_pairs)
-        jobs = [job for pair in zip(y_jobs, z_jobs) for job in pair] + z_jobs[len(y_jobs) :]
-
-        width, col, other, pairs = jobs[0]
-        place = jnp.stack([col // width, vp * vocab + col]).astype(i32)
-        before = first_columns(0, offs[: count + 1], place, xh_a, aux_all, g, w_head, None)
-        n_all, auxc_all, chunk = first_columns(1, offs[count:], place, xh_b, aux_all, g, w_head, before)
-        moved = [(lax.ppermute(chunk, "dp", pairs), other)]
-        whole = None
-        for k, (width, col, other, pairs) in enumerate(jobs):
-            if k == 0:
-                own = (chunk, col)
-                continue
-            merges = [own] if k == 1 else [moved[k - LAG]] if k >= LAG else []
-            chunk, whole = weight_grad(width, col, vp * vocab + col, nt_all, n_all, auxc_all, w_head, whole, merges)
+        y_jobs, z_jobs, own_jobs, base = [], [], [], 0
+        for widths, jobs, pairs in ((Y_WIDTHS, y_jobs, y_pairs), (Z_WIDTHS, z_jobs, z_pairs), (OWN_WIDTHS, own_jobs, None)):
+            for n in dict.fromkeys(widths):
+                stride = n * widths.count(n)
+                jobs += [
+                    (n, base + n * c, stride if pairs is y_pairs else 0, stride if pairs is z_pairs else 0, pairs)
+                    for c in range(widths.count(n))
+                ]
+                base += stride * (2 if pairs else 1)
+        jobs = [job for pair in zip(y_jobs, z_jobs) for job in pair] + own_jobs
+        start, y_step, z_step, v_step = (
+            jnp.array([x for job in jobs for x in entries(job)], i32)
+            for entries in (
+                lambda j: (j[1] // j[0], j[1], j[1], j[1] + j[2] + j[3]),
+                lambda j: (j[2] // j[0], j[2], j[2], -j[2]),
+                lambda j: (j[3] // j[0], j[3], j[3], -j[3]),
+                lambda j: (0, vocab, 0, 0),
+            )
+        )
+        table = start + y_step * (dp % 2) + z_step * (dp // 2 % 2) + v_step * vp
+
+        n_all, auxc_all, chunk = first_columns(offs, table, xh_all, aux_all, g, w_head)
+        own, whole, moved = (chunk, 2), None, []
+        for k, (width, *_, pairs) in enumerate(jobs):
+            if k:
+                merges = [own] if k == 1 else [moved[k - LAG]] if k >= LAG else []
+                chunk, whole = weight_grad(k, width, table, nt_all, n_all, auxc_all, w_head, whole, merges)
             if k == len(jobs) - 1:
-                chunk, parts = lax.optimization_barrier((chunk, parts))
-            moved.append((lax.ppermute(chunk, "dp", pairs), other))
+                whole, parts = lax.optimization_barrier((whole, parts))
+            if pairs:
+                moved.append((lax.ppermute(chunk, "dp", pairs), 4 * k + 3))
         parts = jnp.sum(tiny_gather(parts, everyone, 1), axis=0)
-        for chunk, other in moved[-LAG:]:
-            whole = lax.dynamic_update_slice(whole, chunk, (0, other))
+        for chunk, at in moved[len(jobs) - LAG :]:
+            whole = lax.dynamic_update_slice(whole, chunk, (0, table[at]))
         return parts[6, 0], d_x[None], whole, parts[:6].reshape(DIM)
 
     return jax.shard_map(

time: 985 us -> 971 us (0.986)
  waiting for transfers between devices: 402 us -> 371 us
  local copies, waits for them, and re-layouts: 18.7 us -> 46.2 us
    dynamic_update_slice x4 -> x3, local copies, waits for them, and re-layouts: 8.41 us -> 39.3 us  [local_step(): whole = lax.dynamic_update_slice(whole, chunk, (0, table[at]))]
    all_gather x2 -> x1, waiting for transfers between devices: 236 us -> 213 us  [local_step(): xh_all = lax.all_gather(x_hat, ('dp', 'vp'), axis=0, tiled=True)]
    ppermute x11 -> x8, waiting for transfers between devices: 27 us -> 12.5 us  [local_step(): moved.append((lax.ppermute(chunk, 'dp', pairs), 4 * k + 3))]
    pallas_call x14 -> x11, Pallas kernels: 390 us -> 376 us  [the longest x8 253 us: weight_grad(): pl.pallas_call(functools.partial(dw_kernel, job, [at for _, at in merges]...]
  transfers between devices with their start and end apart: 17 -> 13, of which waited for: 6 -> 6; matrix products, arithmetic and copies ran while one was open for 3% -> 4% of each run, Pallas kernels for 37% -> 34%
where the time goes in v4:
time: 971 us; the launch traced here: 964 us
  Pallas kernels  455 us (47%)
  waiting for transfers between devices  371 us (38%)
  local copies, waits for them, and re-layouts  46.2 us (5%)
  blocking collectives  37.2 us (4%)
  between operations  25.9 us (3%)
  other arithmetic  14.5 us (1%)
  starting transfers between devices  11.8 us (1%)
    pallas_call x8, Pallas kernels, weight_grad(): pl.pallas_call(functools.partial(dw_kernel, job, [at for _, at in merges]...  253 us
    all_gather x1, waiting for transfers between devices, local_step(): xh_all = lax.all_gather(x_hat, ('dp', 'vp'), axis=0, tiled=True)  213 us
    reduce_scatter x1, waiting for transfers between devices, local_step(): d_normed = lax.psum_scatter(dn_part, 'vp', scatter_dimension=0, tiled=True)  112 us
    pallas_call x2, Pallas kernels, forward_stats(): pl.pallas_call(functools.partial(fwd_kernel, group), grid=(vocab // FWD_C...  73.3 us
    pallas_call x1, Pallas kernels, first_columns(): pl.pallas_call(first_kernel, grid_spec=pltpu.PrefetchScalarGridSpec(num_s...  49.2 us
    pallas_call x1, Pallas kernels, backward_dn(): pl.pallas_call(dn_kernel, grid_spec=pltpu.PrefetchScalarGridSpec(num_scal...  40.7 us
    dynamic_update_slice x3, local copies, waits for them, and re-layouts, local_step(): whole = lax.dynamic_update_slice(whole, chunk, (0, table[at]))  39.3 us
    pallas_call x1, Pallas kernels, tiny_gather(): pl.pallas_call(functools.partial(tiny_gather_kernel, dp_count, vp_count),...  38.2 us
  transfers between devices with their start and end apart: 13, of which 6 were waited for; matrix products, arithmetic and copies ran while one was open for 4% of the time, Pallas kernels for 34%

profile of v4, /device:TPU:0, one launch (start us, length us, event | category | flops | bytes accessed | tf_op | source)
XLA Modules:
  0.0 963.7 jit_solution(6521210690664699005)
XLA Ops:
  8.1 1.4 reduce_sum.112
  9.4 0.8 select_reduce_fusion.1
  10.3 1.3 compare_select_fusion.3
  11.6 0.7 multiply_reduce_fusion.2
  12.3 1.1 copy-done.2
  13.6 3.0 collective-permute-start.1
  18.7 32.5 %collective-permute-done.1.xa = f32[512,768]{1,0:T(8,128)} collective-permute-done((f32[512,768]{1,0:T(8,128)S(1)}, f32[512,768]{1,0:T(8,128)}, u32[]{:S(2)}, u32[]{:S(2)}) %collective-permute-start.1) | collective-permute-done | bytes 1572896 | tf_op jit(solution)/shard_map/ppermute | solution.py:476
  51.2 37.0 %fwd_stats.2 = (bf16[1024,768]{1,0:T(8,128)(2,1)}, f32[2,2,512]{2,1,0:T(2,128)}) custom-call(f32[512,768]{1,0:T(8,128)} %copy-done.5, f32[512,768]{1,0:T(8,128)} %collective-permute-done.xb, f32[1,768]{1,0:T(1,128)} %reshape.246.g_ref, bf16[768,16384]{1,0:T(8,128)(2,1)} %w_ref.23), custom_call_target="tpu_custom_call" | custom-call | flops 25769803776 | bytes 33030144 | tf_op jit(solution)/shard_map/fwd_stats/pallas_call | solution.py:135
  88.2 36.3 %fwd_stats.3 = (bf16[1024,768]{1,0:T(8,128)(2,1)}, f32[2,2,512]{2,1,0:T(2,128)}) custom-call(f32[512,768]{1,0:T(8,128)} %collective-permute-done.1.xa, f32[512,768]{1,0:T(8,128)} %collective-permute-done.2.xb, f32[1,768]{1,0:T(1,128)} %reshape.246.g_ref, bf16[768,16384]{1,0:T(8,128)(2,1)} %w_ref.23), custom_call_target="tpu_custom_call" | custom-call | flops 25769803776 | bytes 33030144 | tf_op jit(solution)/shard_map/fwd_stats/pallas_call | solution.py:135
  124.5 0.7 pad_maximum_fusion.2
  125.2 5.5 all-gather
  131.0 31.7 %all_gather.14 = f32[32,3,512]{2,1,0:T(4,128)S(1)} all-gather(f32[4,3,512]{2,1,0:T(4,128)S(1)} %pad_maximum_fusion.1), channel_id=1, replica_groups=mesh['dp'=8,'vp'=4] {'dp'}, dimensions={0}, use_global_device_ids=true | all-gather | bytes 221184 | tf_op jit(solution)/shard_map/all_gather | solution.py:490
  162.8 1.8 fusion.16
  164.6 0.7 fusion.18
  166.9 0.6 bitcast_subtract_fusion.offs_ref
  167.7 0.7 dynamic-slice_reduce_fusion.kept_ref
  169.1 0.7 constant_dynamic-slice_fusion.aux_ref
  169.8 40.7 %backward_dn.1 = (f32[2048,768]{1,0:T(8,128)}, f32[8,128]{1,0:T(8,128)}) custom-call(s32[4]{0:T(128)} %bitcast_subtract_fusion.offs_ref, s32[4]{0:T(128)} %copy-done.17, s32[4]{0:T(128)} %dynamic-slice_reduce_fusion.kept_ref, s32[4]{0:T(128)} %iota_xor_fusion.mine_ref, s32[1]{0:T(128)} %bitcast.34.nt_ref, s32[1]{0:T(128)} %bitcast.35.col_ref, ...), custom_call_target="tpu_custom_call" | custom-call | flops 103079215104 | bytes 34603008 | tf_op jit(solution)/shard_map/backward_dn/pallas_call | solution.py:218
  211.3 0.6 fusion.21
  218.8 1.2 select_reduce_fusion.2
  220.7 0.6 reduce_sum.120
  222.6 112.0 %reduce-scatter.2.cloned.1.call-done = f32[512,768]{1,0:T(8,128)} async-done(((f32[2048,768]{1,0:T(8,128)}), f32[512,768]{1,0:T(8,128)}) %reduce-scatter.2.cloned.1.call-update) | async-done | bytes 1572880 | tf_op jit(solution)/shard_map/reduce_scatter | solution.py:515
  334.6 2.0 multiply_reduce_fusion
  336.6 0.6 concatenate.15.x_ref
  337.2 1.8 fusion
  339.0 213.4 %all-gather.3.cloned.1.call-done = f32[16384,768]{1,0:T(8,128)} async-done(((f32[512,768]{1,0:T(8,128)}), f32[16384,768]{1,0:T(8,128)}) %all-gather.3.cloned.1.call-update) | async-done | bytes 50331664 | tf_op jit(solution)/shard_map/all_gather | solution.py:477
  552.5 49.2 %first_columns.1 = (bf16[16384,768]{1,0:T(8,128)(2,1)}, f32[16384,128]{1,0:T(8,128)}, f32[768,1024]{1,0:T(8,128)}) custom-call(s32[33]{0:T(128)} %pad_add_fusion.offs_ref, s32[36]{0:T(128)} %copy-done.7, f32[32,512,768]{2,1,0:T(8,128)} %bitcast.110, f32[32,8,512]{2,1,0:T(8,128)} %copy-done.6, f32[1,768]{1,0:T(1,128)} %reshape.246.g_ref, ...), custom_call_target="tpu_custom_call" | custom-call | flops 25769803776 | bytes 75497472 | tf_op jit(solution)/shard_map/first_columns/pallas_call | solution.py:330
  601.7 1.5 collective-permute-start.3
  603.2 33.5 %weight_grad.8 = (f32[768,1024]{1,0:T(8,128)}, f32[768,16384]{1,0:T(8,128)}) custom-call(s32[36]{0:T(128)} %copy-done.7, s32[1]{0:T(128)S(6)} %select_n.101.nt_ref, bf16[16384,768]{1,0:T(8,128)(2,1)} %get-tuple-element.32.n_hbm, f32[16384,128]{1,0:T(8,128)} %get-tuple-element.33.aux_hbm, bf16[768,16384]{1,0:T(8,128)(2,1)} %w_ref.23, ...), custom_call_target="tpu_custom_call" | custom-call | flops 25769803776 | bytes 31457280 | tf_op jit(solution)/shard_map/weight_grad/pallas_call | solution.py:423
  636.7 32.5 %weight_grad.9 = (f32[768,1024]{1,0:T(8,128)}, f32[768,16384]{1,0:T(8,128)}) custom-call(s32[36]{0:T(128)} %copy-done.7, s32[1]{0:T(128)S(6)} %select_n.101.nt_ref, bf16[16384,768]{1,0:T(8,128)(2,1)} %get-tuple-element.32.n_hbm, f32[16384,128]{1,0:T(8,128)} %get-tuple-element.33.aux_hbm, bf16[768,16384]{1,0:T(8,128)(2,1)} %w_ref.23, ...), custom_call_target="tpu_custom_call", output_to_operand_aliasing={{1}: (5, {})} | custom-call | flops 25769803776 | bytes 31457280 | tf_op jit(solution)/shard_map/weight_grad/pallas_call | solution.py:423
  669.3 32.5 %weight_grad.10 = (f32[768,1024]{1,0:T(8,128)}, f32[768,16384]{1,0:T(8,128)}) custom-call(s32[36]{0:T(128)} %copy-done.7, s32[1]{0:T(128)S(6)} %select_n.101.nt_ref, bf16[16384,768]{1,0:T(8,128)(2,1)} %get-tuple-element.32.n_hbm, f32[16384,128]{1,0:T(8,128)} %get-tuple-element.33.aux_hbm, ...), custom_call_target="tpu_custom_call", output_to_operand_aliasing={{1}: (5, {})} | custom-call | flops 25769803776 | bytes 31457280 | tf_op jit(solution)/shard_map/weight_grad/pallas_call | solution.py:423
  701.8 2.1 collective-permute-start.6
  704.4 33.6 %weight_grad.11 = (f32[768,1024]{1,0:T(8,128)}, f32[768,16384]{1,0:T(8,128)}) custom-call(s32[36]{0:T(128)} %copy-done.7, s32[1]{0:T(128)S(6)} %select_n.101.nt_ref, bf16[16384,768]{1,0:T(8,128)(2,1)} %get-tuple-element.32.n_hbm, f32[16384,128]{1,0:T(8,128)} %get-tuple-element.33.aux_hbm, ...), custom_call_target="tpu_custom_call", output_to_operand_aliasing={{1}: (5, {})} | custom-call | flops 25769803776 | bytes 31457280 | tf_op jit(solution)/shard_map/weight_grad/pallas_call | solution.py:423
  738.0 1.5 collective-permute-start.7
  739.5 1.1 collective-permute-done.4.rest_1_
  740.6 33.5 %weight_grad.12 = (f32[768,1024]{1,0:T(8,128)}, f32[768,16384]{1,0:T(8,128)}) custom-call(s32[36]{0:T(128)} %copy-done.7, s32[1]{0:T(128)S(6)} %select_n.101.nt_ref, bf16[16384,768]{1,0:T(8,128)(2,1)} %get-tuple-element.32.n_hbm, f32[16384,128]{1,0:T(8,128)} %get-tuple-element.33.aux_hbm, ...), custom_call_target="tpu_custom_call", output_to_operand_aliasing={{1}: (5, {})} | custom-call | flops 25769803776 | bytes 31457280 | tf_op jit(solution)/shard_map/weight_grad/pallas_call | solution.py:423
  774.1 1.0 collective-permute-done.5.rest_1_
  775.2 33.6 %weight_grad.13 = (f32[768,1024]{1,0:T(8,128)}, f32[768,16384]{1,0:T(8,128)}) custom-call(s32[36]{0:T(128)} %copy-done.7, s32[1]{0:T(128)S(6)} %select_n.101.nt_ref, bf16[16384,768]{1,0:T(8,128)(2,1)} %get-tuple-element.32.n_hbm, f32[16384,128]{1,0:T(8,128)} %get-tuple-element.33.aux_hbm, ...), custom_call_target="tpu_custom_call", output_to_operand_aliasing={{1}: (5, {})} | custom-call | flops 25769803776 | bytes 31457280 | tf_op jit(solution)/shard_map/weight_grad/pallas_call | solution.py:423
  808.7 0.6 collective-permute-start.9
  809.4 20.8 %weight_grad.14 = (f32[768,512]{1,0:T(8,128)}, f32[768,16384]{1,0:T(8,128)}) custom-call(s32[36]{0:T(128)} %copy-done.7, s32[1]{0:T(128)S(6)} %select_n.101.nt_ref, bf16[16384,768]{1,0:T(8,128)(2,1)} %get-tuple-element.32.n_hbm, f32[16384,128]{1,0:T(8,128)} %get-tuple-element.33.aux_hbm, bf16[768,16384]{1,0:T(8,128)(2,1)} %w_ref.23, ...), custom_call_target="tpu_custom_call", output_to_operand_aliasing={{1}: (5, {})} | custom-call | flops 12884901888 | bytes 28311552 | tf_op jit(solution)/shard_map/weight_grad/pallas_call | solution.py:423
  830.2 2.0 collective-permute-start.10
  832.2 10.4 %collective-permute-done.7.rest_1_ = f32[768,1024]{1,0:T(8,128)} collective-permute-done((f32[768,1024]{1,0:T(8,128)}, f32[768,1024]{1,0:T(8,128)}, u32[]{:S(2)}, u32[]{:S(2)}) %collective-permute-start.7) | collective-permute-done | bytes 3145760 | tf_op jit(solution)/shard_map/ppermute | solution.py:558
  842.6 33.5 %weight_grad.15 = (f32[768,1024]{1,0:T(8,128)}, f32[768,16384]{1,0:T(8,128)}) custom-call(s32[36]{0:T(128)} %copy-done.7, s32[1]{0:T(128)S(6)} %select_n.101.nt_ref, bf16[16384,768]{1,0:T(8,128)(2,1)} %get-tuple-element.32.n_hbm, f32[16384,128]{1,0:T(8,128)} %get-tuple-element.33.aux_hbm, ...), custom_call_target="tpu_custom_call", output_to_operand_aliasing={{1}: (5, {})} | custom-call | flops 25769803776 | bytes 31457280 | tf_op jit(solution)/shard_map/weight_grad/pallas_call | solution.py:423
  876.1 38.2 %tiny_gather.1 = f32[32,8,128]{2,1,0:T(8,128)} custom-call(f32[8,128]{1,0:T(8,128)} %concatenate.15.x_ref), custom_call_target="tpu_custom_call" | custom-call | tf_op jit(solution)/shard_map/tiny_gather/pallas_call | solution.py:65
  914.4 0.9 reduce_sum.121
  915.8 15.6 %dynamic_update_slice.9 = f32[768,16384]{1,0:T(8,128)} dynamic-update-slice(f32[768,16384]{1,0:T(8,128)} %get-tuple-element.52, f32[768,1024]{1,0:T(8,128)} %collective-permute-done.8, s32[]{:T(128)} %constant.115.clone.1, s32[]{:T(128)S(6)} %select_n.110) | dynamic-update-slice | bytes 6291460 | tf_op jit(solution)/shard_map/dynamic_update_slice | solution.py:561
  931.5 15.6 %dynamic_update_slice.10 = f32[768,16384]{1,0:T(8,128)} dynamic-update-slice(f32[768,16384]{1,0:T(8,128)} %dynamic_update_slice.9, f32[768,1024]{1,0:T(8,128)} %collective-permute-done.9, s32[]{:T(128)} %constant.115.clone.1, s32[]{:T(128)S(6)} %select_n.111) | dynamic-update-slice | bytes 6291460 | tf_op jit(solution)/shard_map/dynamic_update_slice | solution.py:561
  947.7 8.1 dynamic_update_slice.11
  (98 shorter events, 6.8 us)
Async XLA Ops:
  8.0 3.6 copy-start
  8.0 326.5 %reduce-scatter.2.cloned.1.call-start = ((), (), s32[]{:S(2)}) async-start(), calls=%async_computation.2 | async-start | bytes 7864320 | tf_op jit(solution)/shard_map/reduce_scatter | solution.py:515
  11.6 5.7 copy-start.12
  12.3 1.1 copy-start.2
  12.3 1.3 copy-start.8
  13.4 3.9 copy-start.16
  13.5 4.1 copy-start.10
  13.6 37.5 %copy-start.5 = (f32[512,768]{1,0:T(8,128)}, f32[512,768]{1,0:T(8,128)S(1)}, u32[]{:S(2)}) copy-start(f32[512,768]{1,0:T(8,128)S(1)} %broadcast_multiply_fusion.xa) | copy-start | bytes 4718596
  13.6 37.5 %collective-permute-start.1 = (f32[512,768]{1,0:T(8,128)S(1)}, f32[512,768]{1,0:T(8,128)}, u32[]{:S(2)}, u32[]{:S(2)}) collective-permute-start(f32[512,768]{1,0:T(8,128)S(1)} %broadcast_multiply_fusion.xa), channel_id=1, source_target_pairs={{0,2},{1,3},{2,0},{3,1},{4,6},{5,7},{6,4},{7,5},{8,10},{9,11},{10,... | collective-permute-start | bytes 4718600 | tf_op jit(solution)/shard_map/ppermute | solution.py:476
  16.7 34.5 %collective-permute-start = (f32[512,768]{1,0:T(8,128)S(1)}, f32[512,768]{1,0:T(8,128)}, u32[]{:S(2)}, u32[]{:S(2)}) collective-permute-start(f32[512,768]{1,0:T(8,128)S(1)} %broadcast_multiply_fusion.xa), channel_id=1, source_target_pairs={{0,1},{1,0},{2,3},{3,2},{4,5},{5,4},{6,7},{7,6},{8,9},{9,8},{10,11... | collective-permute-start | bytes 4718600 | tf_op jit(solution)/shard_map/ppermute | solution.py:475
  51.2 37.0 %collective-permute-start.2 = (f32[512,768]{1,0:T(8,128)}, f32[512,768]{1,0:T(8,128)}, u32[]{:S(2)}, u32[]{:S(2)}) collective-permute-start(f32[512,768]{1,0:T(8,128)} %collective-permute-done.1.xa), channel_id=1, source_target_pairs={{0,1},{1,0},{2,3},{3,2},{4,5},{5,4},{6,7},{7,6},{8,9},{9,8},{10,11... | collective-permute-start | bytes 4718600 | tf_op jit(solution)/shard_map/ppermute | solution.py:479
  88.2 36.3 %copy-start.14 = (f32[2,2,512]{2,1,0:T(2,128)S(1)}, f32[2,2,512]{2,1,0:T(2,128)}, u32[]{:S(2)}) copy-start(f32[2,2,512]{2,1,0:T(2,128)} %get-tuple-element.30) | copy-start | bytes 24580
  165.3 4.5 copy-start.17
  169.1 41.4 %copy-start.6 = (f32[32,8,512]{2,1,0:T(8,128)}, f32[32,8,512]{2,1,0:T(8,128)S(1)}, u32[]{:S(2)}) copy-start(f32[32,8,512]{2,1,0:T(8,128)S(1)} %stack.50.aux_ref) | copy-start | bytes 1572868
  210.5 0.7 copy-start.18
  210.5 0.7 copy-start.19
  210.5 0.7 copy-start.20
  210.5 0.7 copy-start.21
  210.5 10.2 %copy-start.15 = (f32[8,128]{1,0:T(8,128)S(1)}, f32[8,128]{1,0:T(8,128)}, u32[]{:S(2)}) copy-start(f32[8,128]{1,0:T(8,128)} %get-tuple-element.50) | copy-start | bytes 12292
  210.5 124.0 %copy-start.3 = (f32[512,768]{1,0:T(8,128)S(1)}, f32[512,768]{1,0:T(8,128)}, u32[]{:S(2)}) copy-start(f32[512,768]{1,0:T(8,128)} %copy-done.2) | copy-start | bytes 4718596
  210.6 124.0 %copy-start.9 = (f32[512]{0:T(512)S(1)}, f32[512]{0:T(512)}, u32[]{:S(2)}) copy-start(f32[512]{0:T(512)} %copy-done.8) | copy-start | bytes 6148
  210.6 124.0 %copy-start.11 = (f32[768]{0:T(1024)S(1)}, f32[768]{0:T(1024)}, u32[]{:S(2)}) copy-start(f32[768]{0:T(1024)} %param.12) | copy-start | bytes 9220
  210.6 341.9 %all-gather.3.cloned.1.call-start = ((), (), s32[]{:S(2)}) async-start(), calls=%async_computation.1 | async-start | bytes 51904512 | tf_op jit(solution)/shard_map/all_gather | solution.py:477
  211.2 125.3 %copy-start.7 = (s32[36]{0:T(128)}, s32[36]{0:T(128)S(1)}, u32[]{:S(2)}) copy-start(s32[36]{0:T(128)S(1)} %fusion.13.table_ref) | copy-start | bytes 436
  222.6 114.6 %copy-start.13 = (s32[1,512]{1,0:T(1,128)S(1)}, s32[1,512]{1,0:T(1,128)}, u32[]{:S(2)}) copy-start(s32[1,512]{1,0:T(1,128)} %copy-done.12) | copy-start | bytes 6148
  334.6 2.6 copy-start.4
  601.7 102.8 %collective-permute-start.3 = (f32[768,1024]{1,0:T(8,128)}, f32[768,1024]{1,0:T(8,128)}, u32[]{:S(2)}, u32[]{:S(2)}) collective-permute-start(f32[768,1024]{1,0:T(8,128)} %get-tuple-element.34.rest_0_), channel_id=1, source_target_pairs={{0,4},{4,0},{8,12},{12,8},{16,20},{20,16},{24,28},{28,24},{1,5},{5... | collective-permute-start | bytes 9437192 | tf_op jit(solution)/shard_map/ppermute | solution.py:558
  669.3 71.4 %collective-permute-start.4 = (f32[768,1024]{1,0:T(8,128)}, f32[768,1024]{1,0:T(8,128)}, u32[]{:S(2)}, u32[]{:S(2)}) collective-permute-start(f32[768,1024]{1,0:T(8,128)} %get-tuple-element.39), channel_id=1, source_target_pairs={{0,8},{4,12},{8,0},{12,4},{16,24},{20,28},{24,16},{28,20},{1,9},{5... | collective-permute-start | bytes 9437192 | tf_op jit(solution)/shard_map/ppermute | solution.py:558
  701.8 107.6 %collective-permute-start.6 = (f32[768,1024]{1,0:T(8,128)}, f32[768,1024]{1,0:T(8,128)}, u32[]{:S(2)}, u32[]{:S(2)}) collective-permute-start(f32[768,1024]{1,0:T(8,128)} %get-tuple-element.43), channel_id=1, source_target_pairs={{0,8},{4,12},{8,0},{12,4},{16,24},{20,28},{24,16},{28,20},{1,9},{5... | collective-permute-start | bytes 9437192 | tf_op jit(solution)/shard_map/ppermute | solution.py:558
  703.9 71.3 %collective-permute-start.5 = (f32[768,1024]{1,0:T(8,128)}, f32[768,1024]{1,0:T(8,128)}, u32[]{:S(2)}, u32[]{:S(2)}) collective-permute-start(f32[768,1024]{1,0:T(8,128)} %get-tuple-element.41), channel_id=1, source_target_pairs={{0,4},{4,0},{8,12},{12,8},{16,20},{20,16},{24,28},{28,24},{1,5},{5... | collective-permute-start | bytes 9437192 | tf_op jit(solution)/shard_map/ppermute | solution.py:558
  738.0 104.6 %collective-permute-start.7 = (f32[768,1024]{1,0:T(8,128)}, f32[768,1024]{1,0:T(8,128)}, u32[]{:S(2)}, u32[]{:S(2)}) collective-permute-start(f32[768,1024]{1,0:T(8,128)} %get-tuple-element.45), channel_id=1, source_target_pairs={{0,4},{4,0},{8,12},{12,8},{16,20},{20,16},{24,28},{28,24},{1,5},{5... | collective-permute-start | bytes 9437192 | tf_op jit(solution)/shard_map/ppermute | solution.py:558
  808.7 122.7 %collective-permute-start.9 = (f32[768,1024]{1,0:T(8,128)}, f32[768,1024]{1,0:T(8,128)}, u32[]{:S(2)}, u32[]{:S(2)}) collective-permute-start(f32[768,1024]{1,0:T(8,128)} %get-tuple-element.54), channel_id=1, source_target_pairs={{0,4},{4,0},{8,12},{12,8},{16,20},{20,16},{24,28},{28,24},{1,5},{5... | collective-permute-start | bytes 9437192 | tf_op jit(solution)/shard_map/ppermute | solution.py:558
  809.4 106.5 %collective-permute-start.8 = (f32[768,1024]{1,0:T(8,128)}, f32[768,1024]{1,0:T(8,128)}, u32[]{:S(2)}, u32[]{:S(2)}) collective-permute-start(f32[768,1024]{1,0:T(8,128)} %get-tuple-element.53), channel_id=1, source_target_pairs={{0,8},{4,12},{8,0},{12,4},{16,24},{20,28},{24,16},{28,20},{1,9},{5... | collective-permute-start | bytes 9437192 | tf_op jit(solution)/shard_map/ppermute | solution.py:558
  830.2 117.5 %collective-permute-start.10 = (f32[768,512]{1,0:T(8,128)}, f32[768,512]{1,0:T(8,128)S(1)}, u32[]{:S(2)}, u32[]{:S(2)}) collective-permute-start(f32[768,512]{1,0:T(8,128)} %get-tuple-element.55), channel_id=1, source_target_pairs={{0,8},{4,12},{8,0},{12,4},{16,24},{20,28},{24,16},{28,20},{1,9},{5... | collective-permute-start | bytes 4718600 | tf_op jit(solution)/shard_map/ppermute | solution.py:558
  947.1 8.7 copy-start.1
Sparse Core Ops, SparseCore 0:
  210.6 123.9 reduce-scatter.1
Sparse Core Ops, SparseCore 1:
  213.9 338.4 all-gather.2

commit v5 on v4

--- a/solution.py
+++ b/solution.py
@@ -13,7 +13,7 @@
 DIM = 768
 ALIGN = 16
 FWD_COLS = 2048
-FWD_GROUPS = (256, 1024)
+FWD_GROUP = 1024
 DN_COLS = 2048
 DW_TOK = 1024
 DW_GROUP = 1024
@@ -450,6 +450,41 @@
     )(table, ntiles, n_all, aux_all, w, *held)
 
 
+def finish_kernel(places, table_ref, whole_hbm, *rest):
+    count = len(places)
+    chunks, out_hbm, bufs, sems = rest[:count], rest[count], rest[count + 1 : -1], rest[-1]
+    moves_in = [pltpu.make_async_copy(chunk, buf, sems.at[k, 0]) for k, (chunk, buf) in enumerate(zip(chunks, bufs))]
+    for copy in moves_in:
+        copy.start()
+    moves_out = []
+    for k, (at, buf) in enumerate(zip(places, bufs)):
+        cols = pl.ds(pl.multiple_of(table_ref[at], 128), buf.shape[1])
+        moves_out.append(pltpu.make_async_copy(buf, out_hbm.at[:, cols], sems.at[k, 1]))
+        moves_in[k].wait()
+        moves_out[k].start()
+    for copy in moves_out:
+        copy.wait()
+
+
+def finish(table, whole, chunks):
+    anywhere = pl.BlockSpec(memory_space=pl.ANY)
+    arrays = [chunk for chunk, _ in chunks]
+    return pl.pallas_call(
+        functools.partial(finish_kernel, [at for _, at in chunks]),
+        grid_spec=pltpu.PrefetchScalarGridSpec(
+            num_scalar_prefetch=1,
+            grid=(1,),
+            in_specs=[anywhere] * (len(chunks) + 1),
+            out_specs=anywhere,
+            scratch_shapes=[pltpu.VMEM(a.shape, f32) for a in arrays] + [pltpu.SemaphoreType.DMA((len(chunks), 2))],
+        ),
+        out_shape=jax.ShapeDtypeStruct(whole.shape, f32),
+        input_output_aliases={1: 0},
+        cost_estimate=pl.CostEstimate(flops=0, bytes_accessed=sum(8 * a.size for a in arrays), transcendentals=0),
+        name="finish",
+    )(table, whole, *arrays)
+
+
 def solution(mesh):
     dp_count, vp_count = mesh.shape["dp"], mesh.shape["vp"]
     everyone = (dp_count, vp_count)
@@ -475,9 +510,9 @@
         from_core = lax.ppermute(x_hat, "vp", core_pairs)
         from_x = lax.ppermute(x_hat, "vp", x_pairs)
         xh_all = lax.all_gather(x_hat, ("dp", "vp"), axis=0, tiled=True)
-        n_near, st_near = forward_stats(FWD_GROUPS[0], x_hat, from_core, g, w_head)
+        n_near, st_near = forward_stats(FWD_GROUP, x_hat, from_core, g, w_head)
         from_x_core = lax.ppermute(from_x, "vp", core_pairs)
-        n_far, st_far = forward_stats(FWD_GROUPS[1], from_x, from_x_core, g, w_head)
+        n_far, st_far = forward_stats(FWD_GROUP, from_x, from_x_core, g, w_head)
 
         info = jnp.stack([t_sorted.astype(f32), jnp.full((BLK,), kept.astype(f32))])[None]
         near = lax.all_gather(jnp.concatenate([st_near, st_far, info]), "vp", axis=0)
@@ -498,31 +533,18 @@
         aux_all = jnp.stack([lse_all, w_all, t_all] + [none] * 5, axis=1)
 
         span = (kept_all + ALIGN - 1) // ALIGN * ALIGN
-        ends = jnp.cumsum(span)
-        offs = jnp.concatenate([jnp.zeros((1,), i32), ends])
-        nt_all = ((ends[-1:] + DW_TOK - 1) // DW_TOK).astype(i32)
+        blocks = dp_count * vp_count
+        before = lax.iota(i32, blocks)[None, :] < lax.iota(i32, blocks + 1)[:, None]
+        offs = jnp.sum(jnp.where(before, span[None, :], 0), axis=1)
+        nt_all = (offs[blocks:] + DW_TOK - 1) // DW_TOK
 
         first = dp * vp_count
         kept_row = lax.dynamic_slice(kept_all, (first,), (vp_count,))
         span_row = lax.dynamic_slice(span, (first,), (vp_count,))
         aux_row = lax.dynamic_slice(aux_all, (first, 0, 0), (vp_count, 8, BLK))
-        offs_row = jnp.cumsum(span_row) - span_row
+        offs_row = lax.dynamic_slice(offs, (first,), (vp_count,)) - lax.dynamic_slice(offs, (first,), (1,))
         nt_row = ((jnp.sum(span_row) + BLK - 1) // BLK).reshape(1)
         mine = jnp.bitwise_xor(jnp.arange(vp_count, dtype=i32), vp)
-        dn_part, t_part = backward_dn(
-            offs_row, span_row, kept_row, mine, nt_row, (vp * vocab).reshape(1), n_near, n_far, aux_row, w_head
-        )
-        d_normed = lax.psum_scatter(dn_part, "vp", scatter_dimension=0, tiled=True)
-
-        d_scale = jnp.sum(d_normed * x_hat, axis=0)
-        e = d_normed * norm_scale
-        d_x = inv_rms * (e - x_hat * jnp.mean(e * x_hat, axis=-1, keepdims=True))
-        back = perm.astype(bf16).T
-        d_x = jnp.dot(back, d_x.astype(bf16), preferred_element_type=f32).astype(bf16)
-        lse_own = lax.dynamic_slice(lse_row, (vp, 0), (1, BLK))[0]
-        loss_part = weight * jnp.sum(jnp.where(idx < kept, lse_own, 0.0)) - jnp.sum(t_part)
-        parts = jnp.concatenate([d_scale.reshape(6, 128), jnp.full((2, 128), loss_part, f32)])
-
         y_pairs = [(d, d ^ 1) for d in range(dp_count)]
         z_pairs = [(d, d ^ 2) for d in range(dp_count)]
         y_jobs, z_jobs, own_jobs, base = [], [], [], 0
@@ -545,20 +567,36 @@
             )
         )
         table = start + y_step * (dp % 2) + z_step * (dp // 2 % 2) + v_step * vp
+        aux_row, offs, nt_all, table, aux_all = lax.optimization_barrier((aux_row, offs, nt_all, table, aux_all))
+
+        dn_part, t_part = backward_dn(
+            offs_row, span_row, kept_row, mine, nt_row, (vp * vocab).reshape(1), n_near, n_far, aux_row, w_head
+        )
+        d_normed = lax.psum_scatter(dn_part, "vp", scatter_dimension=0, tiled=True)
+
+        d_scale = jnp.sum(d_normed * x_hat, axis=0)
+        e = d_normed * norm_scale
+        d_x = inv_rms * (e - x_hat * jnp.mean(e * x_hat, axis=-1, keepdims=True))
+        back = perm.astype(bf16).T
+        d_x = jnp.dot(back, d_x.astype(bf16), preferred_element_type=f32).astype(bf16)
+        lse_own = lax.dynamic_slice(lse_row, (vp, 0), (1, BLK))[0]
+        loss_part = weight * jnp.sum(jnp.where(idx < kept, lse_own, 0.0)) - jnp.sum(t_part)
+        parts = jnp.concatenate([d_scale.reshape(6, 128), jnp.full((2, 128), loss_part, f32)])
 
         n_all, auxc_all, chunk = first_columns(offs, table, xh_all, aux_all, g, w_head)
         own, whole, moved = (chunk, 2), None, []
         for k, (width, *_, pairs) in enumerate(jobs):
             if k:
                 merges = [own] if k == 1 else [moved[k - LAG]] if k >= LAG else []
+                if k == len(jobs) - 1:
+                    merges.append(moved[k - LAG + 1])
                 chunk, whole = weight_grad(k, width, table, nt_all, n_all, auxc_all, w_head, whole, merges)
             if k == len(jobs) - 1:
                 whole, parts = lax.optimization_barrier((whole, parts))
             if pairs:
                 moved.append((lax.ppermute(chunk, "dp", pairs), 4 * k + 3))
         parts = jnp.sum(tiny_gather(parts, everyone, 1), axis=0)
-        for chunk, at in moved[len(jobs) - LAG :]:
-            whole = lax.dynamic_update_slice(whole, chunk, (0, table[at]))
+        whole = finish(table, whole, moved[len(jobs) - LAG + 1 :])
         return parts[6, 0], d_x[None], whole, parts[:6].reshape(DIM)
 
     return jax.shard_map(

time: 971 us -> 944 us (0.972)
  waiting for transfers between devices: 371 us -> 412 us
  local copies, waits for them, and re-layouts: 46.2 us -> 7.31 us
  Pallas kernels: 455 us -> 432 us
    dynamic_update_slice x3 -> x0, local copies, waits for them, and re-layouts: 39.3 us -> none  [local_step(): whole = lax.dynamic_update_slice(whole, chunk, (0, table[at]))]
    ppermute x8, waiting for transfers between devices: 12.5 us -> 46.2 us  [local_step(): moved.append((lax.ppermute(chunk, 'dp', pairs), 4 * k + 3))]
    pallas_call x1, Pallas kernels: 38.2 us -> 9.5 us  [tiny_gather(): pl.pallas_call(functools.partial(tiny_gather_kernel, dp_count, vp_count),...]
  transfers between devices with their start and end apart: 13 -> 13, of which waited for: 6 -> 7; matrix products, arithmetic and copies ran while one was open for 4% -> 1% of each run, Pallas kernels for 34% -> 32%
where the time goes in v5:
time: 944 us; the launch traced here: 938 us
  Pallas kernels  432 us (46%)
  waiting for transfers between devices  412 us (44%)
  blocking collectives  37.3 us (4%)
  between operations  20.4 us (2%)
  other arithmetic  14.9 us (2%)
  starting transfers between devices  10.9 us (1%)
    pallas_call x8, Pallas kernels, weight_grad(): pl.pallas_call(functools.partial(dw_kernel, job, [at for _, at in merges]...  256 us
    all_gather x1, waiting for transfers between devices, local_step(): xh_all = lax.all_gather(x_hat, ('dp', 'vp'), axis=0, tiled=True)  213 us
    reduce_scatter x1, waiting for transfers between devices, local_step(): d_normed = lax.psum_scatter(dn_part, 'vp', scatter_dimension=0, tiled=True)  120 us
    pallas_call x2, Pallas kernels, forward_stats(): pl.pallas_call(functools.partial(fwd_kernel, group), grid=(vocab // FWD_C...  72.7 us
    pallas_call x1, Pallas kernels, first_columns(): pl.pallas_call(first_kernel, grid_spec=pltpu.PrefetchScalarGridSpec(num_s...  49.2 us
    ppermute x8, waiting for transfers between devices, local_step(): moved.append((lax.ppermute(chunk, 'dp', pairs), 4 * k + 3))  46.2 us
    pallas_call x1, Pallas kernels, backward_dn(): pl.pallas_call(dn_kernel, grid_spec=pltpu.PrefetchScalarGridSpec(num_scal...  40.7 us
    ppermute x1, waiting for transfers between devices, local_step(): from_x = lax.ppermute(x_hat, 'vp', x_pairs)  31.8 us
  transfers between devices with their start and end apart: 13, of which 7 were waited for; matrix products, arithmetic and copies ran while one was open for 1% of the time, Pallas kernels for 32%

profile of v5, /device:TPU:0, one launch (start us, length us, event | category | flops | bytes accessed | tf_op | source)
XLA Modules:
  0.0 937.8 jit_solution(15498057249881061411)
XLA Ops:
  8.1 1.4 reduce_sum.121
  9.4 0.8 select_reduce_fusion.1
  10.3 1.3 compare_select_fusion.3
  11.6 0.7 multiply_reduce_fusion.2
  12.3 1.1 copy-done.2
  13.7 3.0 collective-permute-start.1
  17.6 0.6 reshape.173.g_ref
  19.4 31.8 %collective-permute-done.1.xa = f32[512,768]{1,0:T(8,128)} collective-permute-done((f32[512,768]{1,0:T(8,128)S(1)}, f32[512,768]{1,0:T(8,128)}, u32[]{:S(2)}, u32[]{:S(2)}) %collective-permute-start.1) | collective-permute-done | bytes 1572896 | tf_op jit(solution)/shard_map/ppermute | solution.py:511
  51.2 36.3 %fwd_stats.2 = (bf16[1024,768]{1,0:T(8,128)(2,1)}, f32[2,2,512]{2,1,0:T(2,128)}) custom-call(f32[512,768]{1,0:T(8,128)} %copy-done.5, f32[512,768]{1,0:T(8,128)} %collective-permute-done.xb, f32[1,768]{1,0:T(1,128)} %reshape.173.g_ref, bf16[768,16384]{1,0:T(8,128)(2,1)} %w_ref.23), custom_call_target="tpu_custom_call" | custom-call | flops 25769803776 | bytes 33030144 | tf_op jit(solution)/shard_map/fwd_stats/pallas_call | solution.py:135
  87.6 36.3 %fwd_stats.3 = (bf16[1024,768]{1,0:T(8,128)(2,1)}, f32[2,2,512]{2,1,0:T(2,128)}) custom-call(f32[512,768]{1,0:T(8,128)} %collective-permute-done.1.xa, f32[512,768]{1,0:T(8,128)} %collective-permute-done.2.xb, f32[1,768]{1,0:T(1,128)} %reshape.173.g_ref, bf16[768,16384]{1,0:T(8,128)(2,1)} %w_ref.23), custom_call_target="tpu_custom_call" | custom-call | flops 25769803776 | bytes 33030144 | tf_op jit(solution)/shard_map/fwd_stats/pallas_call | solution.py:135
  123.9 0.7 pad_maximum_fusion.2
  124.6 5.5 all-gather
  130.4 31.8 %all_gather.14 = f32[32,3,512]{2,1,0:T(4,128)S(1)} all-gather(f32[4,3,512]{2,1,0:T(4,128)S(1)} %pad_maximum_fusion.1), channel_id=1, replica_groups=mesh['dp'=8,'vp'=4] {'dp'}, dimensions={0}, use_global_device_ids=true | all-gather | bytes 221184 | tf_op jit(solution)/shard_map/all_gather | solution.py:525
  162.2 1.2 fusion.15
  163.5 1.2 fusion.17
  167.4 1.2 dynamic-slice_subtract_fusion.offs_ref
  168.9 0.7 dynamic-slice_reduce_fusion.kept_ref
  170.3 0.7 constant_dynamic-slice_fusion.aux_ref
  170.9 40.7 %backward_dn.1 = (f32[2048,768]{1,0:T(8,128)}, f32[8,128]{1,0:T(8,128)}) custom-call(s32[4]{0:T(128)} %dynamic-slice_subtract_fusion.offs_ref, s32[4]{0:T(128)} %get-tuple-element.71.span_ref, s32[4]{0:T(128)} %dynamic-slice_reduce_fusion.kept_ref, s32[4]{0:T(128)} %iota_xor_fusion.mine_ref, s32[1]{0:T(128)} %bitcast.32.nt_ref, s32[1]{0:T(128)} %bitcast.33.col_ref, ...), custom_call_target="tpu_custom_call" | custom-call | flops 103079215104 | bytes 34603008 | tf_op jit(solution)/shard_map/backward_dn/pallas_call | solution.py:218
  212.3 1.2 select_reduce_fusion.3
  214.2 0.6 reduce_sum.130
  215.5 120.2 %reduce-scatter.2.cloned.1.call-done = f32[512,768]{1,0:T(8,128)} async-done(((f32[2048,768]{1,0:T(8,128)}), f32[512,768]{1,0:T(8,128)}) %reduce-scatter.2.cloned.1.call-update) | async-done | bytes 1572880 | tf_op jit(solution)/shard_map/reduce_scatter | solution.py:575
  335.7 2.0 multiply_reduce_fusion
  337.7 0.6 concatenate.11.x_ref
  338.3 1.8 fusion
  340.1 213.5 %all-gather.3.cloned.1.call-done = f32[16384,768]{1,0:T(8,128)} async-done(((f32[512,768]{1,0:T(8,128)}), f32[16384,768]{1,0:T(8,128)}) %all-gather.3.cloned.1.call-update) | async-done | bytes 50331664 | tf_op jit(solution)/shard_map/all_gather | solution.py:512
  553.6 49.2 %first_columns.1 = (bf16[16384,768]{1,0:T(8,128)(2,1)}, f32[16384,128]{1,0:T(8,128)}, f32[768,1024]{1,0:T(8,128)}) custom-call(s32[33]{0:T(128)} %copy-done.15, s32[36]{0:T(128)} %fusion.13.table_ref, f32[32,512,768]{2,1,0:T(8,128)} %bitcast.93, f32[32,8,512]{2,1,0:T(8,128)} %copy-done.7, f32[1,768]{1,0:T(1,128)} %reshape.173.g_ref, bf16[768,16384]{1,0:T(8,128)(2,1)} %w_ref.23), custom_call_target="tpu_custom_call" | custom-call | flops 25769803776 | bytes 75497472 | tf_op jit(solution)/shard_map/first_columns/pallas_call | solution.py:330
  602.8 1.5 collective-permute-start.3
  604.3 33.5 %weight_grad.8 = (f32[768,1024]{1,0:T(8,128)}, f32[768,16384]{1,0:T(8,128)}) custom-call(s32[36]{0:T(128)} %fusion.13.table_ref, s32[1]{0:T(128)S(6)} %select_n.96.nt_ref, bf16[16384,768]{1,0:T(8,128)(2,1)} %get-tuple-element.41.n_hbm, f32[16384,128]{1,0:T(8,128)} %get-tuple-element.42.aux_hbm, bf16[768,16384]{1,0:T(8,128)(2,1)} %w_ref.23, ...), custom_call_target="tpu_custom_call" | custom-call | flops 25769803776 | bytes 31457280 | tf_op jit(solution)/shard_map/weight_grad/pallas_call | solution.py:423
  637.9 32.7 %weight_grad.9 = (f32[768,1024]{1,0:T(8,128)}, f32[768,16384]{1,0:T(8,128)}) custom-call(s32[36]{0:T(128)} %fusion.13.table_ref, s32[1]{0:T(128)S(6)} %select_n.96.nt_ref, bf16[16384,768]{1,0:T(8,128)(2,1)} %get-tuple-element.41.n_hbm, f32[16384,128]{1,0:T(8,128)} %get-tuple-element.42.aux_hbm, ...), custom_call_target="tpu_custom_call", output_to_operand_aliasing={{1}: (5, {})} | custom-call | flops 25769803776 | bytes 31457280 | tf_op jit(solution)/shard_map/weight_grad/pallas_call | solution.py:423
  670.6 32.5 %weight_grad.10 = (f32[768,1024]{1,0:T(8,128)}, f32[768,16384]{1,0:T(8,128)}) custom-call(s32[36]{0:T(128)} %fusion.13.table_ref, s32[1]{0:T(128)S(6)} %select_n.96.nt_ref, bf16[16384,768]{1,0:T(8,128)(2,1)} %get-tuple-element.41.n_hbm, f32[16384,128]{1,0:T(8,128)} %get-tuple-element.42.aux_hbm, ...), custom_call_target="tpu_custom_call", output_to_operand_aliasing={{1}: (5, {})} | custom-call | flops 25769803776 | bytes 31457280 | tf_op jit(solution)/shard_map/weight_grad/pallas_call | solution.py:423
  703.1 2.1 collective-permute-start.6
  705.7 33.5 %weight_grad.11 = (f32[768,1024]{1,0:T(8,128)}, f32[768,16384]{1,0:T(8,128)}) custom-call(s32[36]{0:T(128)} %fusion.13.table_ref, s32[1]{0:T(128)S(6)} %select_n.96.nt_ref, bf16[16384,768]{1,0:T(8,128)(2,1)} %get-tuple-element.41.n_hbm, f32[16384,128]{1,0:T(8,128)} %get-tuple-element.42.aux_hbm, ...), custom_call_target="tpu_custom_call", output_to_operand_aliasing={{1}: (5, {})} | custom-call | flops 25769803776 | bytes 31457280 | tf_op jit(solution)/shard_map/weight_grad/pallas_call | solution.py:423
  739.2 1.5 collective-permute-start.7
  740.8 1.1 collective-permute-done.4.rest_1_
  741.9 33.5 %weight_grad.12 = (f32[768,1024]{1,0:T(8,128)}, f32[768,16384]{1,0:T(8,128)}) custom-call(s32[36]{0:T(128)} %fusion.13.table_ref, s32[1]{0:T(128)S(6)} %select_n.96.nt_ref, bf16[16384,768]{1,0:T(8,128)(2,1)} %get-tuple-element.41.n_hbm, f32[16384,128]{1,0:T(8,128)} %get-tuple-element.42.aux_hbm, ...), custom_call_target="tpu_custom_call", output_to_operand_aliasing={{1}: (5, {})} | custom-call | flops 25769803776 | bytes 31457280 | tf_op jit(solution)/shard_map/weight_grad/pallas_call | solution.py:423
  775.5 0.9 collective-permute-done.5.rest_1_
  776.4 33.5 %weight_grad.13 = (f32[768,1024]{1,0:T(8,128)}, f32[768,16384]{1,0:T(8,128)}) custom-call(s32[36]{0:T(128)} %fusion.13.table_ref, s32[1]{0:T(128)S(6)} %select_n.96.nt_ref, bf16[16384,768]{1,0:T(8,128)(2,1)} %get-tuple-element.41.n_hbm, f32[16384,128]{1,0:T(8,128)} %get-tuple-element.42.aux_hbm, ...), custom_call_target="tpu_custom_call", output_to_operand_aliasing={{1}: (5, {})} | custom-call | flops 25769803776 | bytes 31457280 | tf_op jit(solution)/shard_map/weight_grad/pallas_call | solution.py:423
  809.9 0.6 collective-permute-start.9
  810.6 20.8 %weight_grad.14 = (f32[768,512]{1,0:T(8,128)}, f32[768,16384]{1,0:T(8,128)}) custom-call(s32[36]{0:T(128)} %fusion.13.table_ref, s32[1]{0:T(128)S(6)} %select_n.96.nt_ref, bf16[16384,768]{1,0:T(8,128)(2,1)} %get-tuple-element.41.n_hbm, f32[16384,128]{1,0:T(8,128)} %get-tuple-element.42.aux_hbm, ...), custom_call_target="tpu_custom_call", output_to_operand_aliasing={{1}: (5, {})} | custom-call | flops 12884901888 | bytes 28311552 | tf_op jit(solution)/shard_map/weight_grad/pallas_call | solution.py:423
  831.4 1.2 collective-permute-start.10
  832.5 11.3 %collective-permute-done.7.rest_1_ = f32[768,1024]{1,0:T(8,128)} collective-permute-done((f32[768,1024]{1,0:T(8,128)}, f32[768,1024]{1,0:T(8,128)}, u32[]{:S(2)}, u32[]{:S(2)}) %collective-permute-start.7) | collective-permute-done | bytes 3145760 | tf_op jit(solution)/shard_map/ppermute | solution.py:597
  843.8 32.9 %collective-permute-done.8.rest_2_ = f32[768,1024]{1,0:T(8,128)} collective-permute-done((f32[768,1024]{1,0:T(8,128)}, f32[768,1024]{1,0:T(8,128)}, u32[]{:S(2)}, u32[]{:S(2)}) %collective-permute-start.8) | collective-permute-done | bytes 3145760 | tf_op jit(solution)/shard_map/ppermute | solution.py:597
  876.7 35.5 %weight_grad.15 = (f32[768,1024]{1,0:T(8,128)}, f32[768,16384]{1,0:T(8,128)}) custom-call(s32[36]{0:T(128)} %fusion.13.table_ref, s32[1]{0:T(128)S(6)} %select_n.96.nt_ref, bf16[16384,768]{1,0:T(8,128)(2,1)} %get-tuple-element.41.n_hbm, f32[16384,128]{1,0:T(8,128)} %get-tuple-element.42.aux_hbm, ...), custom_call_target="tpu_custom_call", output_to_operand_aliasing={{1}: (5, {})} | custom-call | flops 25769803776 | bytes 31457280 | tf_op jit(solution)/shard_map/weight_grad/pallas_call | solution.py:423
  912.2 9.5 %tiny_gather.1 = f32[32,8,128]{2,1,0:T(8,128)} custom-call(f32[8,128]{1,0:T(8,128)} %concatenate.11.x_ref), custom_call_target="tpu_custom_call" | custom-call | tf_op jit(solution)/shard_map/tiny_gather/pallas_call | solution.py:65
  921.7 0.9 reduce_sum.131
  923.8 1.2 copy-done.6
  925.0 4.9 finish.1
  (90 shorter events, 5.9 us)
Async XLA Ops:
  8.0 3.6 copy-start
  8.0 327.7 %reduce-scatter.2.cloned.1.call-start = ((), (), s32[]{:S(2)}) async-start(), calls=%async_computation.2 | async-start | bytes 7864320 | tf_op jit(solution)/shard_map/reduce_scatter | solution.py:575
  11.6 5.7 copy-start.12
  12.3 1.1 copy-start.2
  12.3 1.3 copy-start.8
  13.4 3.9 copy-start.17
  13.4 4.1 copy-start.10
  13.4 5.3 copy-start.18
  13.4 5.3 copy-start.19
  13.5 5.3 copy-start.20
  13.5 5.3 copy-start.21
  13.7 37.6 %copy-start.5 = (f32[512,768]{1,0:T(8,128)}, f32[512,768]{1,0:T(8,128)S(1)}, u32[]{:S(2)}) copy-start(f32[512,768]{1,0:T(8,128)S(1)} %broadcast_multiply_fusion.xa) | copy-start | bytes 4718596
  13.7 37.5 %collective-permute-start.1 = (f32[512,768]{1,0:T(8,128)S(1)}, f32[512,768]{1,0:T(8,128)}, u32[]{:S(2)}, u32[]{:S(2)}) collective-permute-start(f32[512,768]{1,0:T(8,128)S(1)} %broadcast_multiply_fusion.xa), channel_id=1, source_target_pairs={{0,2},{1,3},{2,0},{3,1},{4,6},{5,7},{6,4},{7,5},{8,10},{9,11},{10,... | collective-permute-start | bytes 4718600 | tf_op jit(solution)/shard_map/ppermute | solution.py:511
  16.7 34.5 %collective-permute-start = (f32[512,768]{1,0:T(8,128)S(1)}, f32[512,768]{1,0:T(8,128)}, u32[]{:S(2)}, u32[]{:S(2)}) collective-permute-start(f32[512,768]{1,0:T(8,128)S(1)} %broadcast_multiply_fusion.xa), channel_id=1, source_target_pairs={{0,1},{1,0},{2,3},{3,2},{4,5},{5,4},{6,7},{7,6},{8,9},{9,8},{10,11... | collective-permute-start | bytes 4718600 | tf_op jit(solution)/shard_map/ppermute | solution.py:510
  51.2 36.4 %collective-permute-start.2 = (f32[512,768]{1,0:T(8,128)}, f32[512,768]{1,0:T(8,128)}, u32[]{:S(2)}, u32[]{:S(2)}) collective-permute-start(f32[512,768]{1,0:T(8,128)} %collective-permute-done.1.xa), channel_id=1, source_target_pairs={{0,1},{1,0},{2,3},{3,2},{4,5},{5,4},{6,7},{7,6},{8,9},{9,8},{10,11... | collective-permute-start | bytes 4718600 | tf_op jit(solution)/shard_map/ppermute | solution.py:514
  87.6 36.4 %copy-start.14 = (f32[2,2,512]{2,1,0:T(2,128)S(1)}, f32[2,2,512]{2,1,0:T(2,128)}, u32[]{:S(2)}) copy-start(f32[2,2,512]{2,1,0:T(2,128)} %get-tuple-element.35) | copy-start | bytes 24580
  163.5 48.1 %copy-start.15 = (s32[33]{0:T(128)}, s32[33]{0:T(128)S(1)}, u32[]{:S(2)}) copy-start(s32[33]{0:T(128)S(1)} %select_reduce_fusion.2.offs_ref) | copy-start | bytes 400
  170.2 41.4 %copy-start.7 = (f32[32,8,512]{2,1,0:T(8,128)}, f32[32,8,512]{2,1,0:T(8,128)S(1)}, u32[]{:S(2)}) copy-start(f32[32,8,512]{2,1,0:T(8,128)S(1)} %stack.50.aux_ref) | copy-start | bytes 1572868
  211.6 2.6 copy-start.16
  211.6 124.0 %copy-start.3 = (f32[512,768]{1,0:T(8,128)S(1)}, f32[512,768]{1,0:T(8,128)}, u32[]{:S(2)}) copy-start(f32[512,768]{1,0:T(8,128)} %copy-done.2) | copy-start | bytes 4718596
  211.7 124.0 %copy-start.9 = (f32[512]{0:T(512)S(1)}, f32[512]{0:T(512)}, u32[]{:S(2)}) copy-start(f32[512]{0:T(512)} %copy-done.8) | copy-start | bytes 6148
  211.7 124.0 %copy-start.11 = (f32[768]{0:T(1024)S(1)}, f32[768]{0:T(1024)}, u32[]{:S(2)}) copy-start(f32[768]{0:T(1024)} %param.12) | copy-start | bytes 9220
  211.7 341.9 %all-gather.3.cloned.1.call-start = ((), (), s32[]{:S(2)}) async-start(), calls=%async_computation.1 | async-start | bytes 51904512 | tf_op jit(solution)/shard_map/all_gather | solution.py:512
  215.5 122.9 %copy-start.13 = (s32[1,512]{1,0:T(1,128)S(1)}, s32[1,512]{1,0:T(1,128)}, u32[]{:S(2)}) copy-start(s32[1,512]{1,0:T(1,128)} %copy-done.12) | copy-start | bytes 6148
  335.7 2.6 copy-start.4
  602.8 102.9 %collective-permute-start.3 = (f32[768,1024]{1,0:T(8,128)}, f32[768,1024]{1,0:T(8,128)}, u32[]{:S(2)}, u32[]{:S(2)}) collective-permute-start(f32[768,1024]{1,0:T(8,128)} %get-tuple-element.43.rest_0_), channel_id=1, source_target_pairs={{0,4},{4,0},{8,12},{12,8},{16,20},{20,16},{24,28},{28,24},{1,5},{5... | collective-permute-start | bytes 9437192 | tf_op jit(solution)/shard_map/ppermute | solution.py:597
  670.5 71.4 %collective-permute-start.4 = (f32[768,1024]{1,0:T(8,128)}, f32[768,1024]{1,0:T(8,128)}, u32[]{:S(2)}, u32[]{:S(2)}) collective-permute-start(f32[768,1024]{1,0:T(8,128)} %get-tuple-element.48), channel_id=1, source_target_pairs={{0,8},{4,12},{8,0},{12,4},{16,24},{20,28},{24,16},{28,20},{1,9},{5... | collective-permute-start | bytes 9437192 | tf_op jit(solution)/shard_map/ppermute | solution.py:597
  703.1 107.5 %collective-permute-start.6 = (f32[768,1024]{1,0:T(8,128)}, f32[768,1024]{1,0:T(8,128)}, u32[]{:S(2)}, u32[]{:S(2)}) collective-permute-start(f32[768,1024]{1,0:T(8,128)} %get-tuple-element.52), channel_id=1, source_target_pairs={{0,8},{4,12},{8,0},{12,4},{16,24},{20,28},{24,16},{28,20},{1,9},{5... | collective-permute-start | bytes 9437192 | tf_op jit(solution)/shard_map/ppermute | solution.py:597
  705.1 71.3 %collective-permute-start.5 = (f32[768,1024]{1,0:T(8,128)}, f32[768,1024]{1,0:T(8,128)}, u32[]{:S(2)}, u32[]{:S(2)}) collective-permute-start(f32[768,1024]{1,0:T(8,128)} %get-tuple-element.50), channel_id=1, source_target_pairs={{0,4},{4,0},{8,12},{12,8},{16,20},{20,16},{24,28},{28,24},{1,5},{5... | collective-permute-start | bytes 9437192 | tf_op jit(solution)/shard_map/ppermute | solution.py:597
  739.2 104.6 %collective-permute-start.7 = (f32[768,1024]{1,0:T(8,128)}, f32[768,1024]{1,0:T(8,128)}, u32[]{:S(2)}, u32[]{:S(2)}) collective-permute-start(f32[768,1024]{1,0:T(8,128)} %get-tuple-element.54), channel_id=1, source_target_pairs={{0,4},{4,0},{8,12},{12,8},{16,20},{20,16},{24,28},{28,24},{1,5},{5... | collective-permute-start | bytes 9437192 | tf_op jit(solution)/shard_map/ppermute | solution.py:597
  775.4 101.3 %collective-permute-start.8 = (f32[768,1024]{1,0:T(8,128)}, f32[768,1024]{1,0:T(8,128)}, u32[]{:S(2)}, u32[]{:S(2)}) collective-permute-start(f32[768,1024]{1,0:T(8,128)} %get-tuple-element.55), channel_id=1, source_target_pairs={{0,8},{4,12},{8,0},{12,4},{16,24},{20,28},{24,16},{28,20},{1,9},{5... | collective-permute-start | bytes 9437192 | tf_op jit(solution)/shard_map/ppermute | solution.py:597
  809.9 113.9 %collective-permute-start.9 = (f32[768,1024]{1,0:T(8,128)}, f32[768,1024]{1,0:T(8,128)}, u32[]{:S(2)}, u32[]{:S(2)}) collective-permute-start(f32[768,1024]{1,0:T(8,128)} %get-tuple-element.64), channel_id=1, source_target_pairs={{0,4},{4,0},{8,12},{12,8},{16,20},{20,16},{24,28},{28,24},{1,5},{5... | collective-permute-start | bytes 9437192 | tf_op jit(solution)/shard_map/ppermute | solution.py:597
  831.4 92.4 %collective-permute-start.10 = (f32[768,512]{1,0:T(8,128)}, f32[768,512]{1,0:T(8,128)S(1)}, u32[]{:S(2)}, u32[]{:S(2)}) collective-permute-start(f32[768,512]{1,0:T(8,128)} %get-tuple-element.65), channel_id=1, source_target_pairs={{0,8},{4,12},{8,0},{12,4},{16,24},{20,28},{24,16},{28,20},{1,9},{5... | collective-permute-start | bytes 4718600 | tf_op jit(solution)/shard_map/ppermute | solution.py:597
  923.8 1.2 copy-start.6
  925.0 4.9 copy-start.1
Sparse Core Ops, SparseCore 0:
  211.8 123.8 reduce-scatter.1
Sparse Core Ops, SparseCore 1:
  215.0 338.5 all-gather.2

commit v6 on v5

--- a/solution.py
+++ b/solution.py
@@ -27,50 +27,6 @@
 
 
 f32, bf16, i32 = jnp.float32, jnp.bfloat16, jnp.int32
-
-
-def tiny_gather_kernel(dp_count, vp_count, x_ref, out_ref, send_sems, recv_sems):
-    count = dp_count * vp_count
-    me = lax.axis_index("dp") * vp_count + lax.axis_index("vp")
-    barrier = pltpu.get_barrier_semaphore()
-
-    def peer(k):
-        other = lax.rem(me + k, count)
-        return (other // vp_count, lax.rem(other, vp_count))
-
-    for k in range(1, count):
-        pl.semaphore_signal(barrier, inc=1, device_id=peer(k), device_id_type=pl.DeviceIdType.MESH)
-    pl.semaphore_wait(barrier, count - 1)
-    copies = [
-        pltpu.make_async_remote_copy(
-            src_ref=x_ref,
-            dst_ref=out_ref.at[me],
-            send_sem=send_sems.at[k - 1],
-            recv_sem=recv_sems.at[k - 1],
-            device_id=peer(k),
-            device_id_type=pl.DeviceIdType.MESH,
-        )
-        for k in range(1, count)
-    ]
-    for copy in copies:
-        copy.start()
-    out_ref[me] = x_ref[...]
-    for copy in copies:
-        copy.wait()
-
-
-def tiny_gather(x, mesh_shape, collective_id):
-    dp_count, vp_count = mesh_shape
-    count = dp_count * vp_count
-    return pl.pallas_call(
-        functools.partial(tiny_gather_kernel, dp_count, vp_count),
-        out_shape=jax.ShapeDtypeStruct((count, 8, 128), f32),
-        in_specs=[pl.BlockSpec(memory_space=pltpu.VMEM)],
-        out_specs=pl.BlockSpec(memory_space=pltpu.VMEM),
-        scratch_shapes=[pltpu.SemaphoreType.DMA((count - 1,)), pltpu.SemaphoreType.DMA((count - 1,))],
-        compiler_params=pltpu.CompilerParams(collective_id=collective_id, has_side_effects=True),
-        name="tiny_gather",
-    )(x)
 
 
 def place_masked(dst, off, span, new):
@@ -249,19 +205,24 @@
     )(offs, span, kept, mine, ntiles, col0, n_near, n_far, aux_row, w)
 
 
-def dw_tile(load, aux, w_ref, dz_ref, acc_ref, col0):
+def dw_tile(tok, load, aux, w_ref, dz_ref, acc_ref, col0):
     width = acc_ref.shape[1]
     group = min(width, DW_GROUP)
     sub = SUB if width > 256 else 2 * SUB
     for c in range(width // group):
         cols = pl.ds(c * group, group)
-        for u in range(DW_TOK // sub):
+        for u in range(tok // sub):
             rows = pl.ds(u * sub, sub)
             z = jnp.dot(load(u * sub, sub), w_ref[:, cols], preferred_element_type=f32)
             dz_ref[rows, cols], _ = grad_logits(z, aux(u * sub, sub), col0 + c * group)
         acc_ref[:, cols] += lax.dot_general(
-            load(0, DW_TOK), dz_ref[:, cols], (((0,), (0,)), ((), ())), preferred_element_type=f32
-        )
+            load(0, tok), dz_ref[pl.ds(0, tok), cols], (((0,), (0,)), ((), ())), preferred_element_type=f32
+        )
+
+
+def whole_tiles(count):
+    halves = (count + DW_TOK // 2 - 1) // (DW_TOK // 2)
+    return halves // 2, lax.rem(halves, 2)
 
 
 def first_kernel(offs_ref, table_ref, xh_ref, aux_ref, g_ref, w_ref, n_hbm, aux_hbm, acc_ref, n_img, aux_img, dz_ref, sems):
@@ -293,13 +254,15 @@
 
     start = offs_ref[step * xh_ref.shape[0]] // DW_TOK
     stop = offs_ref[(step + 1) * xh_ref.shape[0]] // DW_TOK
-    stop = jnp.where(step == last, (end + DW_TOK - 1) // DW_TOK, stop)
-
-    def tile(t, carry):
+    full, half = whole_tiles(end)
+    stop = jnp.where(step == last, full, stop)
+
+    def add(t, tok):
         for copy in copies(t):
             copy.start()
         row = pl.multiple_of(t * DW_TOK, DW_TOK)
         dw_tile(
+            tok,
             lambda at, size: n_img[pl.ds(row + at, size), :],
             lambda at, size: aux_img[pl.ds(row + at, size), :],
             w_ref,
@@ -307,9 +270,16 @@
             acc_ref,
             table_ref[1],
         )
+
+    def tile(t, carry):
+        add(t, DW_TOK)
         return carry
 
     lax.fori_loop(start, stop, tile, 0)
+
+    @pl.when((step == last) & (half == 1))
+    def _():
+        add(full, DW_TOK // 2)
 
     @pl.when(step == last)
     def _():
@@ -318,7 +288,7 @@
                 copy.wait()
             return carry
 
-        lax.fori_loop(0, stop, drain, 0)
+        lax.fori_loop(0, full + half, drain, 0)
 
 
 def first_columns(offs, table, xh_all, aux_all, g, w):
@@ -359,12 +329,12 @@
     )(offs, table, xh_all.reshape(blocks, BLK, DIM), aux_all, g, w)
 
 
-def dw_kernel(job, places, table_ref, nt_ref, n_hbm, aux_hbm, w_ref, *rest):
+def dw_kernel(job, places, table_ref, count_ref, n_hbm, aux_hbm, w_ref, *rest):
     merges = len(places)
     inputs, rest = rest[: -(6 + merges + 1)], rest[-(6 + merges + 1) :]
     out_ref, all_hbm, nbuf, abuf, dz_ref, sems = rest[:6]
     mbufs, out_sems = rest[6:-1], rest[-1]
-    steps = nt_ref[0]
+    full, half = whole_tiles(count_ref[0])
 
     def fetch(i, slot):
         rows = pl.ds(pl.multiple_of(i * DW_TOK, DW_TOK), DW_TOK)
@@ -384,10 +354,10 @@
         copy.start()
     out_ref[...] = jnp.zeros_like(out_ref)
 
-    def tile(i, carry):
+    def add(i, tok):
         slot = lax.rem(i, 2)
 
-        @pl.when(i + 1 < steps)
+        @pl.when(i + 1 < full + half)
         def _():
             for copy in fetch(i + 1, 1 - slot):
                 copy.start()
@@ -395,6 +365,7 @@
         for copy in fetch(i, slot):
             copy.wait()
         dw_tile(
+            tok,
             lambda start, size: nbuf[slot, pl.ds(start, size), :],
             lambda start, size: abuf[slot, pl.ds(start, size), :],
             w_ref,
@@ -402,9 +373,17 @@
             out_ref,
             table_ref[4 * job + 1],
         )
+
+    def tile(i, carry):
+        add(i, DW_TOK)
         return carry
 
-    lax.fori_loop(0, steps, tile, 0)
+    lax.fori_loop(0, full, tile, 0)
+
+    @pl.when(half == 1)
+    def _():
+        add(full, DW_TOK // 2)
+
     own = put(out_ref, table_ref[4 * job + 2], out_sems.at[merges, 0])
     own.start()
     for copy in moves_in:
@@ -415,7 +394,7 @@
         copy.wait()
 
 
-def weight_grad(job, width, table, ntiles, n_all, aux_all, w, whole, merges):
+def weight_grad(job, width, table, count, n_all, aux_all, w, whole, merges):
     tokens, vocab = n_all.shape[0], w.shape[1]
     anywhere = pl.BlockSpec(memory_space=pl.ANY)
     chunks = [chunk for chunk, _ in merges]
@@ -425,7 +404,7 @@
         grid_spec=pltpu.PrefetchScalarGridSpec(
             num_scalar_prefetch=2,
             grid=(1,),
-            in_specs=[anywhere, anywhere, pl.BlockSpec((DIM, width), lambda s, table, nt: (0, table[4 * job]))]
+            in_specs=[anywhere, anywhere, pl.BlockSpec((DIM, width), lambda s, table, count: (0, table[4 * job]))]
             + [anywhere] * len(held),
             out_specs=[pl.BlockSpec((DIM, width), lambda s, *_: (0, 0)), anywhere],
             scratch_shapes=[
@@ -447,7 +426,7 @@
             flops=2 * tokens * DIM * width, bytes_accessed=2 * tokens * DIM + 8 * DIM * width, transcendentals=tokens * width // 2
         ),
         name="weight_grad",
-    )(table, ntiles, n_all, aux_all, w, *held)
+    )(table, count, n_all, aux_all, w, *held)
 
 
 def finish_kernel(places, table_ref, whole_hbm, *rest):
@@ -487,7 +466,6 @@
 
 def solution(mesh):
     dp_count, vp_count = mesh.shape["dp"], mesh.shape["vp"]
-    everyone = (dp_count, vp_count)
 
     def local_step(hidden, targets, loss_mask, norm_scale, w_head):
         vocab = w_head.shape[1]
@@ -536,7 +514,7 @@
         blocks = dp_count * vp_count
         before = lax.iota(i32, blocks)[None, :] < lax.iota(i32, blocks + 1)[:, None]
         offs = jnp.sum(jnp.where(before, span[None, :], 0), axis=1)
-        nt_all = (offs[blocks:] + DW_TOK - 1) // DW_TOK
+        count = offs[blocks:]
 
         first = dp * vp_count
         kept_row = lax.dynamic_slice(kept_all, (first,), (vp_count,))
@@ -567,7 +545,7 @@
             )
         )
         table = start + y_step * (dp % 2) + z_step * (dp // 2 % 2) + v_step * vp
-        aux_row, offs, nt_all, table, aux_all = lax.optimization_barrier((aux_row, offs, nt_all, table, aux_all))
+        aux_row, offs, count, table, aux_all = lax.optimization_barrier((aux_row, offs, count, table, aux_all))
 
         dn_part, t_part = backward_dn(
             offs_row, span_row, kept_row, mine, nt_row, (vp * vocab).reshape(1), n_near, n_far, aux_row, w_head
@@ -581,22 +559,19 @@
         d_x = jnp.dot(back, d_x.astype(bf16), preferred_element_type=f32).astype(bf16)
         lse_own = lax.dynamic_slice(lse_row, (vp, 0), (1, BLK))[0]
         loss_part = weight * jnp.sum(jnp.where(idx < kept, lse_own, 0.0)) - jnp.sum(t_part)
-        parts = jnp.concatenate([d_scale.reshape(6, 128), jnp.full((2, 128), loss_part, f32)])
+        parts = jnp.concatenate([d_scale.reshape(6, 128), jnp.full((58, 128), loss_part, f32)])
+        parts = lax.all_gather(parts, ("dp", "vp"), axis=0)
+        parts = jnp.sum(parts[:, :8], axis=0)
 
         n_all, auxc_all, chunk = first_columns(offs, table, xh_all, aux_all, g, w_head)
         own, whole, moved = (chunk, 2), None, []
         for k, (width, *_, pairs) in enumerate(jobs):
             if k:
                 merges = [own] if k == 1 else [moved[k - LAG]] if k >= LAG else []
-                if k == len(jobs) - 1:
-                    merges.append(moved[k - LAG + 1])
-                chunk, whole = weight_grad(k, width, table, nt_all, n_all, auxc_all, w_head, whole, merges)
-            if k == len(jobs) - 1:
-                whole, parts = lax.optimization_barrier((whole, parts))
+                chunk, whole = weight_grad(k, width, table, count, n_all, auxc_all, w_head, whole, merges)
             if pairs:
                 moved.append((lax.ppermute(chunk, "dp", pairs), 4 * k + 3))
-        parts = jnp.sum(tiny_gather(parts, everyone, 1), axis=0)
-        whole = finish(table, whole, moved[len(jobs) - LAG + 1 :])
+        whole = finish(table, whole, moved[len(jobs) - LAG :])
         return parts[6, 0], d_x[None], whole, parts[:6].reshape(DIM)
 
     return jax.shard_map(

time: 944 us -> 1060 us (1.12)
  waiting for transfers between devices: 412 us -> 518 us
  Pallas kernels: 432 us -> 444 us
    all_gather x1, waiting for transfers between devices: 213 us -> 275 us  [local_step(): xh_all = lax.all_gather(x_hat, ('dp', 'vp'), axis=0, tiled=True)]
    all_gather x0 -> x1, waiting for transfers between devices: none -> 50.6 us  [local_step(): parts = lax.all_gather(parts, ('dp', 'vp'), axis=0)]
    pallas_call x8, Pallas kernels: 256 us -> 273 us  [weight_grad(): pl.pallas_call(functools.partial(dw_kernel, job, [at for _, at in merges]...]
  transfers between devices with their start and end apart: 13 -> 14, of which waited for: 7 -> 6; matrix products, arithmetic and copies ran while one was open for 1% -> 1% of each run, Pallas kernels for 32% -> 29%
where the time goes in v6:
time: 1060 us; the launch traced here: 1050 us
  waiting for transfers between devices  518 us (49%)
  Pallas kernels  444 us (42%)
  blocking collectives  37 us (3%)
  between operations  18 us (2%)
  other arithmetic  14.8 us (1%)
  starting transfers between devices  12.1 us (1%)
    all_gather x1, waiting for transfers between devices, local_step(): xh_all = lax.all_gather(x_hat, ('dp', 'vp'), axis=0, tiled=True)  275 us
    pallas_call x8, Pallas kernels, weight_grad(): pl.pallas_call(functools.partial(dw_kernel, job, [at for _, at in merges]...  273 us
    reduce_scatter x1, waiting for transfers between devices, local_step(): d_normed = lax.psum_scatter(dn_part, 'vp', scatter_dimension=0, tiled=True)  117 us
    pallas_call x2, Pallas kernels, forward_stats(): pl.pallas_call(functools.partial(fwd_kernel, group), grid=(vocab // FWD_C...  72.7 us
    pallas_call x1, Pallas kernels, first_columns(): pl.pallas_call(first_kernel, grid_spec=pltpu.PrefetchScalarGridSpec(num_s...  51.5 us
    all_gather x1, waiting for transfers between devices, local_step(): parts = lax.all_gather(parts, ('dp', 'vp'), axis=0)  50.6 us
    ppermute x8, waiting for transfers between devices, local_step(): moved.append((lax.ppermute(chunk, 'dp', pairs), 4 * k + 3))  43.3 us
    pallas_call x1, Pallas kernels, backward_dn(): pl.pallas_call(dn_kernel, grid_spec=pltpu.PrefetchScalarGridSpec(num_scal...  40.7 us
  transfers between devices with their start and end apart: 14, of which 6 were waited for; matrix products, arithmetic and copies ran while one was open for 1% of the time, Pallas kernels for 29%

profile of v6, /device:TPU:0, one launch (start us, length us, event | category | flops | bytes accessed | tf_op | source)
XLA Modules:
  0.0 1054.7 jit_solution(6829619393893883224)
XLA Ops:
  7.2 1.4 reduce_sum.121
  8.6 0.8 select_reduce_fusion.1
  9.4 1.3 compare_select_fusion.3
  10.8 0.7 multiply_reduce_fusion.2
  11.5 1.1 copy-done.2
  12.9 3.0 collective-permute-start.1
  17.9 0.6 fusion.13.table_ref
  18.5 31.9 %collective-permute-done.1.xa = f32[512,768]{1,0:T(8,128)} collective-permute-done((f32[512,768]{1,0:T(8,128)S(1)}, f32[512,768]{1,0:T(8,128)}, u32[]{:S(2)}, u32[]{:S(2)}) %collective-permute-start.1) | collective-permute-done | bytes 1572896 | tf_op jit(solution)/shard_map/ppermute | solution.py:489
  50.4 36.3 %fwd_stats.2 = (bf16[1024,768]{1,0:T(8,128)(2,1)}, f32[2,2,512]{2,1,0:T(2,128)}) custom-call(f32[512,768]{1,0:T(8,128)} %copy-done.4, f32[512,768]{1,0:T(8,128)} %collective-permute-done.xb, f32[1,768]{1,0:T(1,128)} %reshape.169.g_ref, bf16[768,16384]{1,0:T(8,128)(2,1)} %w_ref.23), custom_call_target="tpu_custom_call" | custom-call | flops 25769803776 | bytes 33030144 | tf_op jit(solution)/shard_map/fwd_stats/pallas_call | solution.py:91
  86.8 36.3 %fwd_stats.3 = (bf16[1024,768]{1,0:T(8,128)(2,1)}, f32[2,2,512]{2,1,0:T(2,128)}) custom-call(f32[512,768]{1,0:T(8,128)} %collective-permute-done.1.xa, f32[512,768]{1,0:T(8,128)} %collective-permute-done.2.xb, f32[1,768]{1,0:T(1,128)} %reshape.169.g_ref, bf16[768,16384]{1,0:T(8,128)(2,1)} %w_ref.23), custom_call_target="tpu_custom_call" | custom-call | flops 25769803776 | bytes 33030144 | tf_op jit(solution)/shard_map/fwd_stats/pallas_call | solution.py:91
  123.1 0.7 pad_maximum_fusion.2
  123.8 5.5 all-gather
  129.6 31.5 %all_gather.20 = f32[32,3,512]{2,1,0:T(4,128)S(1)} all-gather(f32[4,3,512]{2,1,0:T(4,128)S(1)} %pad_maximum_fusion.1), channel_id=1, replica_groups=mesh['dp'=8,'vp'=4] {'dp'}, dimensions={0}, use_global_device_ids=true | all-gather | bytes 221184 | tf_op jit(solution)/shard_map/all_gather | solution.py:503
  161.1 1.2 fusion.15
  162.4 1.3 fusion.17
  165.1 0.6 fusion.20
  165.7 1.3 dynamic-slice_subtract_fusion.offs_ref
  167.2 0.7 dynamic-slice_reduce_fusion.kept_ref
  168.6 0.7 constant_dynamic-slice_fusion.aux_ref
  169.3 40.7 %backward_dn.1 = (f32[2048,768]{1,0:T(8,128)}, f32[8,128]{1,0:T(8,128)}) custom-call(s32[4]{0:T(128)} %dynamic-slice_subtract_fusion.offs_ref, s32[4]{0:T(128)} %get-tuple-element.67.span_ref, s32[4]{0:T(128)} %dynamic-slice_reduce_fusion.kept_ref, s32[4]{0:T(128)} %iota_xor_fusion.mine_ref, s32[1]{0:T(128)} %bitcast.31.nt_ref, s32[1]{0:T(128)} %bitcast.32.col_ref, ...), custom_call_target="tpu_custom_call" | custom-call | flops 103079215104 | bytes 34603008 | tf_op jit(solution)/shard_map/backward_dn/pallas_call | solution.py:174
  210.1 1.3 select_reduce_fusion.3
  212.1 0.6 reduce_sum.130
  213.4 116.9 %reduce-scatter.2.cloned.1.call-done = f32[512,768]{1,0:T(8,128)} async-done(((f32[2048,768]{1,0:T(8,128)}), f32[512,768]{1,0:T(8,128)}) %reduce-scatter.2.cloned.1.call-update) | async-done | bytes 1572880 | tf_op jit(solution)/shard_map/reduce_scatter | solution.py:553
  330.3 1.9 multiply_reduce_fusion
  332.2 0.6 concatenate.11
  333.6 3.2 fusion
  336.8 50.6 %all-gather.7.cloned.1.call-done = f32[2048,128]{1,0:T(8,128)} async-done(((f32[64,128]{1,0:T(8,128)}), f32[2048,128]{1,0:T(8,128)}) %all-gather.7.cloned.1.call-update) | async-done | bytes 1048592 | tf_op jit(solution)/shard_map/all_gather | solution.py:563
  387.4 0.9 slice_reduce_fusion
  388.8 0.6 slice_bitcast_fusion.17
  389.4 274.6 %all-gather.5.cloned.1.call-done = f32[16384,768]{1,0:T(8,128)} async-done(((f32[512,768]{1,0:T(8,128)}), f32[16384,768]{1,0:T(8,128)}) %all-gather.5.cloned.1.call-update) | async-done | bytes 50331664 | tf_op jit(solution)/shard_map/all_gather | solution.py:490
  664.1 51.5 %first_columns.1 = (bf16[16384,768]{1,0:T(8,128)(2,1)}, f32[16384,128]{1,0:T(8,128)}, f32[768,1024]{1,0:T(8,128)}) custom-call(s32[33]{0:T(128)} %copy-done.14, s32[36]{0:T(128)} %fusion.13.table_ref, f32[32,512,768]{2,1,0:T(8,128)} %bitcast.95, f32[32,8,512]{2,1,0:T(8,128)} %copy-done.6, f32[1,768]{1,0:T(1,128)} %reshape.169.g_ref, bf16[768,16384]{1,0:T(8,128)(2,1)} %w_ref.23), custom_call_target="tpu_custom_call" | custom-call | flops 25769803776 | bytes 75497472 | tf_op jit(solution)/shard_map/first_columns/pallas_call | solution.py:300
  715.6 1.6 collective-permute-start.3
  717.2 36.4 %weight_grad.8 = (f32[768,1024]{1,0:T(8,128)}, f32[768,16384]{1,0:T(8,128)}) custom-call(s32[36]{0:T(128)} %fusion.13.table_ref, s32[1]{0:T(128)} %get-tuple-element.41.count_ref, bf16[16384,768]{1,0:T(8,128)(2,1)} %get-tuple-element.44.n_hbm, f32[16384,128]{1,0:T(8,128)} %get-tuple-element.45.aux_hbm, bf16[768,16384]{1,0:T(8,128)(2,1)} %w_ref.23, ...), custom_call_target="tpu_custom_call" | custom-call | flops 25769803776 | bytes 31457280 | tf_op jit(solution)/shard_map/weight_grad/pallas_call | solution.py:402
  753.6 35.3 %weight_grad.9 = (f32[768,1024]{1,0:T(8,128)}, f32[768,16384]{1,0:T(8,128)}) custom-call(s32[36]{0:T(128)} %fusion.13.table_ref, s32[1]{0:T(128)} %get-tuple-element.41.count_ref, bf16[16384,768]{1,0:T(8,128)(2,1)} %get-tuple-element.44.n_hbm, f32[16384,128]{1,0:T(8,128)} %get-tuple-element.45.aux_hbm, ...), custom_call_target="tpu_custom_call", output_to_operand_aliasing={{1}: (5, {})} | custom-call | flops 25769803776 | bytes 31457280 | tf_op jit(solution)/shard_map/weight_grad/pallas_call | solution.py:402
  789.0 35.3 %weight_grad.10 = (f32[768,1024]{1,0:T(8,128)}, f32[768,16384]{1,0:T(8,128)}) custom-call(s32[36]{0:T(128)} %fusion.13.table_ref, s32[1]{0:T(128)} %get-tuple-element.41.count_ref, bf16[16384,768]{1,0:T(8,128)(2,1)} %get-tuple-element.44.n_hbm, f32[16384,128]{1,0:T(8,128)} %get-tuple-element.45.aux_hbm, ...), custom_call_target="tpu_custom_call", output_to_operand_aliasing={{1}: (5, {})} | custom-call | flops 25769803776 | bytes 31457280 | tf_op jit(solution)/shard_map/weight_grad/pallas_call | solution.py:402
  824.2 2.1 collective-permute-start.6
  826.8 36.3 %weight_grad.11 = (f32[768,1024]{1,0:T(8,128)}, f32[768,16384]{1,0:T(8,128)}) custom-call(s32[36]{0:T(128)} %fusion.13.table_ref, s32[1]{0:T(128)} %get-tuple-element.41.count_ref, bf16[16384,768]{1,0:T(8,128)(2,1)} %get-tuple-element.44.n_hbm, f32[16384,128]{1,0:T(8,128)} %get-tuple-element.45.aux_hbm, ...), custom_call_target="tpu_custom_call", output_to_operand_aliasing={{1}: (5, {})} | custom-call | flops 25769803776 | bytes 31457280 | tf_op jit(solution)/shard_map/weight_grad/pallas_call | solution.py:402
  863.1 1.6 collective-permute-start.7
  864.7 36.2 %weight_grad.12 = (f32[768,1024]{1,0:T(8,128)}, f32[768,16384]{1,0:T(8,128)}) custom-call(s32[36]{0:T(128)} %fusion.13.table_ref, s32[1]{0:T(128)} %get-tuple-element.41.count_ref, bf16[16384,768]{1,0:T(8,128)(2,1)} %get-tuple-element.44.n_hbm, f32[16384,128]{1,0:T(8,128)} %get-tuple-element.45.aux_hbm, ...), custom_call_target="tpu_custom_call", output_to_operand_aliasing={{1}: (5, {})} | custom-call | flops 25769803776 | bytes 31457280 | tf_op jit(solution)/shard_map/weight_grad/pallas_call | solution.py:402
  900.9 36.3 %weight_grad.13 = (f32[768,1024]{1,0:T(8,128)}, f32[768,16384]{1,0:T(8,128)}) custom-call(s32[36]{0:T(128)} %fusion.13.table_ref, s32[1]{0:T(128)} %get-tuple-element.41.count_ref, bf16[16384,768]{1,0:T(8,128)(2,1)} %get-tuple-element.44.n_hbm, f32[16384,128]{1,0:T(8,128)} %get-tuple-element.45.aux_hbm, ...), custom_call_target="tpu_custom_call", output_to_operand_aliasing={{1}: (5, {})} | custom-call | flops 25769803776 | bytes 31457280 | tf_op jit(solution)/shard_map/weight_grad/pallas_call | solution.py:402
  937.2 0.6 collective-permute-start.9
  937.9 20.8 %weight_grad.14 = (f32[768,512]{1,0:T(8,128)}, f32[768,16384]{1,0:T(8,128)}) custom-call(s32[36]{0:T(128)} %fusion.13.table_ref, s32[1]{0:T(128)} %get-tuple-element.41.count_ref, bf16[16384,768]{1,0:T(8,128)(2,1)} %get-tuple-element.44.n_hbm, f32[16384,128]{1,0:T(8,128)} %get-tuple-element.45.aux_hbm, ...), custom_call_target="tpu_custom_call", output_to_operand_aliasing={{1}: (5, {})} | custom-call | flops 12884901888 | bytes 28311552 | tf_op jit(solution)/shard_map/weight_grad/pallas_call | solution.py:402
  958.7 2.0 collective-permute-start.10
  960.7 4.3 collective-permute-done.7.rest_1_
  965.0 36.3 %weight_grad.15 = (f32[768,1024]{1,0:T(8,128)}, f32[768,16384]{1,0:T(8,128)}) custom-call(s32[36]{0:T(128)} %fusion.13.table_ref, s32[1]{0:T(128)} %get-tuple-element.41.count_ref, bf16[16384,768]{1,0:T(8,128)(2,1)} %get-tuple-element.44.n_hbm, f32[16384,128]{1,0:T(8,128)} %get-tuple-element.45.aux_hbm, ...), custom_call_target="tpu_custom_call", output_to_operand_aliasing={{1}: (5, {})} | custom-call | flops 25769803776 | bytes 31457280 | tf_op jit(solution)/shard_map/weight_grad/pallas_call | solution.py:402
  1001.3 39.0 %collective-permute-done.10.rest_2_ = f32[768,512]{1,0:T(8,128)S(1)} collective-permute-done((f32[768,512]{1,0:T(8,128)}, f32[768,512]{1,0:T(8,128)S(1)}, u32[]{:S(2)}, u32[]{:S(2)}) %collective-permute-start.10) | collective-permute-done | bytes 1572896 | tf_op jit(solution)/shard_map/ppermute | solution.py:573
  1040.3 1.1 copy-done.5
  1041.5 6.2 finish.1
  (90 shorter events, 4.9 us)
Async XLA Ops:
  7.2 3.6 copy-start
  7.2 323.1 %reduce-scatter.2.cloned.1.call-start = ((), (), s32[]{:S(2)}) async-start(), calls=%async_computation.1 | async-start | bytes 7864320 | tf_op jit(solution)/shard_map/reduce_scatter | solution.py:553
  10.8 5.8 copy-start.11
  11.5 1.2 copy-start.2
  11.5 1.4 copy-start.7
  12.6 3.9 copy-start.16
  12.6 4.1 copy-start.9
  12.6 5.2 copy-start.17
  12.6 5.2 copy-start.18
  12.7 5.2 copy-start.19
  12.7 5.2 copy-start.20
  12.9 37.6 %copy-start.4 = (f32[512,768]{1,0:T(8,128)}, f32[512,768]{1,0:T(8,128)S(1)}, u32[]{:S(2)}) copy-start(f32[512,768]{1,0:T(8,128)S(1)} %broadcast_multiply_fusion.xa) | copy-start | bytes 4718596
  12.9 37.5 %collective-permute-start.1 = (f32[512,768]{1,0:T(8,128)S(1)}, f32[512,768]{1,0:T(8,128)}, u32[]{:S(2)}, u32[]{:S(2)}) collective-permute-start(f32[512,768]{1,0:T(8,128)S(1)} %broadcast_multiply_fusion.xa), channel_id=1, source_target_pairs={{0,2},{1,3},{2,0},{3,1},{4,6},{5,7},{6,4},{7,5},{8,10},{9,11},{10,... | collective-permute-start | bytes 4718600 | tf_op jit(solution)/shard_map/ppermute | solution.py:489
  15.9 34.5 %collective-permute-start = (f32[512,768]{1,0:T(8,128)S(1)}, f32[512,768]{1,0:T(8,128)}, u32[]{:S(2)}, u32[]{:S(2)}) collective-permute-start(f32[512,768]{1,0:T(8,128)S(1)} %broadcast_multiply_fusion.xa), channel_id=1, source_target_pairs={{0,1},{1,0},{2,3},{3,2},{4,5},{5,4},{6,7},{7,6},{8,9},{9,8},{10,11... | collective-permute-start | bytes 4718600 | tf_op jit(solution)/shard_map/ppermute | solution.py:488
  50.4 36.4 %collective-permute-start.2 = (f32[512,768]{1,0:T(8,128)}, f32[512,768]{1,0:T(8,128)}, u32[]{:S(2)}, u32[]{:S(2)}) collective-permute-start(f32[512,768]{1,0:T(8,128)} %collective-permute-done.1.xa), channel_id=1, source_target_pairs={{0,1},{1,0},{2,3},{3,2},{4,5},{5,4},{6,7},{7,6},{8,9},{9,8},{10,11... | collective-permute-start | bytes 4718600 | tf_op jit(solution)/shard_map/ppermute | solution.py:492
  86.8 36.4 %copy-start.13 = (f32[2,2,512]{2,1,0:T(2,128)S(1)}, f32[2,2,512]{2,1,0:T(2,128)}, u32[]{:S(2)}) copy-start(f32[2,2,512]{2,1,0:T(2,128)} %get-tuple-element.33) | copy-start | bytes 24580
  162.4 47.5 %copy-start.14 = (s32[33]{0:T(128)}, s32[33]{0:T(128)S(1)}, u32[]{:S(2)}) copy-start(s32[33]{0:T(128)S(1)} %select_reduce_fusion.2.offs_ref) | copy-start | bytes 400
  168.6 41.4 %copy-start.6 = (f32[32,8,512]{2,1,0:T(8,128)}, f32[32,8,512]{2,1,0:T(8,128)S(1)}, u32[]{:S(2)}) copy-start(f32[32,8,512]{2,1,0:T(8,128)S(1)} %stack.50.aux_ref) | copy-start | bytes 1572868
  210.0 2.1 copy-start.15
  210.0 120.3 %copy-start.3 = (f32[512,768]{1,0:T(8,128)S(1)}, f32[512,768]{1,0:T(8,128)}, u32[]{:S(2)}) copy-start(f32[512,768]{1,0:T(8,128)} %copy-done.2) | copy-start | bytes 4718596
  210.0 120.3 %copy-start.8 = (f32[512]{0:T(512)S(1)}, f32[512]{0:T(512)}, u32[]{:S(2)}) copy-start(f32[512]{0:T(512)} %copy-done.7) | copy-start | bytes 6148
  210.0 120.3 %copy-start.10 = (f32[768]{0:T(1024)S(1)}, f32[768]{0:T(1024)}, u32[]{:S(2)}) copy-start(f32[768]{0:T(1024)} %param.12) | copy-start | bytes 9220
  210.0 177.4 %all-gather.7.cloned.1.call-start = ((), (), s32[]{:S(2)}) async-start(), calls=%async_computation.3 | async-start | bytes 1081344 | tf_op jit(solution)/shard_map/all_gather | solution.py:563
  332.2 1.4 copy-start.12
  332.8 331.2 %all-gather.5.cloned.1.call-start = ((), (), s32[]{:S(2)}) async-start(), calls=%async_computation.2 | async-start | bytes 51904512 | tf_op jit(solution)/shard_map/all_gather | solution.py:490
  715.6 111.2 %collective-permute-start.3 = (f32[768,1024]{1,0:T(8,128)}, f32[768,1024]{1,0:T(8,128)}, u32[]{:S(2)}, u32[]{:S(2)}) collective-permute-start(f32[768,1024]{1,0:T(8,128)} %get-tuple-element.46.rest_0_), channel_id=1, source_target_pairs={{0,4},{4,0},{8,12},{12,8},{16,20},{20,16},{24,28},{28,24},{1,5},{5... | collective-permute-start | bytes 9437192 | tf_op jit(solution)/shard_map/ppermute | solution.py:573
  788.9 75.8 %collective-permute-start.4 = (f32[768,1024]{1,0:T(8,128)}, f32[768,1024]{1,0:T(8,128)}, u32[]{:S(2)}, u32[]{:S(2)}) collective-permute-start(f32[768,1024]{1,0:T(8,128)} %get-tuple-element.51), channel_id=1, source_target_pairs={{0,8},{4,12},{8,0},{12,4},{16,24},{20,28},{24,16},{28,20},{1,9},{5... | collective-permute-start | bytes 9437192 | tf_op jit(solution)/shard_map/ppermute | solution.py:573
  824.2 113.7 %collective-permute-start.6 = (f32[768,1024]{1,0:T(8,128)}, f32[768,1024]{1,0:T(8,128)}, u32[]{:S(2)}, u32[]{:S(2)}) collective-permute-start(f32[768,1024]{1,0:T(8,128)} %get-tuple-element.55), channel_id=1, source_target_pairs={{0,8},{4,12},{8,0},{12,4},{16,24},{20,28},{24,16},{28,20},{1,9},{5... | collective-permute-start | bytes 9437192 | tf_op jit(solution)/shard_map/ppermute | solution.py:573
  826.3 74.6 %collective-permute-start.5 = (f32[768,1024]{1,0:T(8,128)}, f32[768,1024]{1,0:T(8,128)}, u32[]{:S(2)}, u32[]{:S(2)}) collective-permute-start(f32[768,1024]{1,0:T(8,128)} %get-tuple-element.53), channel_id=1, source_target_pairs={{0,4},{4,0},{8,12},{12,8},{16,20},{20,16},{24,28},{28,24},{1,5},{5... | collective-permute-start | bytes 9437192 | tf_op jit(solution)/shard_map/ppermute | solution.py:573
  863.1 101.9 %collective-permute-start.7 = (f32[768,1024]{1,0:T(8,128)}, f32[768,1024]{1,0:T(8,128)}, u32[]{:S(2)}, u32[]{:S(2)}) collective-permute-start(f32[768,1024]{1,0:T(8,128)} %get-tuple-element.57), channel_id=1, source_target_pairs={{0,4},{4,0},{8,12},{12,8},{16,20},{20,16},{24,28},{28,24},{1,5},{5... | collective-permute-start | bytes 9437192 | tf_op jit(solution)/shard_map/ppermute | solution.py:573
  937.2 103.1 %collective-permute-start.9 = (f32[768,1024]{1,0:T(8,128)}, f32[768,1024]{1,0:T(8,128)}, u32[]{:S(2)}, u32[]{:S(2)}) collective-permute-start(f32[768,1024]{1,0:T(8,128)} %get-tuple-element.60), channel_id=1, source_target_pairs={{0,4},{4,0},{8,12},{12,8},{16,20},{20,16},{24,28},{28,24},{1,5},{5... | collective-permute-start | bytes 9437192 | tf_op jit(solution)/shard_map/ppermute | solution.py:573
  937.8 102.5 %collective-permute-start.8 = (f32[768,1024]{1,0:T(8,128)}, f32[768,1024]{1,0:T(8,128)}, u32[]{:S(2)}, u32[]{:S(2)}) collective-permute-start(f32[768,1024]{1,0:T(8,128)} %get-tuple-element.59), channel_id=1, source_target_pairs={{0,8},{4,12},{8,0},{12,4},{16,24},{20,28},{24,16},{28,20},{1,9},{5... | collective-permute-start | bytes 9437192 | tf_op jit(solution)/shard_map/ppermute | solution.py:573
  958.7 81.6 %collective-permute-start.10 = (f32[768,512]{1,0:T(8,128)}, f32[768,512]{1,0:T(8,128)S(1)}, u32[]{:S(2)}, u32[]{:S(2)}) collective-permute-start(f32[768,512]{1,0:T(8,128)} %get-tuple-element.61), channel_id=1, source_target_pairs={{0,8},{4,12},{8,0},{12,4},{16,24},{20,28},{24,16},{28,20},{1,9},{5... | collective-permute-start | bytes 4718600 | tf_op jit(solution)/shard_map/ppermute | solution.py:573
  1040.3 1.1 copy-start.5
  1041.5 6.3 copy-start.1
Sparse Core Ops, SparseCore 0:
  210.2 120.0 reduce-scatter.1
  333.7 53.6 all-gather.6
  390.3 273.7 all-gather.4

commit v7 on v6

--- a/solution.py
+++ b/solution.py
@@ -329,11 +329,11 @@
     )(offs, table, xh_all.reshape(blocks, BLK, DIM), aux_all, g, w)
 
 
-def dw_kernel(job, places, table_ref, count_ref, n_hbm, aux_hbm, w_ref, *rest):
+def dw_kernel(job, places, table_ref, count_ref, n_hbm, aux_hbm, w_hbm, *rest):
     merges = len(places)
-    inputs, rest = rest[: -(6 + merges + 1)], rest[-(6 + merges + 1) :]
-    out_ref, all_hbm, nbuf, abuf, dz_ref, sems = rest[:6]
-    mbufs, out_sems = rest[6:-1], rest[-1]
+    inputs, rest = rest[: -(9 + merges)], rest[-(9 + merges) :]
+    chunk_hbm, all_hbm, out_ref, w_ref, nbuf, abuf, dz_ref, sems = rest[:8]
+    mbufs, out_sems = rest[8:-1], rest[-1]
     full, half = whole_tiles(count_ref[0])
 
     def fetch(i, slot):
@@ -346,6 +346,9 @@
     def put(ref, col, sem):
         return pltpu.make_async_copy(ref, all_hbm.at[:, pl.ds(pl.multiple_of(col, 128), ref.shape[1])], sem)
 
+    cols = pl.ds(pl.multiple_of(table_ref[4 * job + 2], 128), out_ref.shape[1])
+    columns = pltpu.make_async_copy(w_hbm.at[:, cols], w_ref, out_sems.at[merges, 1])
+    columns.start()
     for copy in fetch(0, 0):
         copy.start()
     moves_in = [pltpu.make_async_copy(src, mbuf, out_sems.at[k, 0]) for k, (src, mbuf) in enumerate(zip(inputs[-merges:], mbufs))]
@@ -353,6 +356,7 @@
     for copy in moves_in:
         copy.start()
     out_ref[...] = jnp.zeros_like(out_ref)
+    columns.wait()
 
     def add(i, tok):
         slot = lax.rem(i, 2)
@@ -385,12 +389,14 @@
         add(full, DW_TOK // 2)
 
     own = put(out_ref, table_ref[4 * job + 2], out_sems.at[merges, 0])
+    sent = pltpu.make_async_copy(out_ref, chunk_hbm, out_sems.at[merges, 1])
+    sent.start()
     own.start()
     for copy in moves_in:
         copy.wait()
     for copy in moves_out:
         copy.start()
-    for copy in (own, *moves_out):
+    for copy in (sent, own, *moves_out):
         copy.wait()
 
 
@@ -404,10 +410,11 @@
         grid_spec=pltpu.PrefetchScalarGridSpec(
             num_scalar_prefetch=2,
             grid=(1,),
-            in_specs=[anywhere, anywhere, pl.BlockSpec((DIM, width), lambda s, table, count: (0, table[4 * job]))]
-            + [anywhere] * len(held),
-            out_specs=[pl.BlockSpec((DIM, width), lambda s, *_: (0, 0)), anywhere],
+            in_specs=[anywhere] * (3 + len(held)),
+            out_specs=[anywhere, anywhere],
             scratch_shapes=[
+                pltpu.VMEM((DIM, width), f32),
+                pltpu.VMEM((DIM, width), bf16),
                 pltpu.VMEM((2, DW_TOK, DIM), bf16),
                 pltpu.VMEM((2, DW_TOK, 128), f32),
                 pltpu.VMEM((DW_TOK, width), bf16),

time: 1060 us -> 1050 us (level)
  Pallas kernels: 444 us -> 432 us
    pallas_call x8, Pallas kernels: 273 us -> 261 us  [weight_grad(): pl.pallas_call(functools.partial(dw_kernel, job, [at for _, at in merges]...]
  transfers between devices with their start and end apart: 14 -> 14, of which waited for: 6 -> 6; matrix products, arithmetic and copies ran while one was open for 1% -> 1% of each run, Pallas kernels for 29% -> 28%
where the time goes in v7:
time: 1050 us
  waiting for transfers between devices  521 us (50%)
  Pallas kernels  432 us (41%)
  blocking collectives  37 us (4%)
  between operations  18 us (2%)
  other arithmetic  14.8 us (1%)
  starting transfers between devices  12.1 us (1%)
    all_gather x1, waiting for transfers between devices, local_step(): xh_all = lax.all_gather(x_hat, ('dp', 'vp'), axis=0, tiled=True)  275 us
    pallas_call x8, Pallas kernels, weight_grad(): pl.pallas_call(functools.partial(dw_kernel, job, [at for _, at in merges]...  261 us
    reduce_scatter x1, waiting for transfers between devices, local_step(): d_normed = lax.psum_scatter(dn_part, 'vp', scatter_dimension=0, tiled=True)  117 us
    pallas_call x2, Pallas kernels, forward_stats(): pl.pallas_call(functools.partial(fwd_kernel, group), grid=(vocab // FWD_C...  72.7 us
    pallas_call x1, Pallas kernels, first_columns(): pl.pallas_call(first_kernel, grid_spec=pltpu.PrefetchScalarGridSpec(num_s...  51.5 us
    all_gather x1, waiting for transfers between devices, local_step(): parts = lax.all_gather(parts, ('dp', 'vp'), axis=0)  50.6 us
    ppermute x8, waiting for transfers between devices, local_step(): moved.append((lax.ppermute(chunk, 'dp', pairs), 4 * k + 3))  46.3 us
    pallas_call x1, Pallas kernels, backward_dn(): pl.pallas_call(dn_kernel, grid_spec=pltpu.PrefetchScalarGridSpec(num_scal...  40.7 us
  transfers between devices with their start and end apart: 14, of which 6 were waited for; matrix products, arithmetic and copies ran while one was open for 1% of the time, Pallas kernels for 28%

profile of v7, /device:TPU:0, one launch (start us, length us, event | category | flops | bytes accessed | tf_op | source)
XLA Modules:
  0.0 1045.7 jit_solution(9324419431826230030)
XLA Ops:
  7.2 1.4 reduce_sum.121
  8.6 0.8 select_reduce_fusion.1
  9.4 1.3 compare_select_fusion.3
  10.8 0.7 multiply_reduce_fusion.2
  11.5 1.1 copy-done.2
  12.9 3.0 collective-permute-start.1
  17.9 0.6 fusion.13.table_ref
  18.5 31.9 %collective-permute-done.1.xa = f32[512,768]{1,0:T(8,128)} collective-permute-done((f32[512,768]{1,0:T(8,128)S(1)}, f32[512,768]{1,0:T(8,128)}, u32[]{:S(2)}, u32[]{:S(2)}) %collective-permute-start.1) | collective-permute-done | bytes 1572896 | tf_op jit(solution)/shard_map/ppermute | solution.py:496
  50.4 36.3 %fwd_stats.2 = (bf16[1024,768]{1,0:T(8,128)(2,1)}, f32[2,2,512]{2,1,0:T(2,128)}) custom-call(f32[512,768]{1,0:T(8,128)} %copy-done.4, f32[512,768]{1,0:T(8,128)} %collective-permute-done.xb, f32[1,768]{1,0:T(1,128)} %reshape.169.g_ref, bf16[768,16384]{1,0:T(8,128)(2,1)} %w_hbm.15), custom_call_target="tpu_custom_call" | custom-call | flops 25769803776 | bytes 33030144 | tf_op jit(solution)/shard_map/fwd_stats/pallas_call | solution.py:91
  86.8 36.3 %fwd_stats.3 = (bf16[1024,768]{1,0:T(8,128)(2,1)}, f32[2,2,512]{2,1,0:T(2,128)}) custom-call(f32[512,768]{1,0:T(8,128)} %collective-permute-done.1.xa, f32[512,768]{1,0:T(8,128)} %collective-permute-done.2.xb, f32[1,768]{1,0:T(1,128)} %reshape.169.g_ref, bf16[768,16384]{1,0:T(8,128)(2,1)} %w_hbm.15), custom_call_target="tpu_custom_call" | custom-call | flops 25769803776 | bytes 33030144 | tf_op jit(solution)/shard_map/fwd_stats/pallas_call | solution.py:91
  123.1 0.7 pad_maximum_fusion.2
  123.8 5.5 all-gather
  129.6 31.5 %all_gather.20 = f32[32,3,512]{2,1,0:T(4,128)S(1)} all-gather(f32[4,3,512]{2,1,0:T(4,128)S(1)} %pad_maximum_fusion.1), channel_id=1, replica_groups=mesh['dp'=8,'vp'=4] {'dp'}, dimensions={0}, use_global_device_ids=true | all-gather | bytes 221184 | tf_op jit(solution)/shard_map/all_gather | solution.py:510
  161.1 1.2 fusion.15
  162.4 1.3 fusion.17
  165.1 0.6 fusion.20
  165.7 1.3 dynamic-slice_subtract_fusion.offs_ref
  167.2 0.7 dynamic-slice_reduce_fusion.kept_ref
  168.6 0.7 constant_dynamic-slice_fusion.aux_ref
  169.3 40.7 %backward_dn.1 = (f32[2048,768]{1,0:T(8,128)}, f32[8,128]{1,0:T(8,128)}) custom-call(s32[4]{0:T(128)} %dynamic-slice_subtract_fusion.offs_ref, s32[4]{0:T(128)} %get-tuple-element.67.span_ref, s32[4]{0:T(128)} %dynamic-slice_reduce_fusion.kept_ref, s32[4]{0:T(128)} %iota_xor_fusion.mine_ref, s32[1]{0:T(128)} %bitcast.31.nt_ref, s32[1]{0:T(128)} %bitcast.32.col_ref, ...), custom_call_target="tpu_custom_call" | custom-call | flops 103079215104 | bytes 34603008 | tf_op jit(solution)/shard_map/backward_dn/pallas_call | solution.py:174
  210.1 1.3 select_reduce_fusion.3
  212.1 0.6 reduce_sum.130
  213.4 116.9 %reduce-scatter.2.cloned.1.call-done = f32[512,768]{1,0:T(8,128)} async-done(((f32[2048,768]{1,0:T(8,128)}), f32[512,768]{1,0:T(8,128)}) %reduce-scatter.2.cloned.1.call-update) | async-done | bytes 1572880 | tf_op jit(solution)/shard_map/reduce_scatter | solution.py:560
  330.3 1.9 multiply_reduce_fusion
  332.2 0.6 concatenate.11
  333.6 3.2 fusion
  336.8 50.6 %all-gather.7.cloned.1.call-done = f32[2048,128]{1,0:T(8,128)} async-done(((f32[64,128]{1,0:T(8,128)}), f32[2048,128]{1,0:T(8,128)}) %all-gather.7.cloned.1.call-update) | async-done | bytes 1048592 | tf_op jit(solution)/shard_map/all_gather | solution.py:570
  387.4 0.9 slice_reduce_fusion
  388.8 0.6 slice_bitcast_fusion.17
  389.4 274.6 %all-gather.5.cloned.1.call-done = f32[16384,768]{1,0:T(8,128)} async-done(((f32[512,768]{1,0:T(8,128)}), f32[16384,768]{1,0:T(8,128)}) %all-gather.5.cloned.1.call-update) | async-done | bytes 50331664 | tf_op jit(solution)/shard_map/all_gather | solution.py:497
  664.1 51.5 %first_columns.1 = (bf16[16384,768]{1,0:T(8,128)(2,1)}, f32[16384,128]{1,0:T(8,128)}, f32[768,1024]{1,0:T(8,128)}) custom-call(s32[33]{0:T(128)} %copy-done.14, s32[36]{0:T(128)} %fusion.13.table_ref, f32[32,512,768]{2,1,0:T(8,128)} %bitcast.95, f32[32,8,512]{2,1,0:T(8,128)} %copy-done.6, f32[1,768]{1,0:T(1,128)} %reshape.169.g_ref, bf16[768,16384]{1,0:T(8,128)(2,1)} %w_hbm.15), custom_call_target="tpu_custom_call" | custom-call | flops 25769803776 | bytes 75497472 | tf_op jit(solution)/shard_map/first_columns/pallas_call | solution.py:300
  715.6 1.6 collective-permute-start.3
  717.2 35.0 %weight_grad.8 = (f32[768,1024]{1,0:T(8,128)}, f32[768,16384]{1,0:T(8,128)}) custom-call(s32[36]{0:T(128)} %fusion.13.table_ref, s32[1]{0:T(128)} %get-tuple-element.41.count_ref, bf16[16384,768]{1,0:T(8,128)(2,1)} %get-tuple-element.44.n_hbm, f32[16384,128]{1,0:T(8,128)} %get-tuple-element.45.aux_hbm, bf16[768,16384]{1,0:T(8,128)(2,1)} %w_hbm.15, ...), custom_call_target="tpu_custom_call" | custom-call | flops 25769803776 | bytes 31457280 | tf_op jit(solution)/shard_map/weight_grad/pallas_call | solution.py:408
  752.1 33.7 %weight_grad.9 = (f32[768,1024]{1,0:T(8,128)}, f32[768,16384]{1,0:T(8,128)}) custom-call(s32[36]{0:T(128)} %fusion.13.table_ref, s32[1]{0:T(128)} %get-tuple-element.41.count_ref, bf16[16384,768]{1,0:T(8,128)(2,1)} %get-tuple-element.44.n_hbm, f32[16384,128]{1,0:T(8,128)} %get-tuple-element.45.aux_hbm, ...), custom_call_target="tpu_custom_call", output_to_operand_aliasing={{1}: (5, {})} | custom-call | flops 25769803776 | bytes 31457280 | tf_op jit(solution)/shard_map/weight_grad/pallas_call | solution.py:408
  785.9 33.7 %weight_grad.10 = (f32[768,1024]{1,0:T(8,128)}, f32[768,16384]{1,0:T(8,128)}) custom-call(s32[36]{0:T(128)} %fusion.13.table_ref, s32[1]{0:T(128)} %get-tuple-element.41.count_ref, bf16[16384,768]{1,0:T(8,128)(2,1)} %get-tuple-element.44.n_hbm, f32[16384,128]{1,0:T(8,128)} %get-tuple-element.45.aux_hbm, ...), custom_call_target="tpu_custom_call", output_to_operand_aliasing={{1}: (5, {})} | custom-call | flops 25769803776 | bytes 31457280 | tf_op jit(solution)/shard_map/weight_grad/pallas_call | solution.py:408
  819.6 2.1 collective-permute-start.6
  822.3 34.8 %weight_grad.11 = (f32[768,1024]{1,0:T(8,128)}, f32[768,16384]{1,0:T(8,128)}) custom-call(s32[36]{0:T(128)} %fusion.13.table_ref, s32[1]{0:T(128)} %get-tuple-element.41.count_ref, bf16[16384,768]{1,0:T(8,128)(2,1)} %get-tuple-element.44.n_hbm, f32[16384,128]{1,0:T(8,128)} %get-tuple-element.45.aux_hbm, ...), custom_call_target="tpu_custom_call", output_to_operand_aliasing={{1}: (5, {})} | custom-call | flops 25769803776 | bytes 31457280 | tf_op jit(solution)/shard_map/weight_grad/pallas_call | solution.py:408
  857.1 1.6 collective-permute-start.7
  858.6 34.8 %weight_grad.12 = (f32[768,1024]{1,0:T(8,128)}, f32[768,16384]{1,0:T(8,128)}) custom-call(s32[36]{0:T(128)} %fusion.13.table_ref, s32[1]{0:T(128)} %get-tuple-element.41.count_ref, bf16[16384,768]{1,0:T(8,128)(2,1)} %get-tuple-element.44.n_hbm, f32[16384,128]{1,0:T(8,128)} %get-tuple-element.45.aux_hbm, ...), custom_call_target="tpu_custom_call", output_to_operand_aliasing={{1}: (5, {})} | custom-call | flops 25769803776 | bytes 31457280 | tf_op jit(solution)/shard_map/weight_grad/pallas_call | solution.py:408
  893.4 34.8 %weight_grad.13 = (f32[768,1024]{1,0:T(8,128)}, f32[768,16384]{1,0:T(8,128)}) custom-call(s32[36]{0:T(128)} %fusion.13.table_ref, s32[1]{0:T(128)} %get-tuple-element.41.count_ref, bf16[16384,768]{1,0:T(8,128)(2,1)} %get-tuple-element.44.n_hbm, f32[16384,128]{1,0:T(8,128)} %get-tuple-element.45.aux_hbm, ...), custom_call_target="tpu_custom_call", output_to_operand_aliasing={{1}: (5, {})} | custom-call | flops 25769803776 | bytes 31457280 | tf_op jit(solution)/shard_map/weight_grad/pallas_call | solution.py:408
  928.2 0.6 collective-permute-start.9
  928.9 19.3 %weight_grad.14 = (f32[768,512]{1,0:T(8,128)}, f32[768,16384]{1,0:T(8,128)}) custom-call(s32[36]{0:T(128)} %fusion.13.table_ref, s32[1]{0:T(128)} %get-tuple-element.41.count_ref, bf16[16384,768]{1,0:T(8,128)(2,1)} %get-tuple-element.44.n_hbm, f32[16384,128]{1,0:T(8,128)} %get-tuple-element.45.aux_hbm, ...), custom_call_target="tpu_custom_call", output_to_operand_aliasing={{1}: (5, {})} | custom-call | flops 12884901888 | bytes 28311552 | tf_op jit(solution)/shard_map/weight_grad/pallas_call | solution.py:408
  948.2 2.0 collective-permute-start.10
  950.2 10.2 collective-permute-done.7.rest_1_
  960.4 34.8 %weight_grad.15 = (f32[768,1024]{1,0:T(8,128)}, f32[768,16384]{1,0:T(8,128)}) custom-call(s32[36]{0:T(128)} %fusion.13.table_ref, s32[1]{0:T(128)} %get-tuple-element.41.count_ref, bf16[16384,768]{1,0:T(8,128)(2,1)} %get-tuple-element.44.n_hbm, f32[16384,128]{1,0:T(8,128)} %get-tuple-element.45.aux_hbm, ...), custom_call_target="tpu_custom_call", output_to_operand_aliasing={{1}: (5, {})} | custom-call | flops 25769803776 | bytes 31457280 | tf_op jit(solution)/shard_map/weight_grad/pallas_call | solution.py:408
  995.2 36.1 %collective-permute-done.10.rest_2_ = f32[768,512]{1,0:T(8,128)S(1)} collective-permute-done((f32[768,512]{1,0:T(8,128)}, f32[768,512]{1,0:T(8,128)S(1)}, u32[]{:S(2)}, u32[]{:S(2)}) %collective-permute-start.10) | collective-permute-done | bytes 1572896 | tf_op jit(solution)/shard_map/ppermute | solution.py:580
  1031.3 1.1 copy-done.5
  1032.5 6.2 finish.1
  (90 shorter events, 4.9 us)
Async XLA Ops:
  7.2 3.6 copy-start
  7.2 323.1 %reduce-scatter.2.cloned.1.call-start = ((), (), s32[]{:S(2)}) async-start(), calls=%async_computation.1 | async-start | bytes 7864320 | tf_op jit(solution)/shard_map/reduce_scatter | solution.py:560
  10.8 5.8 copy-start.11
  11.5 1.2 copy-start.2
  11.5 1.4 copy-start.7
  12.6 3.9 copy-start.16
  12.6 4.1 copy-start.9
  12.6 5.2 copy-start.17
  12.6 5.2 copy-start.18
  12.7 5.2 copy-start.19
  12.7 5.2 copy-start.20
  12.9 37.6 %copy-start.4 = (f32[512,768]{1,0:T(8,128)}, f32[512,768]{1,0:T(8,128)S(1)}, u32[]{:S(2)}) copy-start(f32[512,768]{1,0:T(8,128)S(1)} %broadcast_multiply_fusion.xa) | copy-start | bytes 4718596
  12.9 37.5 %collective-permute-start.1 = (f32[512,768]{1,0:T(8,128)S(1)}, f32[512,768]{1,0:T(8,128)}, u32[]{:S(2)}, u32[]{:S(2)}) collective-permute-start(f32[512,768]{1,0:T(8,128)S(1)} %broadcast_multiply_fusion.xa), channel_id=1, source_target_pairs={{0,2},{1,3},{2,0},{3,1},{4,6},{5,7},{6,4},{7,5},{8,10},{9,11},{10,... | collective-permute-start | bytes 4718600 | tf_op jit(solution)/shard_map/ppermute | solution.py:496
  15.9 34.5 %collective-permute-start = (f32[512,768]{1,0:T(8,128)S(1)}, f32[512,768]{1,0:T(8,128)}, u32[]{:S(2)}, u32[]{:S(2)}) collective-permute-start(f32[512,768]{1,0:T(8,128)S(1)} %broadcast_multiply_fusion.xa), channel_id=1, source_target_pairs={{0,1},{1,0},{2,3},{3,2},{4,5},{5,4},{6,7},{7,6},{8,9},{9,8},{10,11... | collective-permute-start | bytes 4718600 | tf_op jit(solution)/shard_map/ppermute | solution.py:495
  50.4 36.4 %collective-permute-start.2 = (f32[512,768]{1,0:T(8,128)}, f32[512,768]{1,0:T(8,128)}, u32[]{:S(2)}, u32[]{:S(2)}) collective-permute-start(f32[512,768]{1,0:T(8,128)} %collective-permute-done.1.xa), channel_id=1, source_target_pairs={{0,1},{1,0},{2,3},{3,2},{4,5},{5,4},{6,7},{7,6},{8,9},{9,8},{10,11... | collective-permute-start | bytes 4718600 | tf_op jit(solution)/shard_map/ppermute | solution.py:499
  86.8 36.4 %copy-start.13 = (f32[2,2,512]{2,1,0:T(2,128)S(1)}, f32[2,2,512]{2,1,0:T(2,128)}, u32[]{:S(2)}) copy-start(f32[2,2,512]{2,1,0:T(2,128)} %get-tuple-element.33) | copy-start | bytes 24580
  162.4 47.5 %copy-start.14 = (s32[33]{0:T(128)}, s32[33]{0:T(128)S(1)}, u32[]{:S(2)}) copy-start(s32[33]{0:T(128)S(1)} %select_reduce_fusion.2.offs_ref) | copy-start | bytes 400
  168.6 41.4 %copy-start.6 = (f32[32,8,512]{2,1,0:T(8,128)}, f32[32,8,512]{2,1,0:T(8,128)S(1)}, u32[]{:S(2)}) copy-start(f32[32,8,512]{2,1,0:T(8,128)S(1)} %stack.50.aux_ref) | copy-start | bytes 1572868
  210.0 2.1 copy-start.15
  210.0 120.3 %copy-start.3 = (f32[512,768]{1,0:T(8,128)S(1)}, f32[512,768]{1,0:T(8,128)}, u32[]{:S(2)}) copy-start(f32[512,768]{1,0:T(8,128)} %copy-done.2) | copy-start | bytes 4718596
  210.0 120.3 %copy-start.8 = (f32[512]{0:T(512)S(1)}, f32[512]{0:T(512)}, u32[]{:S(2)}) copy-start(f32[512]{0:T(512)} %copy-done.7) | copy-start | bytes 6148
  210.0 120.3 %copy-start.10 = (f32[768]{0:T(1024)S(1)}, f32[768]{0:T(1024)}, u32[]{:S(2)}) copy-start(f32[768]{0:T(1024)} %param.12) | copy-start | bytes 9220
  210.0 177.4 %all-gather.7.cloned.1.call-start = ((), (), s32[]{:S(2)}) async-start(), calls=%async_computation.3 | async-start | bytes 1081344 | tf_op jit(solution)/shard_map/all_gather | solution.py:570
  332.2 1.4 copy-start.12
  332.8 331.2 %all-gather.5.cloned.1.call-start = ((), (), s32[]{:S(2)}) async-start(), calls=%async_computation.2 | async-start | bytes 51904512 | tf_op jit(solution)/shard_map/all_gather | solution.py:497
  715.6 106.7 %collective-permute-start.3 = (f32[768,1024]{1,0:T(8,128)}, f32[768,1024]{1,0:T(8,128)}, u32[]{:S(2)}, u32[]{:S(2)}) collective-permute-start(f32[768,1024]{1,0:T(8,128)} %get-tuple-element.46.rest_0_), channel_id=1, source_target_pairs={{0,4},{4,0},{8,12},{12,8},{16,20},{20,16},{24,28},{28,24},{1,5},{5... | collective-permute-start | bytes 9437192 | tf_op jit(solution)/shard_map/ppermute | solution.py:580
  785.8 72.8 %collective-permute-start.4 = (f32[768,1024]{1,0:T(8,128)}, f32[768,1024]{1,0:T(8,128)}, u32[]{:S(2)}, u32[]{:S(2)}) collective-permute-start(f32[768,1024]{1,0:T(8,128)} %get-tuple-element.51), channel_id=1, source_target_pairs={{0,8},{4,12},{8,0},{12,4},{16,24},{20,28},{24,16},{28,20},{1,9},{5... | collective-permute-start | bytes 9437192 | tf_op jit(solution)/shard_map/ppermute | solution.py:580
  819.6 109.2 %collective-permute-start.6 = (f32[768,1024]{1,0:T(8,128)}, f32[768,1024]{1,0:T(8,128)}, u32[]{:S(2)}, u32[]{:S(2)}) collective-permute-start(f32[768,1024]{1,0:T(8,128)} %get-tuple-element.55), channel_id=1, source_target_pairs={{0,8},{4,12},{8,0},{12,4},{16,24},{20,28},{24,16},{28,20},{1,9},{5... | collective-permute-start | bytes 9437192 | tf_op jit(solution)/shard_map/ppermute | solution.py:580
  821.7 71.7 %collective-permute-start.5 = (f32[768,1024]{1,0:T(8,128)}, f32[768,1024]{1,0:T(8,128)}, u32[]{:S(2)}, u32[]{:S(2)}) collective-permute-start(f32[768,1024]{1,0:T(8,128)} %get-tuple-element.53), channel_id=1, source_target_pairs={{0,4},{4,0},{8,12},{12,8},{16,20},{20,16},{24,28},{28,24},{1,5},{5... | collective-permute-start | bytes 9437192 | tf_op jit(solution)/shard_map/ppermute | solution.py:580
  857.1 103.4 %collective-permute-start.7 = (f32[768,1024]{1,0:T(8,128)}, f32[768,1024]{1,0:T(8,128)}, u32[]{:S(2)}, u32[]{:S(2)}) collective-permute-start(f32[768,1024]{1,0:T(8,128)} %get-tuple-element.57), channel_id=1, source_target_pairs={{0,4},{4,0},{8,12},{12,8},{16,20},{20,16},{24,28},{28,24},{1,5},{5... | collective-permute-start | bytes 9437192 | tf_op jit(solution)/shard_map/ppermute | solution.py:580
  928.2 103.1 %collective-permute-start.9 = (f32[768,1024]{1,0:T(8,128)}, f32[768,1024]{1,0:T(8,128)}, u32[]{:S(2)}, u32[]{:S(2)}) collective-permute-start(f32[768,1024]{1,0:T(8,128)} %get-tuple-element.60), channel_id=1, source_target_pairs={{0,4},{4,0},{8,12},{12,8},{16,20},{20,16},{24,28},{28,24},{1,5},{5... | collective-permute-start | bytes 9437192 | tf_op jit(solution)/shard_map/ppermute | solution.py:580
  928.8 102.5 %collective-permute-start.8 = (f32[768,1024]{1,0:T(8,128)}, f32[768,1024]{1,0:T(8,128)}, u32[]{:S(2)}, u32[]{:S(2)}) collective-permute-start(f32[768,1024]{1,0:T(8,128)} %get-tuple-element.59), channel_id=1, source_target_pairs={{0,8},{4,12},{8,0},{12,4},{16,24},{20,28},{24,16},{28,20},{1,9},{5... | collective-permute-start | bytes 9437192 | tf_op jit(solution)/shard_map/ppermute | solution.py:580
  948.2 83.1 %collective-permute-start.10 = (f32[768,512]{1,0:T(8,128)}, f32[768,512]{1,0:T(8,128)S(1)}, u32[]{:S(2)}, u32[]{:S(2)}) collective-permute-start(f32[768,512]{1,0:T(8,128)} %get-tuple-element.61), channel_id=1, source_target_pairs={{0,8},{4,12},{8,0},{12,4},{16,24},{20,28},{24,16},{28,20},{1,9},{5... | collective-permute-start | bytes 4718600 | tf_op jit(solution)/shard_map/ppermute | solution.py:580
  1031.3 1.1 copy-start.5
  1032.5 6.3 copy-start.1
Sparse Core Ops, SparseCore 0:
  210.2 120.0 reduce-scatter.1
  333.7 53.6 all-gather.6
  390.3 273.7 all-gather.4
